TPU v7x, 128 devices: a whole 4x4x4 slice. The times are simulated.
128 devices in a mesh: row: 8 (over x, core), col: 16 (over z, y).
Axes of the slice: x: 4, y: 4, z: 4, core: 2. Of those that a mesh axis runs over, the one named last changes fastest.
Arguments:
- blocks: float32 [16384, 9216], P(('row', 'col')), may hold values from -6 to 20, as said below
- connect: int32 [16384, 96], P(('row', 'col')), may hold values from 0 to 32767, as said below
- owner_map: int32 [16384], P(('row', 'col')), may hold values from 0 to 127, as said below
- right_side: float32 [32768, 2048], P(('row', 'col')), may hold values from -1000 to 1000
Outputs:
- solution: float32 [32768, 2048], P(('row', 'col'))
- residual: float32 [32768, 2048], P(('row', 'col'))
Inputs may be any that keep to these rules, and one draw needn't show every extreme that they name: `blocks`: each row, read as a 96 x 96 matrix, is symmetric positive definite. `connect`: the 96 ids of a subdomain are distinct and lie among the 512 ids that begin at 256 times its owner, counted modulo 32768. `owner_map`: among the subdomains of one device, no owner is named more than 2 times, and some owner exactly 2 times.
All inputs are finite; a program needn't handle non-finite values.
Results may differ from a plain program's by a relative error of at most 0.0003.
Values sent between devices are 32-bit elements; how exact they have to be, the bound alone decides.
No kernel may reach another device: no remote copies, remote signals or barrier semaphores. Data moves between devices by JAX's collectives and lax.ppermute only.
A program may use at most 128 MiB of HBM per device.

v0:
```python
import jax
import jax.numpy as jnp
from jax import lax
from jax.experimental import pallas as pl
from jax.experimental.pallas import tpu as pltpu
from jax.sharding import PartitionSpec as P


AXES = ("row", "col")
NB = 96
HALF = 48
ROWS = 40
GROUP = 4
HI = lax.Precision.HIGHEST
MID = lax.Precision.HIGH


def split2(x):
    high = x.astype(jnp.bfloat16)
    low = (x - high.astype(jnp.float32)).astype(jnp.bfloat16)
    return high, low


def pack_kernel(owner_ref, ids_ref, x_ref, out0_ref, out1_ref, tail_ref):
    subs = x_ref.shape[0]
    devs = out0_ref.shape[0] // ROWS
    sub = lax.broadcasted_iota(jnp.int32, (devs, subs), 0)
    here = sub == owner_ref[...]
    before = lax.broadcasted_iota(jnp.int32, (subs, subs), 0) < lax.broadcasted_iota(
        jnp.int32, (subs, subs), 1
    )
    count = jnp.dot(
        here.astype(jnp.bfloat16), before.astype(jnp.bfloat16), preferred_element_type=jnp.float32
    )
    first = jnp.where(here & (count < 0.5), 1.0, 0.0).astype(jnp.bfloat16)
    second = jnp.where(here & (count > 0.5), 1.0, 0.0).astype(jnp.bfloat16)
    pick = jnp.concatenate([first, second], axis=0)
    ids = ids_ref[...].astype(jnp.float32).T + 1.0
    ids = jnp.concatenate([ids, jnp.zeros((subs, 128 - NB), jnp.float32)], axis=1)
    pick = jnp.concatenate([pick, pick], axis=1)
    lane = lax.broadcasted_iota(jnp.int32, (subs, 128), 1)

    def flat(start):
        tile, off = divmod(start, 128)
        if off == 0:
            return x_ref[:, tile * 128 : tile * 128 + 128]
        one = pltpu.roll(x_ref[:, tile * 128 : tile * 128 + 128], 128 - off, 1)
        if (tile + 1) * 128 >= x_ref.shape[1]:
            return one
        two = pltpu.roll(x_ref[:, tile * 128 + 128 : tile * 128 + 256], 128 - off, 1)
        return jnp.where(lane < 128 - off, one, two)

    diag = jnp.zeros((subs, 128), jnp.float32)

    def wrow(i, diag):
        top = flat(NB * i)
        bottom = flat(NB * (i + HALF) + HALF)
        row = jnp.where(lane < i, bottom, jnp.where(lane == i, 0.5 * top, top))
        return row, jnp.where(lane == i, 0.5 * bottom, diag)

    for m in range(8):
        row, diag = wrow(ROWS + m, diag)
        tail_ref[m] = row
    order = [i for i in range(0, ROWS, 2) if i not in (26, 28)] + [26, 28]
    kept = {}
    for i in (26, 27, 28, 29):
        kept[i], diag = wrow(i, diag)
    for i0 in order:
        tiles = []
        for i in (i0, i0 + 1):
            if i in kept:
                row = kept[i]
            else:
                row, diag = wrow(i, diag)
            if i < 24:
                extra = pltpu.roll(tail_ref[i % 8], 96 - 32 * (i // 8), 1)
            elif i < 27:
                extra = pltpu.roll(ids, 96 - 32 * (i - 24), 1)
            elif i < 29:
                extra = pltpu.roll(diag, 96 - 32 * (i - 27), 1)
            else:
                extra = jnp.zeros_like(row)
            tiles.append(jnp.where(lane < NB, row, extra))
        high, low = split2(jnp.concatenate(tiles, axis=1))
        out = jnp.dot(
            pick, jnp.concatenate([high, low], axis=0), preferred_element_type=jnp.float32
        )
        for k in range(2):
            part = out[:, 128 * k : 128 * k + 128]
            out0_ref[pl.ds(i0 + k, devs, stride=ROWS), :] = part[:devs]
            out1_ref[pl.ds(i0 + k, devs, stride=ROWS), :] = part[devs:]


def pack(owner_map, ids, blocks, devices):
    shape = jax.ShapeDtypeStruct((devices * ROWS, 128), jnp.float32)
    return pl.pallas_call(
        pack_kernel,
        out_shape=(shape, shape),
        scratch_shapes=[pltpu.VMEM((8, blocks.shape[0], 128), jnp.float32)],
        name="pack",
    )(owner_map.reshape(1, -1), ids, blocks)


def assemble_kernel(last, base_ref, got_ref, *refs):
    place_ref, spread_ref, vec_ref, list_ref, sem = refs[-5:]
    if last:
        prev_ref, s11_ref, s12_ref, low_ref, acc_ref = refs[:5]
    else:
        acc_ref = refs[0]
    window = acc_ref.shape[0]
    half = window // 2
    slots = got_ref.shape[0] // ROWS
    lane = lax.broadcasted_iota(jnp.int32, (slots, slots), 1)
    sub = lax.broadcasted_iota(jnp.int32, (slots, slots), 0)
    filled = got_ref[pl.ds(24, slots, stride=ROWS), :][:, NB : NB + 1] > 0.5
    filled = jnp.broadcast_to(jnp.where(filled, 1.0, 0.0), (slots, slots))
    rank = jnp.dot(
        jnp.where(lane < sub, 1.0, 0.0).astype(jnp.bfloat16),
        filled.astype(jnp.bfloat16),
        preferred_element_type=jnp.float32,
    )
    subf = sub.astype(jnp.float32)
    hit = (filled > 0.5) & (rank == lane.astype(jnp.float32))
    count = jnp.sum(filled, axis=0, keepdims=True)
    spare = jnp.max(jnp.where(filled > 0.5, 0.0, subf), axis=0, keepdims=True)
    chosen = jnp.sum(jnp.where(hit, subf, 0.0), axis=0, keepdims=True)
    chosen = jnp.where(lane[:1].astype(jnp.float32) < count, chosen, spare)
    first_row = lax.broadcasted_iota(jnp.int32, (8, slots), 0) == 0
    vec_ref[...] = jnp.where(first_row, chosen, count).astype(jnp.int32)
    copy = pltpu.make_async_copy(vec_ref, list_ref, sem)
    copy.start()
    acc_ref[...] = prev_ref[...] if last else jnp.zeros_like(acc_ref)
    place_ref[1] = jnp.zeros(place_ref.shape[1:], jnp.bfloat16)
    spread_ref[1] = jnp.zeros(spread_ref.shape[1:], jnp.bfloat16)
    copy.wait()

    lane = lax.broadcasted_iota(jnp.int32, (HALF, 128), 1)
    row = lax.broadcasted_iota(jnp.int32, (HALF, 128), 0)
    lane1 = lax.broadcasted_iota(jnp.int32, (1, 128), 1)
    lane8 = lax.broadcasted_iota(jnp.int32, (8, 128), 1)
    target = lax.broadcasted_iota(jnp.int32, (window, 128), 0).astype(jnp.float32)
    start = base_ref[0].astype(jnp.float32)
    total = base_ref[1].astype(jnp.float32)

    def local(ids):
        moved = ids - 1.0 - start
        return jnp.where(ids > 0.5, jnp.where(moved < 0.0, moved + total, moved), -1.0)


    def lanes(pieces):
        out = pieces[3]
        for k in (2, 1, 0):
            out = jnp.where(lane1 < 32 * (k + 1), pieces[k], out)
        return out

    def onehot(ids):
        return jnp.where(target == local(ids), 1.0, 0.0).astype(jnp.bfloat16)

    def generate(buf, first):
        pieces = []
        for k in range(GROUP):
            slot = list_ref[0, first + k]
            base = pl.multiple_of(slot * ROWS, 8)
            got = got_ref[pl.ds(base, ROWS), :]
            rows = [got[24 + m : 25 + m] for m in range(3)]
            pieces += rows
            ids = lanes([pltpu.roll(rows[m], 32 * (m + 1), 1) for m in range(3)] + [jnp.zeros_like(rows[0])])
            half_diag = jnp.where(
                lane1 < 80, pltpu.roll(got[27:28], 80, 1), pltpu.roll(got[28:29], 112, 1)
            )
            tail = jnp.where(
                lane8 < 32,
                pltpu.roll(got[0:8], 32, 1),
                jnp.where(lane8 < 64, pltpu.roll(got[8:16], 64, 1), pltpu.roll(got[16:24], 96, 1)),
            )
            full = jnp.concatenate([got, tail], axis=0)
            top = jnp.where(lane >= row, full, 0.0)
            bottom = jnp.where(
                lane == row + HALF,
                half_diag,
                jnp.where((lane >= HALF) & (lane < row + HALF), pltpu.roll(full, HALF, 1), 0.0),
            )
            high, low = split2(jnp.concatenate([top, bottom], axis=0))
            spread = lax.dot_general(
                jnp.concatenate([high, low], axis=0),
                onehot(ids),
                (((1,), (1,)), ((), ())),
                preferred_element_type=jnp.float32,
            ).astype(jnp.bfloat16)
            spread_ref[buf, NB * k : NB * k + NB, :] = spread[:NB]
            spread_ref[buf, NB * (GROUP + k) : NB * (GROUP + k) + NB, :] = spread[NB:]
        for t in range(3):
            moved = [
                pltpu.roll(pieces[4 * t + q], (32 * (q + 1)) % 128, 1) if q < 3 else pieces[4 * t + q]
                for q in range(4)
            ]
            place = onehot(lanes(moved))
            place_ref[buf, :, 128 * t : 128 * t + 128] = place
            place_ref[buf, :, 128 * (t + 3) : 128 * (t + 3) + 128] = place

    def absorb(buf):
        acc_ref[...] += jnp.dot(
            place_ref[buf], spread_ref[buf], preferred_element_type=jnp.float32
        )

    def step(g, carry):
        generate(0, g * 2 * GROUP)
        absorb(1)
        generate(1, g * 2 * GROUP + GROUP)
        absorb(0)
        return carry

    lax.fori_loop(0, (list_ref[1, 0] + 2 * GROUP - 1) // (2 * GROUP), step, 0)
    absorb(1)
    if not last:
        return
    a11, a22 = acc_ref[:half, :half], acc_ref[half:, half:]
    s11_ref[...] = a11 + a11.T
    s12 = acc_ref[:half, half:] + acc_ref[half:, :half].T
    s12_ref[...] = s12
    low_ref[:, :half] = s12.T
    low_ref[:, half:] = a22 + a22.T


def assemble(base, got, window, prev=None):
    slots = got.shape[0] // ROWS
    half = window // 2
    last = prev is not None
    square = jax.ShapeDtypeStruct((half, half), jnp.float32)
    whole = jax.ShapeDtypeStruct((window, window), jnp.float32)
    scratch = [
        pltpu.VMEM((2, window, 2 * NB * GROUP), jnp.bfloat16),
        pltpu.VMEM((2, 2 * NB * GROUP, window), jnp.bfloat16),
        pltpu.VMEM((8, slots), jnp.int32),
        pltpu.SMEM((8, slots), jnp.int32),
        pltpu.SemaphoreType.DMA,
    ]
    if last:
        scratch = [pltpu.VMEM((window, window), jnp.float32)] + scratch
    out = (square, square, jax.ShapeDtypeStruct((half, window), jnp.float32)) if last else whole
    return pl.pallas_call(
        lambda *refs: assemble_kernel(last, *refs),
        out_shape=out,
        in_specs=[pl.BlockSpec(memory_space=pltpu.SMEM)]
        + [pl.BlockSpec(memory_space=pltpu.VMEM)] * (2 if last else 1),
        scratch_shapes=scratch,
        name="assemble_last" if last else "assemble_first",
    )(*((base, got, prev) if last else (base, got)))


def inverse_kernel(upper_ref, lower_ref, out_ref, mat_ref):
    size = upper_ref.shape[0]
    eye = jnp.where(
        lax.broadcasted_iota(jnp.int32, (size, size), 0)
        == lax.broadcasted_iota(jnp.int32, (size, size), 1),
        1.0,
        0.0,
    )
    mat = upper_ref[...] + lower_ref[:, size:] + eye
    mat_ref[...] = mat
    norm = jnp.max(jnp.sum(jnp.abs(mat), axis=0, keepdims=True))
    out_ref[...] = eye * (2.0 / (norm + 1.0))

    def cond(state):
        turn, gap = state
        return (turn < 48) & (gap > 1e-8)

    def turn(state):
        now = out_ref[...]
        miss = eye - jnp.dot(mat_ref[...], now, precision=HI, preferred_element_type=jnp.float32)
        out_ref[...] = now + jnp.dot(now, miss, precision=HI, preferred_element_type=jnp.float32)
        return state[0] + 1, jnp.sum(miss * miss)

    lax.while_loop(cond, turn, (0, jnp.float32(1.0)))


def invert(upper, lower):
    return pl.pallas_call(
        inverse_kernel,
        out_shape=jax.ShapeDtypeStruct(upper.shape, jnp.float32),
        scratch_shapes=[pltpu.VMEM(upper.shape, jnp.float32)],
        name="invert",
    )(upper, lower)


def mm(left, right, precision=MID):
    return jnp.dot(left, right, precision=precision, preferred_element_type=jnp.float32)


def column_sums(left, right):
    return jnp.sum(left * right, axis=0)


def safe(num, den):
    return jnp.where(den > 0, num / jnp.where(den > 0, den, 1.0), 0.0)


def coefficients(mu):
    m0, m1, m2, m3, m4, m5 = mu
    l1, l2 = safe(m1, m0), safe(m2, m0)
    d1 = m2 - l1 * m1
    e = m3 - l1 * m2
    l21 = safe(e, d1)
    d2 = m4 - l2 * m2 - l21 * e
    y0 = -m3
    y1 = -m4 - l1 * y0
    y2 = -m5 - l2 * y0 - l21 * y1
    b2 = safe(y2, d2)
    b1 = safe(y1, d1) - l21 * b2
    b0 = safe(y0, m0) - l1 * b1 - l2 * b2
    scale = 1.0 / (b0 - b1 + b2 - 1.0)
    c0, c1, c2, c3 = b0 * scale, b1 * scale, b2 * scale, scale
    return (1.0 - c0, c3 - c2, -c3), (c0, c1, c2, c3)


def finish_kernel(blocks_half, sums_ref, v0, w0, *refs):
    halves, (sol_ref, res_ref) = (refs[:5], refs[5:10]), refs[10:]
    x, c = coefficients([sums_ref[k : k + 1, :] for k in range(6)])

    def write(v1, v2, v3, w1, w2):
        sol_ref[...] = x[0] * w0[...] + x[1] * w1[...] + x[2] * w2[...]
        res_ref[...] = c[0] * v0[...] + c[1] * v1[...] + c[2] * v2[...] + c[3] * v3[...]

    for k in range(2):
        pl.when(pl.program_id(0) // blocks_half == k)(lambda k=k: write(*halves[k]))


def finish(sums, v0, w0, halves):
    rows, _ = v0.shape
    width = 256
    per = halves[0][0].shape[1] // width
    whole = pl.BlockSpec((rows, width), lambda j: (0, j))
    left = pl.BlockSpec((rows, width), lambda j: (0, jnp.minimum(j, per - 1)))
    right = pl.BlockSpec((rows, width), lambda j: (0, jnp.maximum(j - per, 0)))
    return pl.pallas_call(
        lambda *refs: finish_kernel(per, *refs),
        grid=(2 * per,),
        in_specs=[pl.BlockSpec((sums.shape[0], width), lambda j: (0, j)), whole, whole]
        + [left] * 5
        + [right] * 5,
        out_specs=(whole, whole),
        out_shape=(jax.ShapeDtypeStruct(v0.shape, v0.dtype),) * 2,
        name="finish",
    )(sums, v0, w0, *halves[0], *halves[1])


def butterfly(x, devices, bits):
    for bit in bits:
        x = x + lax.ppermute(x, AXES, [(i, i ^ bit) for i in range(devices)])
    return x


def body(blocks, connect, owner_map, right_side):
    devices = lax.axis_size(AXES)
    own = right_side.shape[0]
    window = 2 * own
    up = [(i, (i + 1) % devices) for i in range(devices)]
    down = [(b, a) for a, b in up]

    def from_below(x):
        return lax.ppermute(x, AXES, up)

    def from_above(x):
        return lax.ppermute(x, AXES, down)

    base = jnp.stack([lax.axis_index(AXES) * own, own * devices]).astype(jnp.int32)
    send0, send1 = pack(owner_map, connect.T, blocks, devices)

    def exchange(send):
        got = lax.all_to_all(
            send.reshape(devices, ROWS, 128), AXES, split_axis=0, concat_axis=0, tiled=True
        )
        return got.reshape(devices * ROWS, 128)

    got0 = exchange(send0)
    got1 = exchange(send1)
    v0, got0 = lax.optimization_barrier((right_side, got0))
    v0_low, v0_high = from_below(v0), from_above(v0)
    part = assemble(base, got0, window)
    center, high_band, lower = assemble(base, got1, window, part)
    lower = from_below(lower)
    low_band = lower[:, :own]
    inv = invert(center, lower)
    inv_low, inv_high = from_below(inv), from_above(inv)
    near_low, near_high = mm(low_band, inv_low, HI), mm(high_band, inv_high, HI)

    width = right_side.shape[1] // 2

    def part_of(x, h):
        return lax.slice_in_dim(x, h * width, (h + 1) * width, axis=1)

    v1, w1, w1_low, w1_high = {}, {}, {}, {}
    for h in range(2):
        v1[h] = mm(near_low, part_of(v0_low, h)) + mm(near_high, part_of(v0_high, h))
        w1[h] = mm(inv, v1[h])
        w1_low[h] = from_below(w1[h])
        w1_high[h] = from_above(w1[h])
    w0 = mm(inv, right_side)
    v2, w2 = {}, {}
    for h in range(2):
        v2[h] = mm(low_band, w1_low[h]) + mm(high_band, w1_high[h])
        w2[h] = mm(inv, v2[h])
    w2_high, w2_low = {}, {}
    w2_high[0] = from_above(w2[0])
    w2_low[1] = from_below(w2[1])
    later0, later1 = lax.optimization_barrier((w2[0], w2[1]))
    w2_low[0] = from_below(later0)
    w2_high[1] = from_above(later1)
    side = {0: mm(high_band, w2_high[0]), 1: mm(low_band, w2_low[1])}
    sums = []
    for h in range(2):
        v0h, w0h = part_of(right_side, h), part_of(w0, h)
        pairs = [(v0h, w0h), (v1[h], w0h), (v1[h], w1[h]), (v2[h], w1[h]), (v2[h], w2[h])]
        rows = [column_sums(*pair) for pair in pairs] + [2.0 * column_sums(side[h], w2[h])]
        sums.append(jnp.stack(rows))
    sums = jnp.concatenate(sums, axis=1)
    sums = butterfly(sums, devices, (64, 32, 8, 4, 16))
    sums, low_late, high_late = lax.optimization_barrier((sums, low_band, high_band))
    v3 = {0: side[0] + mm(low_late, w2_low[0]), 1: side[1] + mm(high_late, w2_high[1])}
    sums = butterfly(sums, devices, (2, 1))
    return finish(sums, right_side, w0, [(v1[h], v2[h], v3[h], w1[h], w2[h]) for h in range(2)])


def solution(mesh):
    both = P(AXES, None)
    return jax.shard_map(
        body,
        mesh=mesh,
        in_specs=(both, both, P(AXES), both),
        out_specs=(both, both),
        check_vma=False,
    )
```

profile of v0, /device:TPU:0, one launch (start us, length us, event | category | flops | bytes accessed | tf_op | source)
XLA Modules:
  0.0 310.7 jit_solution(120939182564416540)
XLA Ops:
  0.6 8.7 %pack.1 = (f32[5120,128]{1,0:T(8,128)}, f32[5120,128]{1,0:T(8,128)}) custom-call(s32[1,128]{1,0:T(1,128)} %bitcast.65, s32[96,128]{1,0:T(8,128)} %bitcast.52, f32[128,9216]{1,0:T(8,128)} %x_ref.1), custom_call_target="tpu_custom_call" | custom-call | tf_op jit(solution)/shard_map/pack/pallas_call | solution.py:96
  9.3 46.3 %all_to_all.10 = f32[128,40,128]{2,1,0:T(8,128)} all-to-all(f32[128,40,128]{2,1,0:T(8,128)} %bitcast.51), channel_id=1, replica_groups=mesh['row'=8,'col'=16] {'row','col'}, dimensions={0} | all-to-all | bytes 5242880 | tf_op jit(solution)/shard_map/all_to_all | solution.py:370
  55.6 5.9 %all-to-all-start = ((f32[128,40,128]{2,1,0:T(8,128)}), f32[128,40,128]{2,1,0:T(8,128)}, u32[]{:S(2)}, u32[]{:S(2)}) async-start(f32[128,40,128]{2,1,0:T(8,128)} %bitcast.50), calls=%async_computation | async-start | bytes 5242880 | tf_op jit(solution)/shard_map/all_to_all | solution.py:370
  61.5 7.0 %collective-permute-start.4 = (f32[256,2048]{1,0:T(8,128)S(1)}, f32[256,2048]{1,0:T(8,128)}, u32[]{:S(2)}, u32[]{:S(2)}) collective-permute-start(f32[256,2048]{1,0:T(8,128)S(1)} %copy-done.4), channel_id=1, source_target_pairs={{1,0},{2,1},{3,2},{4,3},{5,4},{6,5},{7,6},{8,7},{9,8},{10,9},{11,1... | collective-permute-start | bytes 6291464 | tf_op jit(solution)/shard_map/ppermute | solution.py:364
  68.5 0.7 pad_add_fusion.refs_0_
  69.2 24.4 %assemble_first.1.refs_2_ = f32[512,512]{1,0:T(8,128)} custom-call(s32[2]{0:T(128)} %pad_add_fusion.refs_0_, f32[5120,128]{1,0:T(8,128)} %bitcast.49), custom_call_target="tpu_custom_call" | custom-call | tf_op jit(solution)/shard_map/assemble_first/pallas_call | solution.py:241
  93.6 2.6 all-to-all-done
  96.3 9.6 %assemble_last.1 = (f32[256,256]{1,0:T(8,128)}, f32[256,256]{1,0:T(8,128)}, f32[256,512]{1,0:T(8,128)}) custom-call(s32[2]{0:T(128)} %pad_add_fusion.refs_0_, f32[5120,128]{1,0:T(8,128)} %bitcast.4.refs_1_, f32[512,512]{1,0:T(8,128)} %assemble_first.1.refs_2_), custom_call_target="tpu_custom_call" | custom-call | tf_op jit(solution)/shard_map/assemble_last/pallas_call | solution.py:241
  105.9 4.0 %collective-permute-start = (f32[256,512]{1,0:T(8,128)}, f32[256,512]{1,0:T(8,128)S(1)}, u32[]{:S(2)}, u32[]{:S(2)}) collective-permute-start(f32[256,512]{1,0:T(8,128)} %get-tuple-element.18), channel_id=1, source_target_pairs={{0,1},{1,2},{2,3},{3,4},{4,5},{5,6},{6,7},{7,8},{8,9},{9,10},{10,1... | collective-permute-start | bytes 1572872 | tf_op jit(solution)/shard_map/ppermute | solution.py:361
  109.9 34.6 %collective-permute-done.lower_ref = f32[256,512]{1,0:T(8,128)S(1)} collective-permute-done((f32[256,512]{1,0:T(8,128)}, f32[256,512]{1,0:T(8,128)S(1)}, u32[]{:S(2)}, u32[]{:S(2)}) %collective-permute-start) | collective-permute-done | bytes 524320 | tf_op jit(solution)/shard_map/ppermute | solution.py:361
  144.4 0.8 copy-done.11
  145.2 7.6 %invert.1 = f32[256,256]{1,0:T(8,128)} custom-call(f32[256,256]{1,0:T(8,128)} %get-tuple-element.17.upper_ref, f32[256,512]{1,0:T(8,128)} %copy-done.11), custom_call_target="tpu_custom_call" | custom-call | tf_op jit(solution)/shard_map/invert/pallas_call | solution.py:278
  152.8 2.4 collective-permute-start.1
  155.2 6.3 %collective-permute-start.3 = (f32[256,256]{1,0:T(8,128)}, f32[256,256]{1,0:T(8,128)S(1)}, u32[]{:S(2)}, u32[]{:S(2)}) collective-permute-start(f32[256,256]{1,0:T(8,128)} %invert.1), channel_id=1, source_target_pairs={{1,0},{2,1},{3,2},{4,3},{5,4},{6,5},{7,6},{8,7},{9,8},{10,9},{11,1... | collective-permute-start | bytes 786440 | tf_op jit(solution)/shard_map/ppermute | solution.py:364
  161.6 4.3 %collective-permute-done.1 = f32[256,256]{1,0:T(8,128)S(1)} collective-permute-done((f32[256,256]{1,0:T(8,128)}, f32[256,256]{1,0:T(8,128)S(1)}, u32[]{:S(2)}, u32[]{:S(2)}) %collective-permute-start.1) | collective-permute-done | bytes 262176 | tf_op jit(solution)/shard_map/ppermute | solution.py:361
  165.8 1.3 fusion.11
  167.2 1.3 fusion.14
  168.5 1.8 fusion
  170.3 0.0 copy-start.9
  170.4 1.9 convolution_add_fusion.3.refs_8_
  172.3 0.6 fusion.18.refs_11_
  172.9 6.0 %collective-permute-start.9 = (f32[256,1024]{1,0:T(8,128)S(1)}, f32[256,1024]{1,0:T(8,128)S(1)}, u32[]{:S(2)}, u32[]{:S(2)}) collective-permute-start(f32[256,1024]{1,0:T(8,128)S(1)} %fusion.18.refs_11_), channel_id=1, source_target_pairs={{1,0},{2,1},{3,2},{4,3},{5,4},{6,5},{7,6},{8,7},{9,8},{10,9},{11,1... | collective-permute-start | bytes 3145736 | tf_op jit(solution)/shard_map/ppermute | solution.py:364
  178.9 1.8 fusion.3
  180.8 1.9 convolution_add_fusion.5.refs_3_
  182.7 0.0 copy-start.12
  182.7 0.6 fusion.15.refs_6_
  183.3 7.2 %collective-permute-start.6 = (f32[256,1024]{1,0:T(8,128)S(1)}, f32[256,1024]{1,0:T(8,128)S(1)}, u32[]{:S(2)}, u32[]{:S(2)}) collective-permute-start(f32[256,1024]{1,0:T(8,128)S(1)} %fusion.15.refs_6_), channel_id=1, source_target_pairs={{1,0},{2,1},{3,2},{4,3},{5,4},{6,5},{7,6},{8,7},{9,8},{10,9},{11,1... | collective-permute-start | bytes 3145736 | tf_op jit(solution)/shard_map/ppermute | solution.py:364
  190.5 6.8 %collective-permute-done.9 = f32[256,1024]{1,0:T(8,128)S(1)} collective-permute-done((f32[256,1024]{1,0:T(8,128)S(1)}, f32[256,1024]{1,0:T(8,128)S(1)}, u32[]{:S(2)}, u32[]{:S(2)}) %collective-permute-start.9) | collective-permute-done | bytes 1048608 | tf_op jit(solution)/shard_map/ppermute | solution.py:364
  197.4 0.7 fusion.19
  198.0 4.4 %collective-permute-done.8 = f32[256,1024]{1,0:T(8,128)S(1)} collective-permute-done((f32[256,1024]{1,0:T(8,128)S(1)}, f32[256,1024]{1,0:T(8,128)S(1)}, u32[]{:S(2)}, u32[]{:S(2)}) %collective-permute-start.8) | collective-permute-done | bytes 1048608 | tf_op jit(solution)/shard_map/ppermute | solution.py:361
  202.5 0.6 convolution_add_fusion.2.refs_9_
  203.1 1.6 fusion.20.refs_12_
  204.7 2.5 collective-permute-start.10
  207.2 12.6 %collective-permute-done.6 = f32[256,1024]{1,0:T(8,128)S(1)} collective-permute-done((f32[256,1024]{1,0:T(8,128)S(1)}, f32[256,1024]{1,0:T(8,128)S(1)}, u32[]{:S(2)}, u32[]{:S(2)}) %collective-permute-start.6) | collective-permute-done | bytes 1048608 | tf_op jit(solution)/shard_map/ppermute | solution.py:364
  219.8 0.7 fusion.16
  220.5 4.1 %collective-permute-done.5 = f32[256,1024]{1,0:T(8,128)S(1)} collective-permute-done((f32[256,1024]{1,0:T(8,128)S(1)}, f32[256,1024]{1,0:T(8,128)S(1)}, u32[]{:S(2)}, u32[]{:S(2)}) %collective-permute-start.5) | collective-permute-done | bytes 1048608 | tf_op jit(solution)/shard_map/ppermute | solution.py:361
  224.6 0.7 convolution_add_fusion.4.refs_4_
  225.3 1.6 fusion.17.refs_7_
  226.9 1.1 fusion.13.refs_2_
  228.0 2.6 collective-permute-start.18
  230.6 4.7 %collective-permute-start.19 = (f32[256,1024]{1,0:T(8,128)}, f32[256,1024]{1,0:T(8,128)}, u32[]{:S(2)}, u32[]{:S(2)}) collective-permute-start(f32[256,1024]{1,0:T(8,128)} %fusion.20.refs_12_), channel_id=1, source_target_pairs={{1,0},{2,1},{3,2},{4,3},{5,4},{6,5},{7,6},{8,7},{9,8},{10,9},{11,1... | collective-permute-start | bytes 3145736 | tf_op jit(solution)/shard_map/ppermute | solution.py:364
  235.3 3.1 %collective-permute-done.10 = f32[256,1024]{1,0:T(8,128)S(1)} collective-permute-done((f32[256,1024]{1,0:T(8,128)}, f32[256,1024]{1,0:T(8,128)S(1)}, u32[]{:S(2)}, u32[]{:S(2)}) %collective-permute-start.10) | collective-permute-done | bytes 1048608 | tf_op jit(solution)/shard_map/ppermute | solution.py:361
  238.4 0.7 fusion.7
  239.1 3.3 %collective-permute-done.7 = f32[256,1024]{1,0:T(8,128)S(1)} collective-permute-done((f32[256,1024]{1,0:T(8,128)}, f32[256,1024]{1,0:T(8,128)S(1)}, u32[]{:S(2)}, u32[]{:S(2)}) %collective-permute-start.7) | collective-permute-done | bytes 1048608 | tf_op jit(solution)/shard_map/ppermute | solution.py:364
  242.4 3.0 multiply_reduce_fusion.6
  245.5 0.1 stack.51
  245.5 0.1 stack.57
  245.6 0.1 collective-permute-start.11
  245.7 5.8 %collective-permute-done.11 = f32[6,2048]{1,0:T(8,128)S(1)} collective-permute-done((f32[6,2048]{1,0:T(8,128)S(1)}, f32[6,2048]{1,0:T(8,128)S(1)}, u32[]{:S(2)}, u32[]{:S(2)}) %collective-permute-start.11) | collective-permute-done | bytes 49184 | tf_op jit(solution)/shard_map/ppermute | solution.py:349
  251.5 0.1 collective-permute-start.12
  251.6 4.3 %collective-permute-done.12 = f32[6,2048]{1,0:T(8,128)S(1)} collective-permute-done((f32[6,2048]{1,0:T(8,128)S(1)}, f32[6,2048]{1,0:T(8,128)S(1)}, u32[]{:S(2)}, u32[]{:S(2)}) %collective-permute-start.12) | collective-permute-done | bytes 49184 | tf_op jit(solution)/shard_map/ppermute | solution.py:349
  255.8 16.3 %collective-permute-start.13 = (f32[6,2048]{1,0:T(8,128)S(1)}, f32[6,2048]{1,0:T(8,128)S(1)}, u32[]{:S(2)}, u32[]{:S(2)}) collective-permute-start(f32[6,2048]{1,0:T(8,128)S(1)} %add.48), channel_id=1, source_target_pairs={{0,8},{1,9},{2,10},{3,11},{4,12},{5,13},{6,14},{7,15},{8,0},{9,1},... | collective-permute-start | bytes 147464 | tf_op jit(solution)/shard_map/ppermute | solution.py:349
  272.1 2.9 collective-permute-done.13
  275.1 1.8 collective-permute-start.14
  276.8 2.6 collective-permute-done.14
  279.4 8.9 %collective-permute-start.15 = (f32[6,2048]{1,0:T(8,128)S(1)}, f32[6,2048]{1,0:T(8,128)S(1)}, u32[]{:S(2)}, u32[]{:S(2)}) collective-permute-start(f32[6,2048]{1,0:T(8,128)S(1)} %add.50), channel_id=1, source_target_pairs={{0,16},{1,17},{2,18},{3,19},{4,20},{5,21},{6,22},{7,23},{8,24},{9,... | collective-permute-start | bytes 147464 | tf_op jit(solution)/shard_map/ppermute | solution.py:349
  288.3 0.9 collective-permute-done.15
  289.2 1.2 collective-permute-start.16
  290.4 2.8 convolution_add_fusion.refs_10_
  293.3 1.9 collective-permute-done.16
  295.2 2.6 collective-permute-start.17
  297.8 2.8 convolution_add_fusion.1.refs_5_
  300.6 0.6 add.53.refs_0_
  301.2 9.3 %finish.1 = (f32[256,2048]{1,0:T(8,128)}, f32[256,2048]{1,0:T(8,128)}) custom-call(f32[6,2048]{1,0:T(8,128)} %add.53.refs_0_, f32[256,2048]{1,0:T(8,128)} %refs_1_.1, f32[256,2048]{1,0:T(8,128)} %copy-done.6, f32[256,1024]{1,0:T(8,128)} %copy-done.1, f32[256,1024]{1,0:T(8,128)} %copy-done.3, f32[256,1024]{1,0:T(8,128)} %convolution_add_fusion.1.refs_5_, ...), custom_call_target="tpu_custom_call" | custom-call | tf_op jit(solution)/shard_map/finish/pallas_call | solution.py:335
  (43 shorter events, 0.2 us)
Async XLA Ops:
  55.6 5.9 %copy-start.4 = (f32[256,2048]{1,0:T(8,128)S(1)}, f32[256,2048]{1,0:T(8,128)}, u32[]{:S(2)}) copy-start(f32[256,2048]{1,0:T(8,128)} %refs_1_.1) | copy-start | bytes 6291460
  55.6 40.7 %all-to-all-start = ((f32[128,40,128]{2,1,0:T(8,128)}), f32[128,40,128]{2,1,0:T(8,128)}, u32[]{:S(2)}, u32[]{:S(2)}) async-start(f32[128,40,128]{2,1,0:T(8,128)} %bitcast.50), calls=%async_computation | async-start | bytes 5242880 | tf_op jit(solution)/shard_map/all_to_all | solution.py:370
  61.5 107.0 %collective-permute-start.4 = (f32[256,2048]{1,0:T(8,128)S(1)}, f32[256,2048]{1,0:T(8,128)}, u32[]{:S(2)}, u32[]{:S(2)}) collective-permute-start(f32[256,2048]{1,0:T(8,128)S(1)} %copy-done.4), channel_id=1, source_target_pairs={{1,0},{2,1},{3,2},{4,3},{5,4},{6,5},{7,6},{8,7},{9,8},{10,9},{11,1... | collective-permute-start | bytes 6291464 | tf_op jit(solution)/shard_map/ppermute | solution.py:364
  68.5 101.8 %collective-permute-start.2 = (f32[256,2048]{1,0:T(8,128)S(1)}, f32[256,2048]{1,0:T(8,128)}, u32[]{:S(2)}, u32[]{:S(2)}) collective-permute-start(f32[256,2048]{1,0:T(8,128)S(1)} %copy-done.4), channel_id=1, source_target_pairs={{0,1},{1,2},{2,3},{3,4},{4,5},{5,6},{6,7},{7,8},{8,9},{9,10},{10,1... | collective-permute-start | bytes 6291464 | tf_op jit(solution)/shard_map/ppermute | solution.py:361
  105.9 38.5 %collective-permute-start = (f32[256,512]{1,0:T(8,128)}, f32[256,512]{1,0:T(8,128)S(1)}, u32[]{:S(2)}, u32[]{:S(2)}) collective-permute-start(f32[256,512]{1,0:T(8,128)} %get-tuple-element.18), channel_id=1, source_target_pairs={{0,1},{1,2},{2,3},{3,4},{4,5},{5,6},{6,7},{7,8},{8,9},{9,10},{10,1... | collective-permute-start | bytes 1572872 | tf_op jit(solution)/shard_map/ppermute | solution.py:361
  144.4 0.8 copy-start.11
  152.8 13.0 %collective-permute-start.1 = (f32[256,256]{1,0:T(8,128)}, f32[256,256]{1,0:T(8,128)S(1)}, u32[]{:S(2)}, u32[]{:S(2)}) collective-permute-start(f32[256,256]{1,0:T(8,128)} %invert.1), channel_id=1, source_target_pairs={{0,1},{1,2},{2,3},{3,4},{4,5},{5,6},{6,7},{7,8},{8,9},{9,10},{10,1... | collective-permute-start | bytes 786440 | tf_op jit(solution)/shard_map/ppermute | solution.py:361
  155.2 11.9 %collective-permute-start.3 = (f32[256,256]{1,0:T(8,128)}, f32[256,256]{1,0:T(8,128)S(1)}, u32[]{:S(2)}, u32[]{:S(2)}) collective-permute-start(f32[256,256]{1,0:T(8,128)} %invert.1), channel_id=1, source_target_pairs={{1,0},{2,1},{3,2},{4,3},{5,4},{6,5},{7,6},{8,7},{9,8},{10,9},{11,1... | collective-permute-start | bytes 786440 | tf_op jit(solution)/shard_map/ppermute | solution.py:364
  170.3 1.9 copy-start.9
  172.3 70.1 %copy-start = (f32[256,1024]{1,0:T(8,128)}, f32[256,1024]{1,0:T(8,128)S(1)}, u32[]{:S(2)}) copy-start(f32[256,1024]{1,0:T(8,128)S(1)} %convolution_add_fusion.3.refs_8_) | copy-start | bytes 3145732
  172.9 69.5 %copy-start.7 = (f32[256,1024]{1,0:T(8,128)}, f32[256,1024]{1,0:T(8,128)S(1)}, u32[]{:S(2)}) copy-start(f32[256,1024]{1,0:T(8,128)S(1)} %fusion.18.refs_11_) | copy-start | bytes 3145732
  172.9 24.4 %collective-permute-start.9 = (f32[256,1024]{1,0:T(8,128)S(1)}, f32[256,1024]{1,0:T(8,128)S(1)}, u32[]{:S(2)}, u32[]{:S(2)}) collective-permute-start(f32[256,1024]{1,0:T(8,128)S(1)} %fusion.18.refs_11_), channel_id=1, source_target_pairs={{1,0},{2,1},{3,2},{4,3},{5,4},{6,5},{7,6},{8,7},{9,8},{10,9},{11,1... | collective-permute-start | bytes 3145736 | tf_op jit(solution)/shard_map/ppermute | solution.py:364
  178.9 23.6 %collective-permute-start.8 = (f32[256,1024]{1,0:T(8,128)S(1)}, f32[256,1024]{1,0:T(8,128)S(1)}, u32[]{:S(2)}, u32[]{:S(2)}) collective-permute-start(f32[256,1024]{1,0:T(8,128)S(1)} %fusion.18.refs_11_), channel_id=1, source_target_pairs={{0,1},{1,2},{2,3},{3,4},{4,5},{5,6},{6,7},{7,8},{8,9},{9,10},{10,1... | collective-permute-start | bytes 3145736 | tf_op jit(solution)/shard_map/ppermute | solution.py:361
  180.7 16.6 %copy-start.10 = (f32[256,256]{1,0:T(8,128)S(1)}, f32[256,256]{1,0:T(8,128)}, u32[]{:S(2)}) copy-start(f32[256,256]{1,0:T(8,128)} %get-tuple-element.24) | copy-start | bytes 786436
  182.6 59.7 %copy-start.1 = (f32[256,1024]{1,0:T(8,128)}, f32[256,1024]{1,0:T(8,128)S(1)}, u32[]{:S(2)}) copy-start(f32[256,1024]{1,0:T(8,128)S(1)} %convolution_add_fusion.5.refs_3_) | copy-start | bytes 3145732
  182.7 19.8 %copy-start.12 = (f32[256,512]{1,0:T(8,128)S(1)}, f32[256,512]{1,0:T(8,128)}, u32[]{:S(2)}) copy-start(f32[256,512]{1,0:T(8,128)} %copy-done.11) | copy-start | bytes 1572868
  183.3 59.1 %copy-start.8 = (f32[256,1024]{1,0:T(8,128)}, f32[256,1024]{1,0:T(8,128)S(1)}, u32[]{:S(2)}) copy-start(f32[256,1024]{1,0:T(8,128)S(1)} %fusion.15.refs_6_) | copy-start | bytes 3145732
  183.3 36.5 %collective-permute-start.6 = (f32[256,1024]{1,0:T(8,128)S(1)}, f32[256,1024]{1,0:T(8,128)S(1)}, u32[]{:S(2)}, u32[]{:S(2)}) collective-permute-start(f32[256,1024]{1,0:T(8,128)S(1)} %fusion.15.refs_6_), channel_id=1, source_target_pairs={{1,0},{2,1},{3,2},{4,3},{5,4},{6,5},{7,6},{8,7},{9,8},{10,9},{11,1... | collective-permute-start | bytes 3145736 | tf_op jit(solution)/shard_map/ppermute | solution.py:364
  190.5 34.1 %collective-permute-start.5 = (f32[256,1024]{1,0:T(8,128)S(1)}, f32[256,1024]{1,0:T(8,128)S(1)}, u32[]{:S(2)}, u32[]{:S(2)}) collective-permute-start(f32[256,1024]{1,0:T(8,128)S(1)} %fusion.15.refs_6_), channel_id=1, source_target_pairs={{0,1},{1,2},{2,3},{3,4},{4,5},{5,6},{6,7},{7,8},{8,9},{9,10},{10,1... | collective-permute-start | bytes 3145736 | tf_op jit(solution)/shard_map/ppermute | solution.py:361
  203.1 39.3 %copy-start.2 = (f32[256,1024]{1,0:T(8,128)}, f32[256,1024]{1,0:T(8,128)S(1)}, u32[]{:S(2)}) copy-start(f32[256,1024]{1,0:T(8,128)S(1)} %convolution_add_fusion.2.refs_9_) | copy-start | bytes 3145732
  204.7 33.7 %collective-permute-start.10 = (f32[256,1024]{1,0:T(8,128)}, f32[256,1024]{1,0:T(8,128)S(1)}, u32[]{:S(2)}, u32[]{:S(2)}) collective-permute-start(f32[256,1024]{1,0:T(8,128)} %fusion.20.refs_12_), channel_id=1, source_target_pairs={{0,1},{1,2},{2,3},{3,4},{4,5},{5,6},{6,7},{7,8},{8,9},{9,10},{10,1... | collective-permute-start | bytes 3145736 | tf_op jit(solution)/shard_map/ppermute | solution.py:361
  220.5 6.4 %copy-start.5 = (f32[256,2048]{1,0:T(8,128)S(1)}, f32[256,2048]{1,0:T(8,128)}, u32[]{:S(2)}) copy-start(f32[256,2048]{1,0:T(8,128)} %refs_1_.1) | copy-start | bytes 6291460
  225.3 17.1 %copy-start.3 = (f32[256,1024]{1,0:T(8,128)}, f32[256,1024]{1,0:T(8,128)S(1)}, u32[]{:S(2)}) copy-start(f32[256,1024]{1,0:T(8,128)S(1)} %convolution_add_fusion.4.refs_4_) | copy-start | bytes 3145732
  226.9 15.5 %collective-permute-start.7 = (f32[256,1024]{1,0:T(8,128)}, f32[256,1024]{1,0:T(8,128)S(1)}, u32[]{:S(2)}, u32[]{:S(2)}) collective-permute-start(f32[256,1024]{1,0:T(8,128)} %fusion.17.refs_7_), channel_id=1, source_target_pairs={{1,0},{2,1},{3,2},{4,3},{5,4},{6,5},{7,6},{8,7},{9,8},{10,9},{11,1... | collective-permute-start | bytes 3145736 | tf_op jit(solution)/shard_map/ppermute | solution.py:364
  228.0 17.4 %copy-start.6 = (f32[256,2048]{1,0:T(8,128)}, f32[256,2048]{1,0:T(8,128)S(1)}, u32[]{:S(2)}) copy-start(f32[256,2048]{1,0:T(8,128)S(1)} %fusion.13.refs_2_) | copy-start | bytes 6291460
  228.0 69.8 %collective-permute-start.18 = (f32[256,1024]{1,0:T(8,128)}, f32[256,1024]{1,0:T(8,128)}, u32[]{:S(2)}, u32[]{:S(2)}) collective-permute-start(f32[256,1024]{1,0:T(8,128)} %fusion.17.refs_7_), channel_id=1, source_target_pairs={{0,1},{1,2},{2,3},{3,4},{4,5},{5,6},{6,7},{7,8},{8,9},{9,10},{10,1... | collective-permute-start | bytes 3145736 | tf_op jit(solution)/shard_map/ppermute | solution.py:361
  230.6 59.9 %collective-permute-start.19 = (f32[256,1024]{1,0:T(8,128)}, f32[256,1024]{1,0:T(8,128)}, u32[]{:S(2)}, u32[]{:S(2)}) collective-permute-start(f32[256,1024]{1,0:T(8,128)} %fusion.20.refs_12_), channel_id=1, source_target_pairs={{1,0},{2,1},{3,2},{4,3},{5,4},{6,5},{7,6},{8,7},{9,8},{10,9},{11,1... | collective-permute-start | bytes 3145736 | tf_op jit(solution)/shard_map/ppermute | solution.py:364
  245.6 5.8 %collective-permute-start.11 = (f32[6,2048]{1,0:T(8,128)S(1)}, f32[6,2048]{1,0:T(8,128)S(1)}, u32[]{:S(2)}, u32[]{:S(2)}) collective-permute-start(f32[6,2048]{1,0:T(8,128)S(1)} %pad_maximum_fusion), channel_id=1, source_target_pairs={{0,64},{1,65},{2,66},{3,67},{4,68},{5,69},{6,70},{7,71},{8,72},{9,... | collective-permute-start | bytes 147464 | tf_op jit(solution)/shard_map/ppermute | solution.py:349
  251.5 4.3 %collective-permute-start.12 = (f32[6,2048]{1,0:T(8,128)S(1)}, f32[6,2048]{1,0:T(8,128)S(1)}, u32[]{:S(2)}, u32[]{:S(2)}) collective-permute-start(f32[6,2048]{1,0:T(8,128)S(1)} %fusion.6), channel_id=1, source_target_pairs={{0,32},{1,33},{2,34},{3,35},{4,36},{5,37},{6,38},{7,39},{8,40},{9,... | collective-permute-start | bytes 147464 | tf_op jit(solution)/shard_map/ppermute | solution.py:349
  255.8 19.2 %collective-permute-start.13 = (f32[6,2048]{1,0:T(8,128)S(1)}, f32[6,2048]{1,0:T(8,128)S(1)}, u32[]{:S(2)}, u32[]{:S(2)}) collective-permute-start(f32[6,2048]{1,0:T(8,128)S(1)} %add.48), channel_id=1, source_target_pairs={{0,8},{1,9},{2,10},{3,11},{4,12},{5,13},{6,14},{7,15},{8,0},{9,1},... | collective-permute-start | bytes 147464 | tf_op jit(solution)/shard_map/ppermute | solution.py:349
  275.1 4.3 %collective-permute-start.14 = (f32[6,2048]{1,0:T(8,128)S(1)}, f32[6,2048]{1,0:T(8,128)S(1)}, u32[]{:S(2)}, u32[]{:S(2)}) collective-permute-start(f32[6,2048]{1,0:T(8,128)S(1)} %add.49), channel_id=1, source_target_pairs={{0,4},{1,5},{2,6},{3,7},{4,0},{5,1},{6,2},{7,3},{8,12},{9,13},{10,... | collective-permute-start | bytes 147464 | tf_op jit(solution)/shard_map/ppermute | solution.py:349
  279.4 18.4 %slice-start = ((f32[256,512]{1,0:T(8,128)}), f32[256,256]{1,0:T(8,128)S(1)}, s32[]{:S(2)}) async-start(f32[256,512]{1,0:T(8,128)} %copy-done.11), calls=%async_computation.2 | async-start | bytes 524288 | tf_op jit(solution)/shard_map/slice | solution.py:382
  279.4 9.8 %collective-permute-start.15 = (f32[6,2048]{1,0:T(8,128)S(1)}, f32[6,2048]{1,0:T(8,128)S(1)}, u32[]{:S(2)}, u32[]{:S(2)}) collective-permute-start(f32[6,2048]{1,0:T(8,128)S(1)} %add.50), channel_id=1, source_target_pairs={{0,16},{1,17},{2,18},{3,19},{4,20},{5,21},{6,22},{7,23},{8,24},{9,... | collective-permute-start | bytes 147464 | tf_op jit(solution)/shard_map/ppermute | solution.py:349
  289.2 5.9 %collective-permute-start.16 = (f32[6,2048]{1,0:T(8,128)S(1)}, f32[6,2048]{1,0:T(8,128)S(1)}, u32[]{:S(2)}, u32[]{:S(2)}) collective-permute-start(f32[6,2048]{1,0:T(8,128)S(1)} %add.51), channel_id=1, source_target_pairs={{0,2},{1,3},{2,0},{3,1},{4,6},{5,7},{6,4},{7,5},{8,10},{9,11},{10,... | collective-permute-start | bytes 147464 | tf_op jit(solution)/shard_map/ppermute | solution.py:349
  295.2 5.4 %collective-permute-start.17 = (f32[6,2048]{1,0:T(8,128)S(1)}, f32[6,2048]{1,0:T(8,128)S(1)}, u32[]{:S(2)}, u32[]{:S(2)}) collective-permute-start(f32[6,2048]{1,0:T(8,128)S(1)} %add.52), channel_id=1, source_target_pairs={{0,1},{1,0},{2,3},{3,2},{4,5},{5,4},{6,7},{7,6},{8,9},{9,8},{10,11... | collective-permute-start | bytes 147464 | tf_op jit(solution)/shard_map/ppermute | solution.py:349
where the time goes:
time: 313 us; the launch traced here: 311 us
  waiting for transfers between devices  94.3 us (30%)
  starting transfers between devices  79.5 us (25%)
  Pallas kernels  59.6 us (19%)
  blocking collectives  46.3 us (15%)
  matrix products  27.5 us (9%)
    ppermute x7, waiting for transfers between devices, from_below(): return lax.ppermute(x, AXES, up)  50.6 us
    all_to_all x1, blocking collectives, exchange(): lax.all_to_all(send.reshape(devices, ROWS, 128), AXES, split_axis=0, conc...  46.3 us
    pallas_call x2, Pallas kernels, assemble(): pl.pallas_call(lambda *refs: assemble_kernel(last, *refs), out_shape=out,...  34 us
    ppermute x6, starting transfers between devices, from_above(): return lax.ppermute(x, AXES, down)  31.3 us
    ppermute x7, starting transfers between devices, butterfly(): x = x + lax.ppermute(x, AXES, [(i, i ^ bit) for i in range(devices)])  30.9 us
    dot_general x19, matrix products, mm(): jnp.dot(left, right, precision=precision, preferred_element_type=jnp.floa...  27.5 us
    ppermute x6, waiting for transfers between devices, from_above(): return lax.ppermute(x, AXES, down)  22.7 us
    ppermute x7, waiting for transfers between devices, butterfly(): x = x + lax.ppermute(x, AXES, [(i, i ^ bit) for i in range(devices)])  18.3 us
  transfers between devices with their start and end apart: 21, of which 15 were waited for; matrix products, arithmetic and copies ran while one was open for 8% of the time, Pallas kernels for 13%

commit v1 on v0

--- a/solution.py
+++ b/solution.py
@@ -313,35 +313,36 @@
     return (1.0 - c0, c3 - c2, -c3), (c0, c1, c2, c3)
 
 
-def finish_kernel(blocks_half, sums_ref, v0, w0, *refs):
-    halves, (sol_ref, res_ref) = (refs[:5], refs[5:10]), refs[10:]
+def finish_kernel(per, sums_ref, v0, w0, v1, w1, *refs):
+    halves, (sol_ref, res_ref) = (refs[:3], refs[3:6]), refs[6:]
     x, c = coefficients([sums_ref[k : k + 1, :] for k in range(6)])
 
-    def write(v1, v2, v3, w1, w2):
+    def write(v2, v3, w2):
         sol_ref[...] = x[0] * w0[...] + x[1] * w1[...] + x[2] * w2[...]
         res_ref[...] = c[0] * v0[...] + c[1] * v1[...] + c[2] * v2[...] + c[3] * v3[...]
 
     for k in range(2):
-        pl.when(pl.program_id(0) // blocks_half == k)(lambda k=k: write(*halves[k]))
-
-
-def finish(sums, v0, w0, halves):
-    rows, _ = v0.shape
+        pl.when(pl.program_id(0) // per == k)(lambda k=k: write(*halves[k]))
+
+
+def finish(sums, wholes, halves):
+    rows, total = wholes[0].shape
     width = 256
-    per = halves[0][0].shape[1] // width
+    per = total // 2 // width
     whole = pl.BlockSpec((rows, width), lambda j: (0, j))
     left = pl.BlockSpec((rows, width), lambda j: (0, jnp.minimum(j, per - 1)))
     right = pl.BlockSpec((rows, width), lambda j: (0, jnp.maximum(j - per, 0)))
     return pl.pallas_call(
         lambda *refs: finish_kernel(per, *refs),
         grid=(2 * per,),
-        in_specs=[pl.BlockSpec((sums.shape[0], width), lambda j: (0, j)), whole, whole]
-        + [left] * 5
-        + [right] * 5,
+        in_specs=[pl.BlockSpec((sums.shape[0], width), lambda j: (0, j))]
+        + [whole] * 4
+        + [left] * 3
+        + [right] * 3,
         out_specs=(whole, whole),
-        out_shape=(jax.ShapeDtypeStruct(v0.shape, v0.dtype),) * 2,
+        out_shape=(jax.ShapeDtypeStruct((rows, total), jnp.float32),) * 2,
         name="finish",
-    )(sums, v0, w0, *halves[0], *halves[1])
+    )(sums, *wholes, *halves[0], *halves[1])
 
 
 def butterfly(x, devices, bits):
@@ -364,6 +365,8 @@
         return lax.ppermute(x, AXES, down)
 
     base = jnp.stack([lax.axis_index(AXES) * own, own * devices]).astype(jnp.int32)
+    v0_low = from_below(right_side)
+    v0_high = from_above(right_side)
     send0, send1 = pack(owner_map, connect.T, blocks, devices)
 
     def exchange(send):
@@ -374,8 +377,6 @@
 
     got0 = exchange(send0)
     got1 = exchange(send1)
-    v0, got0 = lax.optimization_barrier((right_side, got0))
-    v0_low, v0_high = from_below(v0), from_above(v0)
     part = assemble(base, got0, window)
     center, high_band, lower = assemble(base, got1, window, part)
     lower = from_below(lower)
@@ -389,28 +390,27 @@
     def part_of(x, h):
         return lax.slice_in_dim(x, h * width, (h + 1) * width, axis=1)
 
-    v1, w1, w1_low, w1_high = {}, {}, {}, {}
-    for h in range(2):
-        v1[h] = mm(near_low, part_of(v0_low, h)) + mm(near_high, part_of(v0_high, h))
-        w1[h] = mm(inv, v1[h])
-        w1_low[h] = from_below(w1[h])
-        w1_high[h] = from_above(w1[h])
+    v1 = mm(near_low, v0_low) + mm(near_high, v0_high)
+    w1 = mm(inv, v1)
+    w1_low, w1_high = from_below(w1), from_above(w1)
     w0 = mm(inv, right_side)
     v2, w2 = {}, {}
     for h in range(2):
-        v2[h] = mm(low_band, w1_low[h]) + mm(high_band, w1_high[h])
+        v2[h] = mm(low_band, part_of(w1_low, h)) + mm(high_band, part_of(w1_high, h))
         w2[h] = mm(inv, v2[h])
     w2_high, w2_low = {}, {}
     w2_high[0] = from_above(w2[0])
     w2_low[1] = from_below(w2[1])
-    later0, later1 = lax.optimization_barrier((w2[0], w2[1]))
+    w2_high[0], w2_low[1], later0, later1 = lax.optimization_barrier(
+        (w2_high[0], w2_low[1], w2[0], w2[1])
+    )
     w2_low[0] = from_below(later0)
     w2_high[1] = from_above(later1)
     side = {0: mm(high_band, w2_high[0]), 1: mm(low_band, w2_low[1])}
     sums = []
     for h in range(2):
-        v0h, w0h = part_of(right_side, h), part_of(w0, h)
-        pairs = [(v0h, w0h), (v1[h], w0h), (v1[h], w1[h]), (v2[h], w1[h]), (v2[h], w2[h])]
+        v0h, w0h, v1h, w1h = (part_of(x, h) for x in (right_side, w0, v1, w1))
+        pairs = [(v0h, w0h), (v1h, w0h), (v1h, w1h), (v2[h], w1h), (v2[h], w2[h])]
         rows = [column_sums(*pair) for pair in pairs] + [2.0 * column_sums(side[h], w2[h])]
         sums.append(jnp.stack(rows))
     sums = jnp.concatenate(sums, axis=1)
@@ -418,7 +418,7 @@
     sums, low_late, high_late = lax.optimization_barrier((sums, low_band, high_band))
     v3 = {0: side[0] + mm(low_late, w2_low[0]), 1: side[1] + mm(high_late, w2_high[1])}
     sums = butterfly(sums, devices, (2, 1))
-    return finish(sums, right_side, w0, [(v1[h], v2[h], v3[h], w1[h], w2[h]) for h in range(2)])
+    return finish(sums, (right_side, w0, v1, w1), [(v2[h], v3[h], w2[h]) for h in range(2)])
 
 
 def solution(mesh):

time: 313 us -> 329 us (1.051)
  waiting for transfers between devices: 94.3 us -> 145 us
  starting transfers between devices: 79.5 us -> 47.8 us
  matrix products: 27.5 us -> 22 us
    ppermute x7, starting transfers between devices: 30.9 us -> 5.76 us  [butterfly(): x = x + lax.ppermute(x, AXES, [(i, i ^ bit) for i in range(devices)])]
    ppermute x7, waiting for transfers between devices: 18.3 us -> 40.5 us  [butterfly(): x = x + lax.ppermute(x, AXES, [(i, i ^ bit) for i in range(devices)])]
    ppermute x6 -> x5, waiting for transfers between devices: 22.7 us -> 43.6 us  [from_above(): return lax.ppermute(x, AXES, down)]
    ppermute x7 -> x6, waiting for transfers between devices: 50.6 us -> 58 us  [from_below(): return lax.ppermute(x, AXES, up)]
    ppermute x6 -> x5, starting transfers between devices: 31.3 us -> 25 us  [from_above(): return lax.ppermute(x, AXES, down)]
    dot_general x19 -> x16, matrix products: 27.5 us -> 22 us  [mm(): jnp.dot(left, right, precision=precision, preferred_element_type=jnp.floa...]
    ppermute x7 -> x6, starting transfers between devices: 11.4 us -> 11.2 us  [from_below(): return lax.ppermute(x, AXES, up)]
  transfers between devices with their start and end apart: 21 -> 19, of which waited for: 15 -> 14; matrix products, arithmetic and copies ran while one was open for 8% -> 5% of each run, Pallas kernels for 13% -> 13%
where the time goes in v1:
time: 329 us; the launch traced here: 324 us
  waiting for transfers between devices  145 us (44%)
  Pallas kernels  59.5 us (18%)
  starting transfers between devices  47.8 us (15%)
  blocking collectives  46.3 us (14%)
  matrix products  22 us (7%)
    ppermute x6, waiting for transfers between devices, from_below(): return lax.ppermute(x, AXES, up)  58 us
    all_to_all x1, blocking collectives, exchange(): lax.all_to_all(send.reshape(devices, ROWS, 128), AXES, split_axis=0, conc...  46.3 us
    ppermute x5, waiting for transfers between devices, from_above(): return lax.ppermute(x, AXES, down)  43.6 us
    ppermute x7, waiting for transfers between devices, butterfly(): x = x + lax.ppermute(x, AXES, [(i, i ^ bit) for i in range(devices)])  40.5 us
    pallas_call x2, Pallas kernels, assemble(): pl.pallas_call(lambda *refs: assemble_kernel(last, *refs), out_shape=out,...  34 us
    ppermute x5, starting transfers between devices, from_above(): return lax.ppermute(x, AXES, down)  25 us
    dot_general x16, matrix products, mm(): jnp.dot(left, right, precision=precision, preferred_element_type=jnp.floa...  22 us
    ppermute x6, starting transfers between devices, from_below(): return lax.ppermute(x, AXES, up)  11.2 us
  transfers between devices with their start and end apart: 19, of which 14 were waited for; matrix products, arithmetic and copies ran while one was open for 5% of the time, Pallas kernels for 13%

profile of v1, /device:TPU:0, one launch (start us, length us, event | category | flops | bytes accessed | tf_op | source)
XLA Modules:
  0.0 323.8 jit_solution(14326062217555901385)
XLA Ops:
  0.6 8.7 %pack.1 = (f32[5120,128]{1,0:T(8,128)}, f32[5120,128]{1,0:T(8,128)}) custom-call(s32[1,128]{1,0:T(1,128)} %bitcast.59, s32[96,128]{1,0:T(8,128)} %bitcast.46, f32[128,9216]{1,0:T(8,128)} %x_ref.1), custom_call_target="tpu_custom_call" | custom-call | tf_op jit(solution)/shard_map/pack/pallas_call | solution.py:96
  9.3 46.3 %all_to_all.10 = f32[128,40,128]{2,1,0:T(8,128)} all-to-all(f32[128,40,128]{2,1,0:T(8,128)} %bitcast.45), channel_id=1, replica_groups=mesh['row'=8,'col'=16] {'row','col'}, dimensions={0} | all-to-all | bytes 5242880 | tf_op jit(solution)/shard_map/all_to_all | solution.py:373
  55.6 5.9 %all-to-all-start = ((f32[128,40,128]{2,1,0:T(8,128)}), f32[128,40,128]{2,1,0:T(8,128)}, u32[]{:S(2)}, u32[]{:S(2)}) async-start(f32[128,40,128]{2,1,0:T(8,128)} %bitcast.44), calls=%async_computation | async-start | bytes 5242880 | tf_op jit(solution)/shard_map/all_to_all | solution.py:373
  61.5 7.0 %collective-permute-start.4 = (f32[256,2048]{1,0:T(8,128)S(1)}, f32[256,2048]{1,0:T(8,128)}, u32[]{:S(2)}, u32[]{:S(2)}) collective-permute-start(f32[256,2048]{1,0:T(8,128)S(1)} %copy-done.3), channel_id=1, source_target_pairs={{1,0},{2,1},{3,2},{4,3},{5,4},{6,5},{7,6},{8,7},{9,8},{10,9},{11,1... | collective-permute-start | bytes 6291464 | tf_op jit(solution)/shard_map/ppermute | solution.py:365
  68.6 0.0 collective-permute-start.2
  68.6 0.6 pad_add_fusion.refs_0_
  69.2 24.4 %assemble_first.1.refs_2_ = f32[512,512]{1,0:T(8,128)} custom-call(s32[2]{0:T(128)} %pad_add_fusion.refs_0_, f32[5120,128]{1,0:T(8,128)} %bitcast.43), custom_call_target="tpu_custom_call" | custom-call | tf_op jit(solution)/shard_map/assemble_first/pallas_call | solution.py:241
  93.6 2.7 all-to-all-done
  96.3 9.6 %assemble_last.1 = (f32[256,256]{1,0:T(8,128)}, f32[256,256]{1,0:T(8,128)}, f32[256,512]{1,0:T(8,128)}) custom-call(s32[2]{0:T(128)} %pad_add_fusion.refs_0_, f32[5120,128]{1,0:T(8,128)} %bitcast.4.refs_1_, f32[512,512]{1,0:T(8,128)} %assemble_first.1.refs_2_), custom_call_target="tpu_custom_call" | custom-call | tf_op jit(solution)/shard_map/assemble_last/pallas_call | solution.py:241
  105.9 4.0 %collective-permute-start = (f32[256,512]{1,0:T(8,128)}, f32[256,512]{1,0:T(8,128)S(1)}, u32[]{:S(2)}, u32[]{:S(2)}) collective-permute-start(f32[256,512]{1,0:T(8,128)} %get-tuple-element.17), channel_id=1, source_target_pairs={{0,1},{1,2},{2,3},{3,4},{4,5},{5,6},{6,7},{7,8},{8,9},{9,10},{10,1... | collective-permute-start | bytes 1572872 | tf_op jit(solution)/shard_map/ppermute | solution.py:362
  109.9 34.6 %collective-permute-done.lower_ref = f32[256,512]{1,0:T(8,128)S(1)} collective-permute-done((f32[256,512]{1,0:T(8,128)}, f32[256,512]{1,0:T(8,128)S(1)}, u32[]{:S(2)}, u32[]{:S(2)}) %collective-permute-start) | collective-permute-done | bytes 524320 | tf_op jit(solution)/shard_map/ppermute | solution.py:362
  144.5 0.8 copy-done.11
  145.2 7.6 %invert.1 = f32[256,256]{1,0:T(8,128)} custom-call(f32[256,256]{1,0:T(8,128)} %get-tuple-element.16.upper_ref, f32[256,512]{1,0:T(8,128)} %copy-done.11), custom_call_target="tpu_custom_call" | custom-call | tf_op jit(solution)/shard_map/invert/pallas_call | solution.py:278
  152.9 2.4 collective-permute-start.1
  155.2 6.3 %collective-permute-start.3 = (f32[256,256]{1,0:T(8,128)}, f32[256,256]{1,0:T(8,128)S(1)}, u32[]{:S(2)}, u32[]{:S(2)}) collective-permute-start(f32[256,256]{1,0:T(8,128)} %invert.1), channel_id=1, source_target_pairs={{1,0},{2,1},{3,2},{4,3},{5,4},{6,5},{7,6},{8,7},{9,8},{10,9},{11,1... | collective-permute-start | bytes 786440 | tf_op jit(solution)/shard_map/ppermute | solution.py:365
  161.6 4.3 %collective-permute-done.1 = f32[256,256]{1,0:T(8,128)S(1)} collective-permute-done((f32[256,256]{1,0:T(8,128)}, f32[256,256]{1,0:T(8,128)S(1)}, u32[]{:S(2)}, u32[]{:S(2)}) %collective-permute-start.1) | collective-permute-done | bytes 262176 | tf_op jit(solution)/shard_map/ppermute | solution.py:362
  165.8 1.3 fusion.11
  167.2 1.3 fusion.14
  168.5 0.0 collective-permute-done.4
  168.5 2.6 fusion.15
  171.2 0.0 copy-start.9
  171.2 0.0 collective-permute-done.2
  171.2 2.8 convolution_add_fusion.refs_3_
  174.0 1.1 fusion.16.refs_4_
  175.1 0.0 copy-start.12
  175.1 6.0 %collective-permute-start.6 = (f32[256,2048]{1,0:T(8,128)S(1)}, f32[256,2048]{1,0:T(8,128)S(1)}, u32[]{:S(2)}, u32[]{:S(2)}) collective-permute-start(f32[256,2048]{1,0:T(8,128)S(1)} %fusion.16.refs_4_), channel_id=1, source_target_pairs={{1,0},{2,1},{3,2},{4,3},{5,4},{6,5},{7,6},{8,7},{9,8},{10,9},{11,1... | collective-permute-start | bytes 6291464 | tf_op jit(solution)/shard_map/ppermute | solution.py:365
  181.1 0.0 collective-permute-start.5
  181.1 40.9 %collective-permute-done.6 = f32[256,2048]{1,0:T(8,128)S(1)} collective-permute-done((f32[256,2048]{1,0:T(8,128)S(1)}, f32[256,2048]{1,0:T(8,128)S(1)}, u32[]{:S(2)}, u32[]{:S(2)}) %collective-permute-start.6) | collective-permute-done | bytes 2097184 | tf_op jit(solution)/shard_map/ppermute | solution.py:365
  222.0 0.6 fusion.3
  222.7 4.2 %collective-permute-done.5 = f32[256,2048]{1,0:T(8,128)S(1)} collective-permute-done((f32[256,2048]{1,0:T(8,128)S(1)}, f32[256,2048]{1,0:T(8,128)S(1)}, u32[]{:S(2)}, u32[]{:S(2)}) %collective-permute-start.5) | collective-permute-done | bytes 2097184 | tf_op jit(solution)/shard_map/ppermute | solution.py:362
  226.8 0.7 convolution_add_fusion.4.refs_5_
  227.5 0.6 fusion.17.refs_7_
  228.1 0.6 fusion
  228.8 0.0 copy-start.4
  228.8 0.7 convolution_add_fusion.3.refs_8_
  229.5 0.6 fusion.18.refs_10_
  230.1 2.6 collective-permute-start.8
  232.7 4.7 %collective-permute-start.7 = (f32[256,1024]{1,0:T(8,128)S(1)}, f32[256,1024]{1,0:T(8,128)S(1)}, u32[]{:S(2)}, u32[]{:S(2)}) collective-permute-start(f32[256,1024]{1,0:T(8,128)S(1)} %fusion.17.refs_7_), channel_id=1, source_target_pairs={{1,0},{2,1},{3,2},{4,3},{5,4},{6,5},{7,6},{8,7},{9,8},{10,9},{11,1... | collective-permute-start | bytes 3145736 | tf_op jit(solution)/shard_map/ppermute | solution.py:365
  237.4 1.1 fusion.13.refs_2_
  238.5 15.0 %collective-permute-done.8 = f32[256,1024]{1,0:T(8,128)S(1)} collective-permute-done((f32[256,1024]{1,0:T(8,128)S(1)}, f32[256,1024]{1,0:T(8,128)S(1)}, u32[]{:S(2)}, u32[]{:S(2)}) %collective-permute-start.8) | collective-permute-done | bytes 1048608 | tf_op jit(solution)/shard_map/ppermute | solution.py:362
  253.5 2.7 collective-permute-done.7
  256.2 1.0 collective-permute-start.17
  257.1 0.7 fusion.7
  257.8 2.8 multiply_reduce_fusion.6
  260.7 0.1 stack.57
  260.8 0.1 collective-permute-start.9
  260.9 2.3 collective-permute-start.16
  263.2 3.5 %collective-permute-done.9 = f32[6,2048]{1,0:T(8,128)S(1)} collective-permute-done((f32[6,2048]{1,0:T(8,128)S(1)}, f32[6,2048]{1,0:T(8,128)S(1)}, u32[]{:S(2)}, u32[]{:S(2)}) %collective-permute-start.9) | collective-permute-done | bytes 49184 | tf_op jit(solution)/shard_map/ppermute | solution.py:350
  266.7 0.1 collective-permute-start.10
  266.8 4.3 %collective-permute-done.10 = f32[6,2048]{1,0:T(8,128)S(1)} collective-permute-done((f32[6,2048]{1,0:T(8,128)S(1)}, f32[6,2048]{1,0:T(8,128)S(1)}, u32[]{:S(2)}, u32[]{:S(2)}) %collective-permute-start.10) | collective-permute-done | bytes 49184 | tf_op jit(solution)/shard_map/ppermute | solution.py:350
  271.0 4.5 %collective-permute-start.11 = (f32[6,2048]{1,0:T(8,128)S(1)}, f32[6,2048]{1,0:T(8,128)S(1)}, u32[]{:S(2)}, u32[]{:S(2)}) collective-permute-start(f32[6,2048]{1,0:T(8,128)S(1)} %add.44), channel_id=1, source_target_pairs={{0,8},{1,9},{2,10},{3,11},{4,12},{5,13},{6,14},{7,15},{8,0},{9,1},... | collective-permute-start | bytes 147464 | tf_op jit(solution)/shard_map/ppermute | solution.py:350
  275.5 17.5 %collective-permute-done.11 = f32[6,2048]{1,0:T(8,128)S(1)} collective-permute-done((f32[6,2048]{1,0:T(8,128)S(1)}, f32[6,2048]{1,0:T(8,128)S(1)}, u32[]{:S(2)}, u32[]{:S(2)}) %collective-permute-start.11) | collective-permute-done | bytes 49184 | tf_op jit(solution)/shard_map/ppermute | solution.py:350
  293.0 0.1 collective-permute-start.12
  293.1 4.3 %collective-permute-done.12 = f32[6,2048]{1,0:T(8,128)S(1)} collective-permute-done((f32[6,2048]{1,0:T(8,128)S(1)}, f32[6,2048]{1,0:T(8,128)S(1)}, u32[]{:S(2)}, u32[]{:S(2)}) %collective-permute-start.12) | collective-permute-done | bytes 49184 | tf_op jit(solution)/shard_map/ppermute | solution.py:350
  297.4 0.9 collective-permute-start.13
  298.2 0.9 collective-permute-done.13
  299.1 0.1 collective-permute-start.14
  299.2 5.8 %collective-permute-done.14 = f32[6,2048]{1,0:T(8,128)S(1)} collective-permute-done((f32[6,2048]{1,0:T(8,128)S(1)}, f32[6,2048]{1,0:T(8,128)S(1)}, u32[]{:S(2)}, u32[]{:S(2)}) %collective-permute-start.14) | collective-permute-done | bytes 49184 | tf_op jit(solution)/shard_map/ppermute | solution.py:350
  305.1 0.1 collective-permute-start.15
  305.2 4.3 %collective-permute-done.15 = f32[6,2048]{1,0:T(8,128)S(1)} collective-permute-done((f32[6,2048]{1,0:T(8,128)S(1)}, f32[6,2048]{1,0:T(8,128)S(1)}, u32[]{:S(2)}, u32[]{:S(2)}) %collective-permute-start.15) | collective-permute-done | bytes 49184 | tf_op jit(solution)/shard_map/ppermute | solution.py:350
  309.4 0.6 add.49.refs_0_
  310.1 2.8 convolution_add_fusion.1.refs_9_
  312.9 1.6 convolution_add_fusion.2.refs_6_
  314.5 9.2 %finish.1 = (f32[256,2048]{1,0:T(8,128)}, f32[256,2048]{1,0:T(8,128)}) custom-call(f32[6,2048]{1,0:T(8,128)} %add.49.refs_0_, f32[256,2048]{1,0:T(8,128)} %refs_1_.1, f32[256,2048]{1,0:T(8,128)} %copy-done.6, f32[256,2048]{1,0:T(8,128)} %copy-done, f32[256,2048]{1,0:T(8,128)} %copy-done.5, f32[256,1024]{1,0:T(8,128)} %copy-done.1, ...), custom_call_target="tpu_custom_call" | custom-call | tf_op jit(solution)/shard_map/finish/pallas_call | solution.py:335
  (38 shorter events, 0.2 us)
Async XLA Ops:
  55.6 5.9 %copy-start.3 = (f32[256,2048]{1,0:T(8,128)S(1)}, f32[256,2048]{1,0:T(8,128)}, u32[]{:S(2)}) copy-start(f32[256,2048]{1,0:T(8,128)} %refs_1_.1) | copy-start | bytes 6291460
  55.6 40.7 %all-to-all-start = ((f32[128,40,128]{2,1,0:T(8,128)}), f32[128,40,128]{2,1,0:T(8,128)}, u32[]{:S(2)}, u32[]{:S(2)}) async-start(f32[128,40,128]{2,1,0:T(8,128)} %bitcast.44), calls=%async_computation | async-start | bytes 5242880 | tf_op jit(solution)/shard_map/all_to_all | solution.py:373
  61.5 107.0 %collective-permute-start.4 = (f32[256,2048]{1,0:T(8,128)S(1)}, f32[256,2048]{1,0:T(8,128)}, u32[]{:S(2)}, u32[]{:S(2)}) collective-permute-start(f32[256,2048]{1,0:T(8,128)S(1)} %copy-done.3), channel_id=1, source_target_pairs={{1,0},{2,1},{3,2},{4,3},{5,4},{6,5},{7,6},{8,7},{9,8},{10,9},{11,1... | collective-permute-start | bytes 6291464 | tf_op jit(solution)/shard_map/ppermute | solution.py:365
  68.6 102.6 %collective-permute-start.2 = (f32[256,2048]{1,0:T(8,128)S(1)}, f32[256,2048]{1,0:T(8,128)}, u32[]{:S(2)}, u32[]{:S(2)}) collective-permute-start(f32[256,2048]{1,0:T(8,128)S(1)} %copy-done.3), channel_id=1, source_target_pairs={{0,1},{1,2},{2,3},{3,4},{4,5},{5,6},{6,7},{7,8},{8,9},{9,10},{10,1... | collective-permute-start | bytes 6291464 | tf_op jit(solution)/shard_map/ppermute | solution.py:362
  105.9 38.5 %collective-permute-start = (f32[256,512]{1,0:T(8,128)}, f32[256,512]{1,0:T(8,128)S(1)}, u32[]{:S(2)}, u32[]{:S(2)}) collective-permute-start(f32[256,512]{1,0:T(8,128)} %get-tuple-element.17), channel_id=1, source_target_pairs={{0,1},{1,2},{2,3},{3,4},{4,5},{5,6},{6,7},{7,8},{8,9},{9,10},{10,1... | collective-permute-start | bytes 1572872 | tf_op jit(solution)/shard_map/ppermute | solution.py:362
  144.4 0.8 copy-start.11
  152.9 13.0 %collective-permute-start.1 = (f32[256,256]{1,0:T(8,128)}, f32[256,256]{1,0:T(8,128)S(1)}, u32[]{:S(2)}, u32[]{:S(2)}) collective-permute-start(f32[256,256]{1,0:T(8,128)} %invert.1), channel_id=1, source_target_pairs={{0,1},{1,2},{2,3},{3,4},{4,5},{5,6},{6,7},{7,8},{8,9},{9,10},{10,1... | collective-permute-start | bytes 786440 | tf_op jit(solution)/shard_map/ppermute | solution.py:362
  155.2 11.9 %collective-permute-start.3 = (f32[256,256]{1,0:T(8,128)}, f32[256,256]{1,0:T(8,128)S(1)}, u32[]{:S(2)}, u32[]{:S(2)}) collective-permute-start(f32[256,256]{1,0:T(8,128)} %invert.1), channel_id=1, source_target_pairs={{1,0},{2,1},{3,2},{4,3},{5,4},{6,5},{7,6},{8,7},{9,8},{10,9},{11,1... | collective-permute-start | bytes 786440 | tf_op jit(solution)/shard_map/ppermute | solution.py:365
  171.2 2.8 copy-start.9
  174.0 83.8 %copy-start = (f32[256,2048]{1,0:T(8,128)}, f32[256,2048]{1,0:T(8,128)S(1)}, u32[]{:S(2)}) copy-start(f32[256,2048]{1,0:T(8,128)S(1)} %convolution_add_fusion.refs_3_) | copy-start | bytes 6291460
  174.0 48.1 %copy-start.10 = (f32[256,256]{1,0:T(8,128)S(1)}, f32[256,256]{1,0:T(8,128)}, u32[]{:S(2)}) copy-start(f32[256,256]{1,0:T(8,128)} %get-tuple-element.24) | copy-start | bytes 786436
  175.1 82.7 %copy-start.5 = (f32[256,2048]{1,0:T(8,128)}, f32[256,2048]{1,0:T(8,128)S(1)}, u32[]{:S(2)}) copy-start(f32[256,2048]{1,0:T(8,128)S(1)} %fusion.16.refs_4_) | copy-start | bytes 6291460
  175.1 51.7 %copy-start.12 = (f32[256,512]{1,0:T(8,128)S(1)}, f32[256,512]{1,0:T(8,128)}, u32[]{:S(2)}) copy-start(f32[256,512]{1,0:T(8,128)} %copy-done.11) | copy-start | bytes 1572868
  175.1 46.9 %collective-permute-start.6 = (f32[256,2048]{1,0:T(8,128)S(1)}, f32[256,2048]{1,0:T(8,128)S(1)}, u32[]{:S(2)}, u32[]{:S(2)}) collective-permute-start(f32[256,2048]{1,0:T(8,128)S(1)} %fusion.16.refs_4_), channel_id=1, source_target_pairs={{1,0},{2,1},{3,2},{4,3},{5,4},{6,5},{7,6},{8,7},{9,8},{10,9},{11,1... | collective-permute-start | bytes 6291464 | tf_op jit(solution)/shard_map/ppermute | solution.py:365
  181.1 45.7 %collective-permute-start.5 = (f32[256,2048]{1,0:T(8,128)S(1)}, f32[256,2048]{1,0:T(8,128)S(1)}, u32[]{:S(2)}, u32[]{:S(2)}) collective-permute-start(f32[256,2048]{1,0:T(8,128)S(1)} %fusion.16.refs_4_), channel_id=1, source_target_pairs={{0,1},{1,2},{2,3},{3,4},{4,5},{5,6},{6,7},{7,8},{8,9},{9,10},{10,1... | collective-permute-start | bytes 6291464 | tf_op jit(solution)/shard_map/ppermute | solution.py:362
  227.5 30.3 %copy-start.1 = (f32[256,1024]{1,0:T(8,128)}, f32[256,1024]{1,0:T(8,128)S(1)}, u32[]{:S(2)}) copy-start(f32[256,1024]{1,0:T(8,128)S(1)} %convolution_add_fusion.4.refs_5_) | copy-start | bytes 3145732
  228.1 32.8 %copy-start.7 = (f32[256,1024]{1,0:T(8,128)}, f32[256,1024]{1,0:T(8,128)S(1)}, u32[]{:S(2)}) copy-start(f32[256,1024]{1,0:T(8,128)S(1)} %fusion.17.refs_7_) | copy-start | bytes 3145732
  228.8 8.6 %copy-start.4 = (f32[256,2048]{1,0:T(8,128)S(1)}, f32[256,2048]{1,0:T(8,128)}, u32[]{:S(2)}) copy-start(f32[256,2048]{1,0:T(8,128)} %refs_1_.1) | copy-start | bytes 6291460
  229.5 28.3 %copy-start.2 = (f32[256,1024]{1,0:T(8,128)}, f32[256,1024]{1,0:T(8,128)S(1)}, u32[]{:S(2)}) copy-start(f32[256,1024]{1,0:T(8,128)S(1)} %convolution_add_fusion.3.refs_8_) | copy-start | bytes 3145732
  230.1 27.7 %copy-start.8 = (f32[256,1024]{1,0:T(8,128)}, f32[256,1024]{1,0:T(8,128)S(1)}, u32[]{:S(2)}) copy-start(f32[256,1024]{1,0:T(8,128)S(1)} %fusion.18.refs_10_) | copy-start | bytes 3145732
  230.1 23.4 %collective-permute-start.8 = (f32[256,1024]{1,0:T(8,128)S(1)}, f32[256,1024]{1,0:T(8,128)S(1)}, u32[]{:S(2)}, u32[]{:S(2)}) collective-permute-start(f32[256,1024]{1,0:T(8,128)S(1)} %fusion.18.refs_10_), channel_id=1, source_target_pairs={{0,1},{1,2},{2,3},{3,4},{4,5},{5,6},{6,7},{7,8},{8,9},{9,10},{10,1... | collective-permute-start | bytes 3145736 | tf_op jit(solution)/shard_map/ppermute | solution.py:362
  232.7 23.5 %collective-permute-start.7 = (f32[256,1024]{1,0:T(8,128)S(1)}, f32[256,1024]{1,0:T(8,128)S(1)}, u32[]{:S(2)}, u32[]{:S(2)}) collective-permute-start(f32[256,1024]{1,0:T(8,128)S(1)} %fusion.17.refs_7_), channel_id=1, source_target_pairs={{1,0},{2,1},{3,2},{4,3},{5,4},{6,5},{7,6},{8,7},{9,8},{10,9},{11,1... | collective-permute-start | bytes 3145736 | tf_op jit(solution)/shard_map/ppermute | solution.py:365
  238.5 22.2 %copy-start.6 = (f32[256,2048]{1,0:T(8,128)}, f32[256,2048]{1,0:T(8,128)S(1)}, u32[]{:S(2)}) copy-start(f32[256,2048]{1,0:T(8,128)S(1)} %fusion.13.refs_2_) | copy-start | bytes 6291460
  256.2 53.9 %collective-permute-start.17 = (f32[256,1024]{1,0:T(8,128)S(1)}, f32[256,1024]{1,0:T(8,128)}, u32[]{:S(2)}, u32[]{:S(2)}) collective-permute-start(f32[256,1024]{1,0:T(8,128)S(1)} %fusion.18.refs_10_), channel_id=1, source_target_pairs={{1,0},{2,1},{3,2},{4,3},{5,4},{6,5},{7,6},{8,7},{9,8},{10,9},{11,1... | collective-permute-start | bytes 3145736 | tf_op jit(solution)/shard_map/ppermute | solution.py:365
  260.8 5.8 %collective-permute-start.9 = (f32[6,2048]{1,0:T(8,128)S(1)}, f32[6,2048]{1,0:T(8,128)S(1)}, u32[]{:S(2)}, u32[]{:S(2)}) collective-permute-start(f32[6,2048]{1,0:T(8,128)S(1)} %pad_maximum_fusion), channel_id=1, source_target_pairs={{0,64},{1,65},{2,66},{3,67},{4,68},{5,69},{6,70},{7,71},{8,72},{9,... | collective-permute-start | bytes 147464 | tf_op jit(solution)/shard_map/ppermute | solution.py:350
  260.9 52.0 %collective-permute-start.16 = (f32[256,1024]{1,0:T(8,128)S(1)}, f32[256,1024]{1,0:T(8,128)S(1)}, u32[]{:S(2)}, u32[]{:S(2)}) collective-permute-start(f32[256,1024]{1,0:T(8,128)S(1)} %fusion.17.refs_7_), channel_id=1, source_target_pairs={{0,1},{1,2},{2,3},{3,4},{4,5},{5,6},{6,7},{7,8},{8,9},{9,10},{10,1... | collective-permute-start | bytes 3145736 | tf_op jit(solution)/shard_map/ppermute | solution.py:362
  266.7 4.3 %collective-permute-start.10 = (f32[6,2048]{1,0:T(8,128)S(1)}, f32[6,2048]{1,0:T(8,128)S(1)}, u32[]{:S(2)}, u32[]{:S(2)}) collective-permute-start(f32[6,2048]{1,0:T(8,128)S(1)} %fusion.6), channel_id=1, source_target_pairs={{0,32},{1,33},{2,34},{3,35},{4,36},{5,37},{6,38},{7,39},{8,40},{9,... | collective-permute-start | bytes 147464 | tf_op jit(solution)/shard_map/ppermute | solution.py:350
  271.0 22.0 %collective-permute-start.11 = (f32[6,2048]{1,0:T(8,128)S(1)}, f32[6,2048]{1,0:T(8,128)S(1)}, u32[]{:S(2)}, u32[]{:S(2)}) collective-permute-start(f32[6,2048]{1,0:T(8,128)S(1)} %add.44), channel_id=1, source_target_pairs={{0,8},{1,9},{2,10},{3,11},{4,12},{5,13},{6,14},{7,15},{8,0},{9,1},... | collective-permute-start | bytes 147464 | tf_op jit(solution)/shard_map/ppermute | solution.py:350
  293.0 4.3 %collective-permute-start.12 = (f32[6,2048]{1,0:T(8,128)S(1)}, f32[6,2048]{1,0:T(8,128)S(1)}, u32[]{:S(2)}, u32[]{:S(2)}) collective-permute-start(f32[6,2048]{1,0:T(8,128)S(1)} %add.45), channel_id=1, source_target_pairs={{0,4},{1,5},{2,6},{3,7},{4,0},{5,1},{6,2},{7,3},{8,12},{9,13},{10,... | collective-permute-start | bytes 147464 | tf_op jit(solution)/shard_map/ppermute | solution.py:350
  297.4 1.8 collective-permute-start.13
  298.2 14.7 %slice-start = ((f32[256,512]{1,0:T(8,128)}), f32[256,256]{1,0:T(8,128)S(1)}, s32[]{:S(2)}) async-start(f32[256,512]{1,0:T(8,128)} %copy-done.11), calls=%async_computation.2 | async-start | bytes 524288 | tf_op jit(solution)/shard_map/slice | solution.py:383
  298.2 14.7 %copy-start.13 = (f32[256,1024]{1,0:T(8,128)S(1)}, f32[256,1024]{1,0:T(8,128)}, u32[]{:S(2)}) copy-start(f32[256,1024]{1,0:T(8,128)} %get-tuple-element.54) | copy-start | bytes 3145732
  299.1 5.9 %collective-permute-start.14 = (f32[6,2048]{1,0:T(8,128)S(1)}, f32[6,2048]{1,0:T(8,128)S(1)}, u32[]{:S(2)}, u32[]{:S(2)}) collective-permute-start(f32[6,2048]{1,0:T(8,128)S(1)} %add.47), channel_id=1, source_target_pairs={{0,2},{1,3},{2,0},{3,1},{4,6},{5,7},{6,4},{7,5},{8,10},{9,11},{10,... | collective-permute-start | bytes 147464 | tf_op jit(solution)/shard_map/ppermute | solution.py:350
  305.1 4.3 %collective-permute-start.15 = (f32[6,2048]{1,0:T(8,128)S(1)}, f32[6,2048]{1,0:T(8,128)S(1)}, u32[]{:S(2)}, u32[]{:S(2)}) collective-permute-start(f32[6,2048]{1,0:T(8,128)S(1)} %add.48), channel_id=1, source_target_pairs={{0,1},{1,0},{2,3},{3,2},{4,5},{5,4},{6,7},{7,6},{8,9},{9,8},{10,11... | collective-permute-start | bytes 147464 | tf_op jit(solution)/shard_map/ppermute | solution.py:350

commit v2 on v1

--- a/solution.py
+++ b/solution.py
@@ -12,7 +12,6 @@
 ROWS = 40
 GROUP = 4
 HI = lax.Precision.HIGHEST
-MID = lax.Precision.HIGH
 
 
 def split2(x):
@@ -283,12 +282,111 @@
     )(upper, lower)
 
 
-def mm(left, right, precision=MID):
-    return jnp.dot(left, right, precision=precision, preferred_element_type=jnp.float32)
-
-
-def column_sums(left, right):
-    return jnp.sum(left * right, axis=0)
+def mm(left, right):
+    return jnp.dot(left, right, precision=HI, preferred_element_type=jnp.float32)
+
+
+def left3(x):
+    high, low = split2(x)
+    return jnp.concatenate([high, high, low], axis=1)
+
+
+def right3(x):
+    high, low = split2(x)
+    return jnp.concatenate([high, low, high], axis=0)
+
+
+def dot3(left, right):
+    return jnp.dot(left, right, preferred_element_type=jnp.float32)
+
+
+def at_row(k, value):
+    row = lax.broadcasted_iota(jnp.int32, (8, value.shape[1]), 0)
+    return jnp.where(row == k, value, 0.0)
+
+
+def sums_of(left, right):
+    return jnp.sum(left * right, axis=0, keepdims=True)
+
+
+BLOCK = 256
+
+
+def in_blocks(kernel, matrices, wholes, lefts, rights, sums, outs):
+    rows = matrices[0].shape[0]
+    per = (lefts + rights)[0].shape[1] // BLOCK if lefts else wholes[0].shape[1] // BLOCK // 2
+    square = pl.BlockSpec((rows, rows), lambda j: (0, 0))
+    maps = {
+        "whole": lambda j: (0, j),
+        "left": lambda j: (0, jnp.minimum(j, per - 1)),
+        "right": lambda j: (0, jnp.maximum(j - per, 0)),
+        "sums": lambda j: (0, j),
+    }
+
+    def spec(kind):
+        return pl.BlockSpec((8 if kind == "sums" else rows, BLOCK), maps[kind])
+
+    total = 2 * per * BLOCK
+    shapes = {
+        "whole": (rows, total),
+        "left": (rows, total // 2),
+        "right": (rows, total // 2),
+        "sums": (8, total),
+    }
+    return pl.pallas_call(
+        lambda *refs: kernel(pl.program_id(0) < per, *refs),
+        grid=(2 * per,),
+        in_specs=[square] * len(matrices)
+        + [spec("whole")] * len(wholes)
+        + [spec("left")] * len(lefts)
+        + [spec("right")] * len(rights)
+        + [spec("sums")] * len(sums),
+        out_specs=tuple(spec(kind) for kind in outs),
+        out_shape=tuple(jax.ShapeDtypeStruct(shapes[kind], jnp.float32) for kind in outs),
+    )(*matrices, *wholes, *lefts, *rights, *sums)
+
+
+def first_kernel(is_left, low, high, inv, low0, high0, low1, high1, v_ref, w_ref, m_ref):
+    def run(x_low, x_high):
+        v = dot3(left3(low[...]), right3(x_low[...])) + dot3(left3(high[...]), right3(x_high[...]))
+        w = dot3(left3(inv[...]), right3(v))
+        v_ref[...] = v
+        w_ref[...] = w
+        m_ref[...] = at_row(2, sums_of(v, w))
+
+    pl.when(is_left)(lambda: run(low0, high0))
+    pl.when(jnp.logical_not(is_left))(lambda: run(low1, high1))
+
+
+def start_kernel(is_left, inv, v0, v1, m_in, w_ref, m_ref):
+    w = dot3(left3(inv[...]), right3(v0[...]))
+    w_ref[...] = w
+    m_ref[...] = m_in[...] + at_row(0, sums_of(v0[...], w)) + at_row(1, sums_of(v1[...], w))
+
+
+def second_kernel(is_left, low, high, inv, x_low, x_high, w1, m_in, v_ref, left_ref, right_ref, m_ref):
+    v = dot3(left3(low[...]), right3(x_low[...])) + dot3(left3(high[...]), right3(x_high[...]))
+    w = dot3(left3(inv[...]), right3(v))
+    v_ref[...] = v
+    m_ref[...] = m_in[...] + at_row(3, sums_of(v, w1[...])) + at_row(4, sums_of(v, w))
+
+    @pl.when(is_left)
+    def _():
+        left_ref[...] = w
+
+    @pl.when(jnp.logical_not(is_left))
+    def _():
+        right_ref[...] = w
+
+
+def side_kernel(is_left, low, high, w0_half, x_high, w1_half, x_low, m_in, t_ref, m_ref):
+    def run(band, x, w):
+        t = dot3(left3(band[...]), right3(x[...]))
+        t_ref[...] = t
+        m_ref[...] = m_in[...] + at_row(5, 2.0 * sums_of(t, w[...]))
+
+    pl.when(is_left)(lambda: run(high, x_high, w0_half))
+    pl.when(jnp.logical_not(is_left))(lambda: run(low, x_low, w1_half))
 
 
 def safe(num, den):
@@ -313,36 +411,18 @@
     return (1.0 - c0, c3 - c2, -c3), (c0, c1, c2, c3)
 
 
-def finish_kernel(per, sums_ref, v0, w0, v1, w1, *refs):
-    halves, (sol_ref, res_ref) = (refs[:3], refs[3:6]), refs[6:]
-    x, c = coefficients([sums_ref[k : k + 1, :] for k in range(6)])
-
-    def write(v2, v3, w2):
+def finish_kernel(
+    is_left, low, high, v0, w0, v1, w1, v2, t, w2_0, x_low, w2_1, x_high, sums, sol_ref, res_ref
+):
+    x, c = coefficients([sums[k : k + 1, :] for k in range(6)])
+
+    def run(band, far, w2):
+        v3 = t[...] + dot3(left3(band[...]), right3(far[...]))
         sol_ref[...] = x[0] * w0[...] + x[1] * w1[...] + x[2] * w2[...]
-        res_ref[...] = c[0] * v0[...] + c[1] * v1[...] + c[2] * v2[...] + c[3] * v3[...]
-
-    for k in range(2):
-        pl.when(pl.program_id(0) // per == k)(lambda k=k: write(*halves[k]))
-
-
-def finish(sums, wholes, halves):
-    rows, total = wholes[0].shape
-    width = 256
-    per = total // 2 // width
-    whole = pl.BlockSpec((rows, width), lambda j: (0, j))
-    left = pl.BlockSpec((rows, width), lambda j: (0, jnp.minimum(j, per - 1)))
-    right = pl.BlockSpec((rows, width), lambda j: (0, jnp.maximum(j - per, 0)))
-    return pl.pallas_call(
-        lambda *refs: finish_kernel(per, *refs),
-        grid=(2 * per,),
-        in_specs=[pl.BlockSpec((sums.shape[0], width), lambda j: (0, j))]
-        + [whole] * 4
-        + [left] * 3
-        + [right] * 3,
-        out_specs=(whole, whole),
-        out_shape=(jax.ShapeDtypeStruct((rows, total), jnp.float32),) * 2,
-        name="finish",
-    )(sums, *wholes, *halves[0], *halves[1])
+        res_ref[...] = c[0] * v0[...] + c[1] * v1[...] + c[2] * v2[...] + c[3] * v3
+
+    pl.when(is_left)(lambda: run(low, x_low, w2_0))
+    pl.when(jnp.logical_not(is_left))(lambda: run(high, x_high, w2_1))
 
 
 def butterfly(x, devices, bits):
@@ -365,8 +445,11 @@
         return lax.ppermute(x, AXES, down)
 
     base = jnp.stack([lax.axis_index(AXES) * own, own * devices]).astype(jnp.int32)
-    v0_low = from_below(right_side)
-    v0_high = from_above(right_side)
+    width = right_side.shape[1] // 2
+    r_low, r_high = {}, {}
+    start = right_side[:, :width]
+    r_low[0] = from_below(start)
+    r_high[0] = from_above(start)
     send0, send1 = pack(owner_map, connect.T, blocks, devices)
 
     def exchange(send):
@@ -377,48 +460,57 @@
 
     got0 = exchange(send0)
     got1 = exchange(send1)
+    rest, got0 = lax.optimization_barrier((right_side, got0))
+    rest = rest[:, width:]
+    r_low[1], r_high[1] = from_below(rest), from_above(rest)
     part = assemble(base, got0, window)
     center, high_band, lower = assemble(base, got1, window, part)
     lower = from_below(lower)
     low_band = lower[:, :own]
     inv = invert(center, lower)
     inv_low, inv_high = from_below(inv), from_above(inv)
-    near_low, near_high = mm(low_band, inv_low, HI), mm(high_band, inv_high, HI)
-
-    width = right_side.shape[1] // 2
-
-    def part_of(x, h):
-        return lax.slice_in_dim(x, h * width, (h + 1) * width, axis=1)
-
-    v1 = mm(near_low, v0_low) + mm(near_high, v0_high)
-    w1 = mm(inv, v1)
+    near_low, near_high = mm(low_band, inv_low), mm(high_band, inv_high)
+
+    v0 = right_side
+    v1, w1, sums = in_blocks(
+        first_kernel,
+        (near_low, near_high, inv),
+        (),
+        (r_low[0], r_high[0]),
+        (r_low[1], r_high[1]),
+        (),
+        ("whole", "whole", "sums"),
+    )
     w1_low, w1_high = from_below(w1), from_above(w1)
-    w0 = mm(inv, right_side)
-    v2, w2 = {}, {}
-    for h in range(2):
-        v2[h] = mm(low_band, part_of(w1_low, h)) + mm(high_band, part_of(w1_high, h))
-        w2[h] = mm(inv, v2[h])
-    w2_high, w2_low = {}, {}
-    w2_high[0] = from_above(w2[0])
-    w2_low[1] = from_below(w2[1])
-    w2_high[0], w2_low[1], later0, later1 = lax.optimization_barrier(
-        (w2_high[0], w2_low[1], w2[0], w2[1])
-    )
-    w2_low[0] = from_below(later0)
-    w2_high[1] = from_above(later1)
-    side = {0: mm(high_band, w2_high[0]), 1: mm(low_band, w2_low[1])}
-    sums = []
-    for h in range(2):
-        v0h, w0h, v1h, w1h = (part_of(x, h) for x in (right_side, w0, v1, w1))
-        pairs = [(v0h, w0h), (v1h, w0h), (v1h, w1h), (v2[h], w1h), (v2[h], w2[h])]
-        rows = [column_sums(*pair) for pair in pairs] + [2.0 * column_sums(side[h], w2[h])]
-        sums.append(jnp.stack(rows))
-    sums = jnp.concatenate(sums, axis=1)
-    sums = butterfly(sums, devices, (64, 32, 8, 4, 16))
-    sums, low_late, high_late = lax.optimization_barrier((sums, low_band, high_band))
-    v3 = {0: side[0] + mm(low_late, w2_low[0]), 1: side[1] + mm(high_late, w2_high[1])}
-    sums = butterfly(sums, devices, (2, 1))
-    return finish(sums, (right_side, w0, v1, w1), [(v2[h], v3[h], w2[h]) for h in range(2)])
+    w0, sums = in_blocks(start_kernel, (inv,), (v0, v1), (), (), (sums,), ("whole", "sums"))
+    v2, w2_0, w2_1, sums = in_blocks(
+        second_kernel,
+        (low_band, high_band, inv),
+        (w1_low, w1_high, w1),
+        (),
+        (),
+        (sums,),
+        ("whole", "left", "right", "sums"),
+    )
+    near_0 = from_above(w2_0)
+    near_1 = from_below(w2_1)
+    near_0, near_1, later_0, later_1 = lax.optimization_barrier((near_0, near_1, w2_0, w2_1))
+    far_0 = from_below(later_0)
+    far_1 = from_above(later_1)
+    bands = (low_band, high_band)
+    t, sums = in_blocks(
+        side_kernel, bands, (), (w2_0, near_0), (w2_1, near_1), (sums,), ("whole", "sums")
+    )
+    sums = butterfly(sums, devices, (64, 32, 8, 4, 16, 2, 1))
+    return in_blocks(
+        finish_kernel,
+        bands,
+        (v0, w0, v1, w1, v2, t),
+        (w2_0, far_0),
+        (w2_1, far_1),
+        (sums,),
+        ("whole", "whole"),
+    )
 
 
 def solution(mesh):

time: 329 us -> 352 us (1.070); the launches traced: 324 us -> 351 us
  Pallas kernels: 59.5 us -> 97.2 us
  matrix products: 22 us -> 3.12 us
  waiting for transfers between devices: 145 us -> 134 us
  starting transfers between devices: 47.8 us -> 58.7 us
  local copies, waits for them, and re-layouts: 0.96 us -> 8.29 us
    pallas_call x1 -> x5, Pallas kernels: 9.15 us -> 46.8 us  [in_blocks(): pl.pallas_call(lambda *refs: kernel(pl.program_id(0) < per, *refs), grid=...]
    dot_general x16 -> x2, matrix products: 22 us -> 3.12 us  [mm(): jnp.dot(left, right, precision=HI, preferred_element_type=jnp.float32)]
    ppermute x6 -> x7, waiting for transfers between devices: 58 us -> 39.4 us  [from_below(): return lax.ppermute(x, AXES, up)]
    ppermute x7, starting transfers between devices: 5.76 us -> 22.4 us  [butterfly(): x = x + lax.ppermute(x, AXES, [(i, i ^ bit) for i in range(devices)])]
    ppermute x5 -> x6, waiting for transfers between devices: 43.6 us -> 60.1 us  [from_above(): return lax.ppermute(x, AXES, down)]
    ppermute x7, waiting for transfers between devices: 40.5 us -> 24.8 us  [butterfly(): x = x + lax.ppermute(x, AXES, [(i, i ^ bit) for i in range(devices)])]
    ppermute x5 -> x6, starting transfers between devices: 25 us -> 16.2 us  [from_above(): return lax.ppermute(x, AXES, down)]
    all_to_all x1, waiting for transfers between devices: 2.69 us -> 9.65 us  [exchange(): lax.all_to_all(send.reshape(devices, ROWS, 128), AXES, split_axis=0, conc...]
  transfers between devices with their start and end apart: 19 -> 21, of which waited for: 14 -> 14; matrix products, arithmetic and copies ran while one was open for 5% -> 2% of each run, Pallas kernels for 13% -> 13%
where the time goes in v2:
time: 352 us; the launch traced here: 351 us
  waiting for transfers between devices  134 us (38%)
  Pallas kernels  97.2 us (28%)
  starting transfers between devices  58.7 us (17%)
  blocking collectives  46.3 us (13%)
  local copies, waits for them, and re-layouts  8.29 us (2%)
    ppermute x6, waiting for transfers between devices, from_above(): return lax.ppermute(x, AXES, down)  60.1 us
    pallas_call x5, Pallas kernels, in_blocks(): pl.pallas_call(lambda *refs: kernel(pl.program_id(0) < per, *refs), grid=...  46.8 us
    all_to_all x1, blocking collectives, exchange(): lax.all_to_all(send.reshape(devices, ROWS, 128), AXES, split_axis=0, conc...  46.3 us
    ppermute x7, waiting for transfers between devices, from_below(): return lax.ppermute(x, AXES, up)  39.4 us
    pallas_call x2, Pallas kernels, assemble(): pl.pallas_call(lambda *refs: assemble_kernel(last, *refs), out_shape=out,...  34 us
    ppermute x7, waiting for transfers between devices, butterfly(): x = x + lax.ppermute(x, AXES, [(i, i ^ bit) for i in range(devices)])  24.8 us
    ppermute x7, starting transfers between devices, butterfly(): x = x + lax.ppermute(x, AXES, [(i, i ^ bit) for i in range(devices)])  22.4 us
    ppermute x6, starting transfers between devices, from_above(): return lax.ppermute(x, AXES, down)  16.2 us
  transfers between devices with their start and end apart: 21, of which 14 were waited for; matrix products, arithmetic and copies ran while one was open for 2% of the time, Pallas kernels for 13%

profile of v2, /device:TPU:0, one launch (start us, length us, event | category | flops | bytes accessed | tf_op | source)
XLA Modules:
  0.0 350.5 jit_solution(15961911979883689135)
XLA Ops:
  0.6 8.7 %pack.1 = (f32[5120,128]{1,0:T(8,128)}, f32[5120,128]{1,0:T(8,128)}) custom-call(s32[1,128]{1,0:T(1,128)} %bitcast.13, s32[96,128]{1,0:T(8,128)} %bitcast.12, f32[128,9216]{1,0:T(8,128)} %x_ref.1), custom_call_target="tpu_custom_call" | custom-call | tf_op jit(solution)/shard_map/pack/pallas_call | solution.py:95
  9.3 46.3 %all_to_all.10 = f32[128,40,128]{2,1,0:T(8,128)} all-to-all(f32[128,40,128]{2,1,0:T(8,128)} %bitcast.11), channel_id=1, replica_groups=mesh['row'=8,'col'=16] {'row','col'}, dimensions={0} | all-to-all | bytes 5242880 | tf_op jit(solution)/shard_map/all_to_all | solution.py:456
  55.7 5.7 %all-to-all-start = ((f32[128,40,128]{2,1,0:T(8,128)}), f32[128,40,128]{2,1,0:T(8,128)}, u32[]{:S(2)}, u32[]{:S(2)}) async-start(f32[128,40,128]{2,1,0:T(8,128)} %bitcast.3), calls=%async_computation | async-start | bytes 5242880 | tf_op jit(solution)/shard_map/all_to_all | solution.py:456
  61.4 0.6 pad_add_fusion.refs_0_
  62.0 24.4 %assemble_first.1.refs_2_ = f32[512,512]{1,0:T(8,128)} custom-call(s32[2]{0:T(128)} %pad_add_fusion.refs_0_, f32[5120,128]{1,0:T(8,128)} %bitcast.10), custom_call_target="tpu_custom_call" | custom-call | tf_op jit(solution)/shard_map/assemble_first/pallas_call | solution.py:240
  86.4 0.0 copy-start
  86.4 9.7 %all-to-all-done = f32[128,40,128]{2,1,0:T(8,128)} async-done(((f32[128,40,128]{2,1,0:T(8,128)}), f32[128,40,128]{2,1,0:T(8,128)}, u32[]{:S(2)}, u32[]{:S(2)}) %all-to-all-start) | async-done | bytes 2621472 | tf_op jit(solution)/shard_map/all_to_all | solution.py:456
  96.1 9.6 %assemble_last.1 = (f32[256,256]{1,0:T(8,128)}, f32[256,256]{1,0:T(8,128)}, f32[256,512]{1,0:T(8,128)}) custom-call(s32[2]{0:T(128)} %pad_add_fusion.refs_0_, f32[5120,128]{1,0:T(8,128)} %bitcast.4.refs_1_, f32[512,512]{1,0:T(8,128)} %assemble_first.1.refs_2_), custom_call_target="tpu_custom_call" | custom-call | tf_op jit(solution)/shard_map/assemble_last/pallas_call | solution.py:240
  105.7 4.1 %collective-permute-start = (f32[256,512]{1,0:T(8,128)}, f32[256,512]{1,0:T(8,128)S(1)}, u32[]{:S(2)}, u32[]{:S(2)}) collective-permute-start(f32[256,512]{1,0:T(8,128)} %get-tuple-element.27), channel_id=1, source_target_pairs={{0,1},{1,2},{2,3},{3,4},{4,5},{5,6},{6,7},{7,8},{8,9},{9,10},{10,1... | collective-permute-start | bytes 1572872 | tf_op jit(solution)/shard_map/ppermute | solution.py:442
  109.8 1.0 slice.10
  110.8 3.2 collective-permute-start.4
  114.0 0.0 collective-permute-start.3
  114.0 1.0 slice.11
  115.0 7.2 %collective-permute-start.6 = (f32[256,1024]{1,0:T(8,128)}, f32[256,1024]{1,0:T(8,128)S(1)}, u32[]{:S(2)}, u32[]{:S(2)}) collective-permute-start(f32[256,1024]{1,0:T(8,128)} %slice.11), channel_id=1, source_target_pairs={{1,0},{2,1},{3,2},{4,3},{5,4},{6,5},{7,6},{8,7},{9,8},{10,9},{11,1... | collective-permute-start | bytes 3145736 | tf_op jit(solution)/shard_map/ppermute | solution.py:445
  122.2 0.0 collective-permute-start.5
  122.2 0.2 collective-permute-done.lower_ref
  122.4 0.8 copy-done.3
  123.3 7.6 %invert.1.refs_2_.refs_0_ = f32[256,256]{1,0:T(8,128)} custom-call(f32[256,256]{1,0:T(8,128)} %get-tuple-element.29.upper_ref, f32[256,512]{1,0:T(8,128)} %copy-done.3), custom_call_target="tpu_custom_call" | custom-call | tf_op jit(solution)/shard_map/invert/pallas_call | solution.py:277
  130.9 2.4 collective-permute-start.1
  133.3 39.1 %collective-permute-done.1 = f32[256,256]{1,0:T(8,128)S(1)} collective-permute-done((f32[256,256]{1,0:T(8,128)}, f32[256,256]{1,0:T(8,128)S(1)}, u32[]{:S(2)}, u32[]{:S(2)}) %collective-permute-start.1) | collective-permute-done | bytes 262176 | tf_op jit(solution)/shard_map/ppermute | solution.py:442
  172.4 0.2 collective-permute-start.2
  172.5 2.0 fusion.refs_0_
  174.6 5.2 %collective-permute-done.2 = f32[256,256]{1,0:T(8,128)S(1)} collective-permute-done((f32[256,256]{1,0:T(8,128)}, f32[256,256]{1,0:T(8,128)S(1)}, u32[]{:S(2)}, u32[]{:S(2)}) %collective-permute-start.2) | collective-permute-done | bytes 262176 | tf_op jit(solution)/shard_map/ppermute | solution.py:445
  179.8 1.1 fusion.2.refs_1_
  180.9 0.0 collective-permute-done.6.refs_6_
  180.9 0.0 copy-start.7
  180.9 0.9 copy-done.7
  181.9 10.3 %shard_map.59 = (f32[256,2048]{1,0:T(8,128)}, f32[256,2048]{1,0:T(8,128)}, f32[8,2048]{1,0:T(8,128)}) custom-call(f32[256,256]{1,0:T(8,128)} %fusion.refs_0_, f32[256,256]{1,0:T(8,128)} %fusion.2.refs_1_, f32[256,256]{1,0:T(8,128)} %invert.1.refs_2_.refs_0_, f32[256,1024]{1,0:T(8,128)} %collective-permute-done.3.refs_3_, ...), custom_call_target="tpu_custom_call" | custom-call | tf_op jit(solution)/shard_map/pallas_call | solution.py:336
  192.2 4.3 %collective-permute-start.8 = (f32[256,2048]{1,0:T(8,128)}, f32[256,2048]{1,0:T(8,128)S(1)}, u32[]{:S(2)}, u32[]{:S(2)}) collective-permute-start(f32[256,2048]{1,0:T(8,128)} %get-tuple-element.34.refs_5_), channel_id=1, source_target_pairs={{1,0},{2,1},{3,2},{4,3},{5,4},{6,5},{7,6},{8,7},{9,8},{10,9},{11,1... | collective-permute-start | bytes 6291464 | tf_op jit(solution)/shard_map/ppermute | solution.py:445
  196.5 0.0 collective-permute-start.7
  196.5 0.7 slice.12.refs_0_
  197.3 7.3 %shard_map.60 = (f32[256,2048]{1,0:T(8,128)}, f32[8,2048]{1,0:T(8,128)}) custom-call(f32[256,256]{1,0:T(8,128)} %invert.1.refs_2_.refs_0_, f32[256,2048]{1,0:T(8,128)} %refs_2_.1, f32[256,2048]{1,0:T(8,128)} %get-tuple-element.31.refs_2_.refs_4_, f32[8,2048]{1,0:T(8,128)} %get-tuple-element.32.refs_3_), custom_call_target="tpu_custom_call" | custom-call | tf_op jit(solution)/shard_map/pallas_call | solution.py:336
  204.6 36.9 %collective-permute-done.8.refs_4_ = f32[256,2048]{1,0:T(8,128)S(1)} collective-permute-done((f32[256,2048]{1,0:T(8,128)}, f32[256,2048]{1,0:T(8,128)S(1)}, u32[]{:S(2)}, u32[]{:S(2)}) %collective-permute-start.8) | collective-permute-done | bytes 2097184 | tf_op jit(solution)/shard_map/ppermute | solution.py:445
  241.5 1.3 copy-done.2
  242.8 10.6 %shard_map.61 = (f32[256,2048]{1,0:T(8,128)}, f32[256,1024]{1,0:T(8,128)}, f32[256,1024]{1,0:T(8,128)}, f32[8,2048]{1,0:T(8,128)}) custom-call(f32[256,256]{1,0:T(8,128)} %slice.12.refs_0_, f32[256,256]{1,0:T(8,128)} %get-tuple-element.28.refs_1_, f32[256,256]{1,0:T(8,128)} %invert.1.refs_2_.refs_0_, f32[256,2048]{1,0:T(8,128)} %collective-permute-done.7.refs_3_, ...), custom_call_target="tpu_custom_call" | custom-call | tf_op jit(solution)/shard_map/pallas_call | solution.py:336
  253.5 0.1 collective-permute-start.9
  253.6 2.0 collective-permute-start.10
  255.6 18.0 %collective-permute-done.9.refs_3_ = f32[256,1024]{1,0:T(8,128)S(1)} collective-permute-done((f32[256,1024]{1,0:T(8,128)}, f32[256,1024]{1,0:T(8,128)S(1)}, u32[]{:S(2)}, u32[]{:S(2)}) %collective-permute-start.9) | collective-permute-done | bytes 1048608 | tf_op jit(solution)/shard_map/ppermute | solution.py:445
  273.5 0.1 collective-permute-done.10.refs_5_
  273.6 1.0 copy-done.9
  274.6 5.9 %collective-permute-start.11 = (f32[256,1024]{1,0:T(8,128)}, f32[256,1024]{1,0:T(8,128)S(1)}, u32[]{:S(2)}, u32[]{:S(2)}) collective-permute-start(f32[256,1024]{1,0:T(8,128)} %get-tuple-element.43.refs_2_.refs_8_), channel_id=1, source_target_pairs={{0,1},{1,2},{2,3},{3,4},{4,5},{5,6},{6,7},{7,8},{8,9},{9,10},{10,1... | collective-permute-start | bytes 3145736 | tf_op jit(solution)/shard_map/ppermute | solution.py:442
  280.5 1.3 collective-permute-start.12
  281.8 7.6 %shard_map.62 = (f32[256,2048]{1,0:T(8,128)}, f32[8,2048]{1,0:T(8,128)}) custom-call(f32[256,256]{1,0:T(8,128)} %slice.12.refs_0_, f32[256,256]{1,0:T(8,128)} %get-tuple-element.28.refs_1_, f32[256,1024]{1,0:T(8,128)} %get-tuple-element.43.refs_2_.refs_8_, f32[256,1024]{1,0:T(8,128)} %copy-done.8, f32[256,1024]{1,0:T(8,128)} %get-tuple-element.44.refs_4_.refs_10_, ...), custom_call_target="tpu_custom_call" | custom-call | tf_op jit(solution)/shard_map/pallas_call | solution.py:336
  289.4 0.8 collective-permute-start.13
  290.3 5.1 %collective-permute-done.13 = f32[8,2048]{1,0:T(8,128)S(1)} collective-permute-done((f32[8,2048]{1,0:T(8,128)}, f32[8,2048]{1,0:T(8,128)S(1)}, u32[]{:S(2)}, u32[]{:S(2)}) %collective-permute-start.13) | collective-permute-done | bytes 65568 | tf_op jit(solution)/shard_map/ppermute | solution.py:430
  295.4 0.9 add.25
  296.3 3.9 %collective-permute-start.14 = (f32[8,2048]{1,0:T(8,128)S(1)}, f32[8,2048]{1,0:T(8,128)S(1)}, u32[]{:S(2)}, u32[]{:S(2)}) collective-permute-start(f32[8,2048]{1,0:T(8,128)S(1)} %add.25), channel_id=1, source_target_pairs={{0,32},{1,33},{2,34},{3,35},{4,36},{5,37},{6,38},{7,39},{8,40},{9,... | collective-permute-start | bytes 196616 | tf_op jit(solution)/shard_map/ppermute | solution.py:430
  300.2 2.2 collective-permute-done.14
  302.5 8.1 %collective-permute-start.15 = (f32[8,2048]{1,0:T(8,128)S(1)}, f32[8,2048]{1,0:T(8,128)S(1)}, u32[]{:S(2)}, u32[]{:S(2)}) collective-permute-start(f32[8,2048]{1,0:T(8,128)S(1)} %add.26), channel_id=1, source_target_pairs={{0,8},{1,9},{2,10},{3,11},{4,12},{5,13},{6,14},{7,15},{8,0},{9,1},... | collective-permute-start | bytes 196616 | tf_op jit(solution)/shard_map/ppermute | solution.py:430
  310.6 2.9 collective-permute-done.15
  313.5 0.9 collective-permute-start.16
  314.4 3.4 collective-permute-done.16
  317.9 8.4 %collective-permute-start.17 = (f32[8,2048]{1,0:T(8,128)S(1)}, f32[8,2048]{1,0:T(8,128)S(1)}, u32[]{:S(2)}, u32[]{:S(2)}) collective-permute-start(f32[8,2048]{1,0:T(8,128)S(1)} %add.28), channel_id=1, source_target_pairs={{0,16},{1,17},{2,18},{3,19},{4,20},{5,21},{6,22},{7,23},{8,24},{9,... | collective-permute-start | bytes 196616 | tf_op jit(solution)/shard_map/ppermute | solution.py:430
  326.3 0.9 collective-permute-done.17
  327.2 0.1 collective-permute-start.18
  327.3 5.8 %collective-permute-done.18 = f32[8,2048]{1,0:T(8,128)S(1)} collective-permute-done((f32[8,2048]{1,0:T(8,128)S(1)}, f32[8,2048]{1,0:T(8,128)S(1)}, u32[]{:S(2)}, u32[]{:S(2)}) %collective-permute-start.18) | collective-permute-done | bytes 65568 | tf_op jit(solution)/shard_map/ppermute | solution.py:430
  333.2 0.1 collective-permute-start.19
  333.3 4.3 %collective-permute-done.19 = f32[8,2048]{1,0:T(8,128)S(1)} collective-permute-done((f32[8,2048]{1,0:T(8,128)S(1)}, f32[8,2048]{1,0:T(8,128)S(1)}, u32[]{:S(2)}, u32[]{:S(2)}) %collective-permute-start.19) | collective-permute-done | bytes 65568 | tf_op jit(solution)/shard_map/ppermute | solution.py:430
  337.5 0.6 add.31.refs_12_
  338.2 0.0 collective-permute-done.11.refs_9_
  338.2 0.0 collective-permute-done.12.refs_11_
  338.2 1.0 copy-done.5
  339.1 0.3 copy-done.6
  339.5 10.9 %shard_map.63 = (f32[256,2048]{1,0:T(8,128)}, f32[256,2048]{1,0:T(8,128)}) custom-call(f32[256,256]{1,0:T(8,128)} %slice.12.refs_0_, f32[256,256]{1,0:T(8,128)} %get-tuple-element.28.refs_1_, f32[256,2048]{1,0:T(8,128)} %refs_2_.1, f32[256,2048]{1,0:T(8,128)} %get-tuple-element.33.refs_3_, f32[256,2048]{1,0:T(8,128)} %get-tuple-element.31.refs_2_.refs_4_, ...), custom_call_target="tpu_custom_call" | custom-call | tf_op jit(solution)/shard_map/pallas_call | solution.py:336
  (21 shorter events, 0.1 us)
Async XLA Ops:
  55.7 40.4 %all-to-all-start = ((f32[128,40,128]{2,1,0:T(8,128)}), f32[128,40,128]{2,1,0:T(8,128)}, u32[]{:S(2)}, u32[]{:S(2)}) async-start(f32[128,40,128]{2,1,0:T(8,128)} %bitcast.3), calls=%async_computation | async-start | bytes 5242880 | tf_op jit(solution)/shard_map/all_to_all | solution.py:456
  86.4 23.4 %copy-start = (f32[256,2048]{1,0:T(8,128)S(1)}, f32[256,2048]{1,0:T(8,128)}, u32[]{:S(2)}) copy-start(f32[256,2048]{1,0:T(8,128)} %refs_2_.1) | copy-start | bytes 6291460
  105.7 16.7 %collective-permute-start = (f32[256,512]{1,0:T(8,128)}, f32[256,512]{1,0:T(8,128)S(1)}, u32[]{:S(2)}, u32[]{:S(2)}) collective-permute-start(f32[256,512]{1,0:T(8,128)} %get-tuple-element.27), channel_id=1, source_target_pairs={{0,1},{1,2},{2,3},{3,4},{4,5},{5,6},{6,7},{7,8},{8,9},{9,10},{10,1... | collective-permute-start | bytes 1572872 | tf_op jit(solution)/shard_map/ppermute | solution.py:442
  110.8 69.0 %copy-start.1 = (f32[256,256]{1,0:T(8,128)S(1)}, f32[256,256]{1,0:T(8,128)}, u32[]{:S(2)}) copy-start(f32[256,256]{1,0:T(8,128)} %get-tuple-element.28.refs_1_) | copy-start | bytes 786436
  110.8 70.0 %collective-permute-start.4 = (f32[256,1024]{1,0:T(8,128)}, f32[256,1024]{1,0:T(8,128)}, u32[]{:S(2)}, u32[]{:S(2)}) collective-permute-start(f32[256,1024]{1,0:T(8,128)} %slice.10), channel_id=1, source_target_pairs={{1,0},{2,1},{3,2},{4,3},{5,4},{6,5},{7,6},{8,7},{9,8},{10,9},{11,1... | collective-permute-start | bytes 3145736 | tf_op jit(solution)/shard_map/ppermute | solution.py:445
  114.0 66.9 %collective-permute-start.3 = (f32[256,1024]{1,0:T(8,128)}, f32[256,1024]{1,0:T(8,128)}, u32[]{:S(2)}, u32[]{:S(2)}) collective-permute-start(f32[256,1024]{1,0:T(8,128)} %slice.10), channel_id=1, source_target_pairs={{0,1},{1,2},{2,3},{3,4},{4,5},{5,6},{6,7},{7,8},{8,9},{9,10},{10,1... | collective-permute-start | bytes 3145736 | tf_op jit(solution)/shard_map/ppermute | solution.py:442
  115.0 65.8 %collective-permute-start.6 = (f32[256,1024]{1,0:T(8,128)}, f32[256,1024]{1,0:T(8,128)S(1)}, u32[]{:S(2)}, u32[]{:S(2)}) collective-permute-start(f32[256,1024]{1,0:T(8,128)} %slice.11), channel_id=1, source_target_pairs={{1,0},{2,1},{3,2},{4,3},{5,4},{6,5},{7,6},{8,7},{9,8},{10,9},{11,1... | collective-permute-start | bytes 3145736 | tf_op jit(solution)/shard_map/ppermute | solution.py:445
  122.2 58.7 %collective-permute-start.5 = (f32[256,1024]{1,0:T(8,128)}, f32[256,1024]{1,0:T(8,128)}, u32[]{:S(2)}, u32[]{:S(2)}) collective-permute-start(f32[256,1024]{1,0:T(8,128)} %slice.11), channel_id=1, source_target_pairs={{0,1},{1,2},{2,3},{3,4},{4,5},{5,6},{6,7},{7,8},{8,9},{9,10},{10,1... | collective-permute-start | bytes 3145736 | tf_op jit(solution)/shard_map/ppermute | solution.py:442
  122.4 0.8 copy-start.3
  130.9 41.5 %collective-permute-start.1 = (f32[256,256]{1,0:T(8,128)}, f32[256,256]{1,0:T(8,128)S(1)}, u32[]{:S(2)}, u32[]{:S(2)}) collective-permute-start(f32[256,256]{1,0:T(8,128)} %invert.1.refs_2_.refs_0_), channel_id=1, source_target_pairs={{0,1},{1,2},{2,3},{3,4},{4,5},{5,6},{6,7},{7,8},{8,9},{9,10},{10,1... | collective-permute-start | bytes 786440 | tf_op jit(solution)/shard_map/ppermute | solution.py:442
  172.4 7.4 %collective-permute-start.2 = (f32[256,256]{1,0:T(8,128)}, f32[256,256]{1,0:T(8,128)S(1)}, u32[]{:S(2)}, u32[]{:S(2)}) collective-permute-start(f32[256,256]{1,0:T(8,128)} %invert.1.refs_2_.refs_0_), channel_id=1, source_target_pairs={{1,0},{2,1},{3,2},{4,3},{5,4},{6,5},{7,6},{8,7},{9,8},{10,9},{11,1... | collective-permute-start | bytes 786440 | tf_op jit(solution)/shard_map/ppermute | solution.py:445
  180.9 15.7 %copy-start.4 = (f32[256,512]{1,0:T(8,128)S(1)}, f32[256,512]{1,0:T(8,128)}, u32[]{:S(2)}) copy-start(f32[256,512]{1,0:T(8,128)} %copy-done.3) | copy-start | bytes 1572868
  180.9 1.0 copy-start.7
  192.2 49.3 %collective-permute-start.8 = (f32[256,2048]{1,0:T(8,128)}, f32[256,2048]{1,0:T(8,128)S(1)}, u32[]{:S(2)}, u32[]{:S(2)}) collective-permute-start(f32[256,2048]{1,0:T(8,128)} %get-tuple-element.34.refs_5_), channel_id=1, source_target_pairs={{1,0},{2,1},{3,2},{4,3},{5,4},{6,5},{7,6},{8,7},{9,8},{10,9},{11,1... | collective-permute-start | bytes 6291464 | tf_op jit(solution)/shard_map/ppermute | solution.py:445
  196.5 45.0 %collective-permute-start.7 = (f32[256,2048]{1,0:T(8,128)}, f32[256,2048]{1,0:T(8,128)}, u32[]{:S(2)}, u32[]{:S(2)}) collective-permute-start(f32[256,2048]{1,0:T(8,128)} %get-tuple-element.34.refs_5_), channel_id=1, source_target_pairs={{0,1},{1,2},{2,3},{3,4},{4,5},{5,6},{6,7},{7,8},{8,9},{9,10},{10,1... | collective-permute-start | bytes 6291464 | tf_op jit(solution)/shard_map/ppermute | solution.py:442
  241.5 1.3 copy-start.2
  253.5 20.1 %collective-permute-start.9 = (f32[256,1024]{1,0:T(8,128)}, f32[256,1024]{1,0:T(8,128)S(1)}, u32[]{:S(2)}, u32[]{:S(2)}) collective-permute-start(f32[256,1024]{1,0:T(8,128)} %get-tuple-element.43.refs_2_.refs_8_), channel_id=1, source_target_pairs={{1,0},{2,1},{3,2},{4,3},{5,4},{6,5},{7,6},{8,7},{9,8},{10,9},{11,1... | collective-permute-start | bytes 3145736 | tf_op jit(solution)/shard_map/ppermute | solution.py:445
  253.6 20.0 %collective-permute-start.10 = (f32[256,1024]{1,0:T(8,128)}, f32[256,1024]{1,0:T(8,128)S(1)}, u32[]{:S(2)}, u32[]{:S(2)}) collective-permute-start(f32[256,1024]{1,0:T(8,128)} %get-tuple-element.44.refs_4_.refs_10_), channel_id=1, source_target_pairs={{0,1},{1,2},{2,3},{3,4},{4,5},{5,6},{6,7},{7,8},{8,9},{9,10},{10,1... | collective-permute-start | bytes 3145736 | tf_op jit(solution)/shard_map/ppermute | solution.py:442
  273.5 8.3 %copy-start.8 = (f32[256,1024]{1,0:T(8,128)}, f32[256,1024]{1,0:T(8,128)S(1)}, u32[]{:S(2)}) copy-start(f32[256,1024]{1,0:T(8,128)S(1)} %collective-permute-done.9.refs_3_) | copy-start | bytes 3145732
  273.6 1.0 copy-start.9
  274.6 63.5 %collective-permute-start.11 = (f32[256,1024]{1,0:T(8,128)}, f32[256,1024]{1,0:T(8,128)S(1)}, u32[]{:S(2)}, u32[]{:S(2)}) collective-permute-start(f32[256,1024]{1,0:T(8,128)} %get-tuple-element.43.refs_2_.refs_8_), channel_id=1, source_target_pairs={{0,1},{1,2},{2,3},{3,4},{4,5},{5,6},{6,7},{7,8},{8,9},{9,10},{10,1... | collective-permute-start | bytes 3145736 | tf_op jit(solution)/shard_map/ppermute | solution.py:442
  280.5 57.6 %collective-permute-start.12 = (f32[256,1024]{1,0:T(8,128)}, f32[256,1024]{1,0:T(8,128)S(1)}, u32[]{:S(2)}, u32[]{:S(2)}) collective-permute-start(f32[256,1024]{1,0:T(8,128)} %get-tuple-element.44.refs_4_.refs_10_), channel_id=1, source_target_pairs={{1,0},{2,1},{3,2},{4,3},{5,4},{6,5},{7,6},{8,7},{9,8},{10,9},{11,1... | collective-permute-start | bytes 3145736 | tf_op jit(solution)/shard_map/ppermute | solution.py:445
  289.4 6.0 %collective-permute-start.13 = (f32[8,2048]{1,0:T(8,128)}, f32[8,2048]{1,0:T(8,128)S(1)}, u32[]{:S(2)}, u32[]{:S(2)}) collective-permute-start(f32[8,2048]{1,0:T(8,128)} %get-tuple-element.45), channel_id=1, source_target_pairs={{0,64},{1,65},{2,66},{3,67},{4,68},{5,69},{6,70},{7,71},{8,72},{9,... | collective-permute-start | bytes 196616 | tf_op jit(solution)/shard_map/ppermute | solution.py:430
  296.3 6.2 %collective-permute-start.14 = (f32[8,2048]{1,0:T(8,128)S(1)}, f32[8,2048]{1,0:T(8,128)S(1)}, u32[]{:S(2)}, u32[]{:S(2)}) collective-permute-start(f32[8,2048]{1,0:T(8,128)S(1)} %add.25), channel_id=1, source_target_pairs={{0,32},{1,33},{2,34},{3,35},{4,36},{5,37},{6,38},{7,39},{8,40},{9,... | collective-permute-start | bytes 196616 | tf_op jit(solution)/shard_map/ppermute | solution.py:430
  302.5 11.1 %collective-permute-start.15 = (f32[8,2048]{1,0:T(8,128)S(1)}, f32[8,2048]{1,0:T(8,128)S(1)}, u32[]{:S(2)}, u32[]{:S(2)}) collective-permute-start(f32[8,2048]{1,0:T(8,128)S(1)} %add.26), channel_id=1, source_target_pairs={{0,8},{1,9},{2,10},{3,11},{4,12},{5,13},{6,14},{7,15},{8,0},{9,1},... | collective-permute-start | bytes 196616 | tf_op jit(solution)/shard_map/ppermute | solution.py:430
  313.5 4.3 %collective-permute-start.16 = (f32[8,2048]{1,0:T(8,128)S(1)}, f32[8,2048]{1,0:T(8,128)S(1)}, u32[]{:S(2)}, u32[]{:S(2)}) collective-permute-start(f32[8,2048]{1,0:T(8,128)S(1)} %add.27), channel_id=1, source_target_pairs={{0,4},{1,5},{2,6},{3,7},{4,0},{5,1},{6,2},{7,3},{8,12},{9,13},{10,... | collective-permute-start | bytes 196616 | tf_op jit(solution)/shard_map/ppermute | solution.py:430
  317.9 9.3 %collective-permute-start.17 = (f32[8,2048]{1,0:T(8,128)S(1)}, f32[8,2048]{1,0:T(8,128)S(1)}, u32[]{:S(2)}, u32[]{:S(2)}) collective-permute-start(f32[8,2048]{1,0:T(8,128)S(1)} %add.28), channel_id=1, source_target_pairs={{0,16},{1,17},{2,18},{3,19},{4,20},{5,21},{6,22},{7,23},{8,24},{9,... | collective-permute-start | bytes 196616 | tf_op jit(solution)/shard_map/ppermute | solution.py:430
  327.2 5.9 %collective-permute-start.18 = (f32[8,2048]{1,0:T(8,128)S(1)}, f32[8,2048]{1,0:T(8,128)S(1)}, u32[]{:S(2)}, u32[]{:S(2)}) collective-permute-start(f32[8,2048]{1,0:T(8,128)S(1)} %add.29), channel_id=1, source_target_pairs={{0,2},{1,3},{2,0},{3,1},{4,6},{5,7},{6,4},{7,5},{8,10},{9,11},{10,... | collective-permute-start | bytes 196616 | tf_op jit(solution)/shard_map/ppermute | solution.py:430
  333.2 4.3 %collective-permute-start.19 = (f32[8,2048]{1,0:T(8,128)S(1)}, f32[8,2048]{1,0:T(8,128)S(1)}, u32[]{:S(2)}, u32[]{:S(2)}) collective-permute-start(f32[8,2048]{1,0:T(8,128)S(1)} %add.30), channel_id=1, source_target_pairs={{0,1},{1,0},{2,3},{3,2},{4,5},{5,4},{6,7},{7,6},{8,9},{9,8},{10,11... | collective-permute-start | bytes 196616 | tf_op jit(solution)/shard_map/ppermute | solution.py:430
  338.2 1.0 copy-start.5
  338.2 1.3 copy-start.6

commit v3 on v2

--- a/solution.py
+++ b/solution.py
@@ -309,84 +309,103 @@
     return jnp.sum(left * right, axis=0, keepdims=True)
 
 
-BLOCK = 256
-
-
-def in_blocks(kernel, matrices, wholes, lefts, rights, sums, outs):
+BLOCK = 512
+
+
+def in_blocks(kernel, matrices, wholes, lefts, rights, sums, outs, kept):
     rows = matrices[0].shape[0]
-    per = (lefts + rights)[0].shape[1] // BLOCK if lefts else wholes[0].shape[1] // BLOCK // 2
-    square = pl.BlockSpec((rows, rows), lambda j: (0, 0))
+    total = wholes[0].shape[1] if wholes else 2 * lefts[0].shape[1]
+    per = total // 2 // BLOCK
     maps = {
         "whole": lambda j: (0, j),
         "left": lambda j: (0, jnp.minimum(j, per - 1)),
         "right": lambda j: (0, jnp.maximum(j - per, 0)),
         "sums": lambda j: (0, j),
     }
-
-    def spec(kind):
-        return pl.BlockSpec((8 if kind == "sums" else rows, BLOCK), maps[kind])
-
-    total = 2 * per * BLOCK
     shapes = {
         "whole": (rows, total),
         "left": (rows, total // 2),
         "right": (rows, total // 2),
         "sums": (8, total),
     }
+
+    def spec(kind, height):
+        return pl.BlockSpec((height, BLOCK), maps[kind])
+
+    ins = [("whole", x) for x in wholes] + [("left", x) for x in lefts]
+    ins += [("right", x) for x in rights] + [("sums", x) for x in sums]
+
+    def run(*refs):
+        mats, mid, three = refs[: len(matrices)], refs[len(matrices) : -1], refs[-1]
+        kernel(pl.program_id(0), per, mats, three, *mid)
+
     return pl.pallas_call(
-        lambda *refs: kernel(pl.program_id(0) < per, *refs),
+        run,
         grid=(2 * per,),
-        in_specs=[square] * len(matrices)
-        + [spec("whole")] * len(wholes)
-        + [spec("left")] * len(lefts)
-        + [spec("right")] * len(rights)
-        + [spec("sums")] * len(sums),
-        out_specs=tuple(spec(kind) for kind in outs),
+        in_specs=[pl.BlockSpec(x.shape, lambda j: (0, 0)) for x in matrices]
+        + [spec(kind, x.shape[0]) for kind, x in ins],
+        out_specs=tuple(spec(kind, shapes[kind][0]) for kind in outs),
         out_shape=tuple(jax.ShapeDtypeStruct(shapes[kind], jnp.float32) for kind in outs),
-    )(*matrices, *wholes, *lefts, *rights, *sums)
-
-
-def first_kernel(is_left, low, high, inv, low0, high0, low1, high1, v_ref, w_ref, m_ref):
-    def run(x_low, x_high):
-        v = dot3(left3(low[...]), right3(x_low[...])) + dot3(left3(high[...]), right3(x_high[...]))
-        w = dot3(left3(inv[...]), right3(v))
-        v_ref[...] = v
-        w_ref[...] = w
-        m_ref[...] = at_row(2, sums_of(v, w))
-
-    pl.when(is_left)(lambda: run(low0, high0))
-    pl.when(jnp.logical_not(is_left))(lambda: run(low1, high1))
-
-
-def start_kernel(is_left, inv, v0, v1, m_in, w_ref, m_ref):
-    w = dot3(left3(inv[...]), right3(v0[...]))
+        scratch_shapes=[pltpu.VMEM((kept, rows, 3 * rows), jnp.bfloat16)],
+    )(*matrices, *(x for _, x in ins))
+
+
+def keep(step, mats, three):
+    @pl.when(step == 0)
+    def _():
+        for k, mat in enumerate(mats):
+            three[k] = left3(mat[...])
+
+
+def first_kernel(step, per, mats, three, low0, high0, low1, high1, v_ref, w_ref, m_ref):
+    low, high, inv, inv_low, inv_high = mats
+
+    @pl.when(step == 0)
+    def _():
+        three[0] = left3(mm(low[...], inv_low[...]))
+        three[1] = left3(mm(high[...], inv_high[...]))
+        three[2] = left3(inv[...])
+
+    x_low = jnp.concatenate([low0[...], low1[...]], axis=0)
+    x_high = jnp.concatenate([high0[...], high1[...]], axis=0)
+    v = dot3(three[0], right3(x_low)) + dot3(three[1], right3(x_high))
+    w = dot3(three[2], right3(v))
+    v_ref[...] = v
+    w_ref[...] = w
+    m_ref[...] = at_row(2, sums_of(v, w))
+
+
+def start_kernel(step, per, mats, three, v0, v1, m_in, w_ref, m_ref):
+    keep(step, mats, three)
+    w = dot3(three[0], right3(v0[...]))
     w_ref[...] = w
     m_ref[...] = m_in[...] + at_row(0, sums_of(v0[...], w)) + at_row(1, sums_of(v1[...], w))
 
 
-def second_kernel(is_left, low, high, inv, x_low, x_high, w1, m_in, v_ref, left_ref, right_ref, m_ref):
-    v = dot3(left3(low[...]), right3(x_low[...])) + dot3(left3(high[...]), right3(x_high[...]))
-    w = dot3(left3(inv[...]), right3(v))
+def second_kernel(step, per, mats, three, x_low, x_high, w1, m_in, v_ref, left_ref, right_ref, m_ref):
+    keep(step, mats, three)
+    v = dot3(three[0], right3(x_low[...])) + dot3(three[1], right3(x_high[...]))
+    w = dot3(three[2], right3(v))
     v_ref[...] = v
     m_ref[...] = m_in[...] + at_row(3, sums_of(v, w1[...])) + at_row(4, sums_of(v, w))
 
-    @pl.when(is_left)
+    @pl.when(step < per)
     def _():
         left_ref[...] = w
 
-    @pl.when(jnp.logical_not(is_left))
+    @pl.when(step >= per)
     def _():
         right_ref[...] = w
 
 
-def side_kernel(is_left, low, high, w0_half, x_high, w1_half, x_low, m_in, t_ref, m_ref):
-    def run(band, x, w):
-        t = dot3(left3(band[...]), right3(x[...]))
-        t_ref[...] = t
-        m_ref[...] = m_in[...] + at_row(5, 2.0 * sums_of(t, w[...]))
-
-    pl.when(is_left)(lambda: run(high, x_high, w0_half))
-    pl.when(jnp.logical_not(is_left))(lambda: run(low, x_low, w1_half))
+def side_kernel(step, per, mats, three, w_left, x_high, w_right, x_low, m_in, t_ref, m_ref):
+    keep(step, mats, three)
+    left = step < per
+    x = jnp.where(left, x_high[...], x_low[...])
+    w = jnp.where(left, w_left[...], w_right[...])
+    t = dot3(three[jnp.where(left, 1, 0)], right3(x))
+    t_ref[...] = t
+    m_ref[...] = m_in[...] + at_row(5, 2.0 * sums_of(t, w))
 
 
 def safe(num, den):
@@ -412,17 +431,16 @@
 
 
 def finish_kernel(
-    is_left, low, high, v0, w0, v1, w1, v2, t, w2_0, x_low, w2_1, x_high, sums, sol_ref, res_ref
+    step, per, mats, three, v0, w0, v1, w1, v2, t, w_left, x_low, w_right, x_high, sums, sol, res
 ):
+    keep(step, mats, three)
+    left = step < per
+    far = jnp.where(left, x_low[...], x_high[...])
+    w2 = jnp.where(left, w_left[...], w_right[...])
+    v3 = t[...] + dot3(three[jnp.where(left, 0, 1)], right3(far))
     x, c = coefficients([sums[k : k + 1, :] for k in range(6)])
-
-    def run(band, far, w2):
-        v3 = t[...] + dot3(left3(band[...]), right3(far[...]))
-        sol_ref[...] = x[0] * w0[...] + x[1] * w1[...] + x[2] * w2[...]
-        res_ref[...] = c[0] * v0[...] + c[1] * v1[...] + c[2] * v2[...] + c[3] * v3
-
-    pl.when(is_left)(lambda: run(low, x_low, w2_0))
-    pl.when(jnp.logical_not(is_left))(lambda: run(high, x_high, w2_1))
+    sol[...] = x[0] * w0[...] + x[1] * w1[...] + x[2] * w2
+    res[...] = c[0] * v0[...] + c[1] * v1[...] + c[2] * v2[...] + c[3] * v3
 
 
 def butterfly(x, devices, bits):
@@ -445,9 +463,8 @@
         return lax.ppermute(x, AXES, down)
 
     base = jnp.stack([lax.axis_index(AXES) * own, own * devices]).astype(jnp.int32)
-    width = right_side.shape[1] // 2
     r_low, r_high = {}, {}
-    start = right_side[:, :width]
+    start = right_side[: own // 2]
     r_low[0] = from_below(start)
     r_high[0] = from_above(start)
     send0, send1 = pack(owner_map, connect.T, blocks, devices)
@@ -461,7 +478,7 @@
     got0 = exchange(send0)
     got1 = exchange(send1)
     rest, got0 = lax.optimization_barrier((right_side, got0))
-    rest = rest[:, width:]
+    rest = rest[own // 2 :]
     r_low[1], r_high[1] = from_below(rest), from_above(rest)
     part = assemble(base, got0, window)
     center, high_band, lower = assemble(base, got1, window, part)
@@ -469,20 +486,19 @@
     low_band = lower[:, :own]
     inv = invert(center, lower)
     inv_low, inv_high = from_below(inv), from_above(inv)
-    near_low, near_high = mm(low_band, inv_low), mm(high_band, inv_high)
-
     v0 = right_side
     v1, w1, sums = in_blocks(
         first_kernel,
-        (near_low, near_high, inv),
+        (low_band, high_band, inv, inv_low, inv_high),
+        (r_low[0], r_high[0], r_low[1], r_high[1]),
         (),
-        (r_low[0], r_high[0]),
-        (r_low[1], r_high[1]),
+        (),
         (),
         ("whole", "whole", "sums"),
+        3,
     )
     w1_low, w1_high = from_below(w1), from_above(w1)
-    w0, sums = in_blocks(start_kernel, (inv,), (v0, v1), (), (), (sums,), ("whole", "sums"))
+    w0, sums = in_blocks(start_kernel, (inv,), (v0, v1), (), (), (sums,), ("whole", "sums"), 1)
     v2, w2_0, w2_1, sums = in_blocks(
         second_kernel,
         (low_band, high_band, inv),
@@ -491,6 +507,7 @@
         (),
         (sums,),
         ("whole", "left", "right", "sums"),
+        3,
     )
     near_0 = from_above(w2_0)
     near_1 = from_below(w2_1)
@@ -499,7 +516,7 @@
     far_1 = from_above(later_1)
     bands = (low_band, high_band)
     t, sums = in_blocks(
-        side_kernel, bands, (), (w2_0, near_0), (w2_1, near_1), (sums,), ("whole", "sums")
+        side_kernel, bands, (), (w2_0, near_0), (w2_1, near_1), (sums,), ("whole", "sums"), 2
     )
     sums = butterfly(sums, devices, (64, 32, 8, 4, 16, 2, 1))
     return in_blocks(
@@ -510,6 +527,7 @@
         (w2_1, far_1),
         (sums,),
         ("whole", "whole"),
+        2,
     )
 
 

time: 352 us -> 322 us (0.915)
  Pallas kernels: 97.2 us -> 86.2 us
  waiting for transfers between devices: 134 us -> 126 us
  starting transfers between devices: 58.7 us -> 50.9 us
    ppermute x7, starting transfers between devices: 22.4 us -> 10.5 us  [butterfly(): x = x + lax.ppermute(x, AXES, [(i, i ^ bit) for i in range(devices)])]
    pallas_call x5, Pallas kernels: 46.8 us -> 35.9 us  [in_blocks(): pl.pallas_call(run, grid=(2 * per,), in_specs=[pl.BlockSpec(x.shape, lamb...]
    ppermute x6, starting transfers between devices: 16.2 us -> 26.8 us  [from_above(): return lax.ppermute(x, AXES, down)]
    all_to_all x1, waiting for transfers between devices: 9.65 us -> 0.01 us  [exchange(): lax.all_to_all(send.reshape(devices, ROWS, 128), AXES, split_axis=0, conc...]
    ppermute x7, starting transfers between devices: 14.4 us -> 7.71 us  [from_below(): return lax.ppermute(x, AXES, up)]
  transfers between devices with their start and end apart: 21 -> 21, of which waited for: 14 -> 14; matrix products, arithmetic and copies ran while one was open for 2% -> 2% of each run, Pallas kernels for 13% -> 16%
where the time goes in v3:
time: 322 us; the launch traced here: 320 us
  waiting for transfers between devices  126 us (39%)
  Pallas kernels  86.2 us (27%)
  starting transfers between devices  50.9 us (16%)
  blocking collectives  46.3 us (14%)
  local copies, waits for them, and re-layouts  7.5 us (2%)
    ppermute x6, waiting for transfers between devices, from_above(): return lax.ppermute(x, AXES, down)  59.3 us
    all_to_all x1, blocking collectives, exchange(): lax.all_to_all(send.reshape(devices, ROWS, 128), AXES, split_axis=0, conc...  46.3 us
    ppermute x7, waiting for transfers between devices, from_below(): return lax.ppermute(x, AXES, up)  40.8 us
    pallas_call x5, Pallas kernels, in_blocks(): pl.pallas_call(run, grid=(2 * per,), in_specs=[pl.BlockSpec(x.shape, lamb...  35.9 us
    pallas_call x2, Pallas kernels, assemble(): pl.pallas_call(lambda *refs: assemble_kernel(last, *refs), out_shape=out,...  34 us
    ppermute x6, starting transfers between devices, from_above(): return lax.ppermute(x, AXES, down)  26.8 us
    ppermute x7, waiting for transfers between devices, butterfly(): x = x + lax.ppermute(x, AXES, [(i, i ^ bit) for i in range(devices)])  26.3 us
    ppermute x7, starting transfers between devices, butterfly(): x = x + lax.ppermute(x, AXES, [(i, i ^ bit) for i in range(devices)])  10.5 us
  transfers between devices with their start and end apart: 21, of which 14 were waited for; matrix products, arithmetic and copies ran while one was open for 2% of the time, Pallas kernels for 16%

profile of v3, /device:TPU:0, one launch (start us, length us, event | category | flops | bytes accessed | tf_op | source)
XLA Modules:
  0.0 320.5 jit_solution(15749980105038454837)
XLA Ops:
  0.6 8.7 %pack.1 = (f32[5120,128]{1,0:T(8,128)}, f32[5120,128]{1,0:T(8,128)}) custom-call(s32[1,128]{1,0:T(1,128)} %bitcast.11, s32[96,128]{1,0:T(8,128)} %bitcast.10, f32[128,9216]{1,0:T(8,128)} %x_ref.1), custom_call_target="tpu_custom_call" | custom-call | tf_op jit(solution)/shard_map/pack/pallas_call | solution.py:95
  9.3 46.3 %all_to_all.10 = f32[128,40,128]{2,1,0:T(8,128)} all-to-all(f32[128,40,128]{2,1,0:T(8,128)} %bitcast.9), channel_id=1, replica_groups=mesh['row'=8,'col'=16] {'row','col'}, dimensions={0} | all-to-all | bytes 5242880 | tf_op jit(solution)/shard_map/all_to_all | solution.py:473
  55.7 5.9 %all-to-all-start = ((f32[128,40,128]{2,1,0:T(8,128)}), f32[128,40,128]{2,1,0:T(8,128)}, u32[]{:S(2)}, u32[]{:S(2)}) async-start(f32[128,40,128]{2,1,0:T(8,128)} %bitcast.8), calls=%async_computation | async-start | bytes 5242880 | tf_op jit(solution)/shard_map/all_to_all | solution.py:473
  61.5 1.0 slice.10
  62.6 7.0 %collective-permute-start.4 = (f32[128,2048]{1,0:T(8,128)}, f32[128,2048]{1,0:T(8,128)}, u32[]{:S(2)}, u32[]{:S(2)}) collective-permute-start(f32[128,2048]{1,0:T(8,128)} %slice.10), channel_id=1, source_target_pairs={{1,0},{2,1},{3,2},{4,3},{5,4},{6,5},{7,6},{8,7},{9,8},{10,9},{11,1... | collective-permute-start | bytes 3145736 | tf_op jit(solution)/shard_map/ppermute | solution.py:463
  69.5 0.0 collective-permute-start.3
  69.6 0.1 slice.11
  69.6 7.2 %collective-permute-start.6 = (f32[128,2048]{1,0:T(8,128)S(1)}, f32[128,2048]{1,0:T(8,128)S(1)}, u32[]{:S(2)}, u32[]{:S(2)}) collective-permute-start(f32[128,2048]{1,0:T(8,128)S(1)} %slice.11), channel_id=1, source_target_pairs={{1,0},{2,1},{3,2},{4,3},{5,4},{6,5},{7,6},{8,7},{9,8},{10,9},{11,1... | collective-permute-start | bytes 3145736 | tf_op jit(solution)/shard_map/ppermute | solution.py:463
  76.9 0.0 collective-permute-start.5
  76.9 0.6 pad_add_fusion.refs_0_
  77.5 24.4 %assemble_first.1.refs_2_ = f32[512,512]{1,0:T(8,128)} custom-call(s32[2]{0:T(128)} %pad_add_fusion.refs_0_, f32[5120,128]{1,0:T(8,128)} %bitcast.7), custom_call_target="tpu_custom_call" | custom-call | tf_op jit(solution)/shard_map/assemble_first/pallas_call | solution.py:240
  101.9 0.0 all-to-all-done
  101.9 9.6 %assemble_last.1 = (f32[256,256]{1,0:T(8,128)}, f32[256,256]{1,0:T(8,128)}, f32[256,512]{1,0:T(8,128)}) custom-call(s32[2]{0:T(128)} %pad_add_fusion.refs_0_, f32[5120,128]{1,0:T(8,128)} %bitcast.4.refs_1_, f32[512,512]{1,0:T(8,128)} %assemble_first.1.refs_2_), custom_call_target="tpu_custom_call" | custom-call | tf_op jit(solution)/shard_map/assemble_last/pallas_call | solution.py:240
  111.6 0.3 collective-permute-start
  111.8 32.6 %collective-permute-done.lower_ref = f32[256,512]{1,0:T(8,128)S(1)} collective-permute-done((f32[256,512]{1,0:T(8,128)}, f32[256,512]{1,0:T(8,128)S(1)}, u32[]{:S(2)}, u32[]{:S(2)}) %collective-permute-start) | collective-permute-done | bytes 524320 | tf_op jit(solution)/shard_map/ppermute | solution.py:460
  144.5 0.8 copy-done.2
  145.3 7.6 %invert.1.refs_2_.refs_0_ = f32[256,256]{1,0:T(8,128)} custom-call(f32[256,256]{1,0:T(8,128)} %get-tuple-element.29.upper_ref, f32[256,512]{1,0:T(8,128)} %copy-done.2), custom_call_target="tpu_custom_call" | custom-call | tf_op jit(solution)/shard_map/invert/pallas_call | solution.py:277
  152.9 8.7 %collective-permute-start.2 = (f32[256,256]{1,0:T(8,128)}, f32[256,256]{1,0:T(8,128)S(1)}, u32[]{:S(2)}, u32[]{:S(2)}) collective-permute-start(f32[256,256]{1,0:T(8,128)} %invert.1.refs_2_.refs_0_), channel_id=1, source_target_pairs={{1,0},{2,1},{3,2},{4,3},{5,4},{6,5},{7,6},{8,7},{9,8},{10,9},{11,1... | collective-permute-start | bytes 786440 | tf_op jit(solution)/shard_map/ppermute | solution.py:463
  161.6 0.0 collective-permute-done.4.refs_6_
  161.6 0.0 collective-permute-start.1
  161.6 1.7 slice.12.refs_0_
  163.3 0.0 collective-permute-done.3.refs_5_
  163.3 2.6 collective-permute-done.2.refs_4_
  165.9 7.2 %collective-permute-done.1.refs_3_ = f32[256,256]{1,0:T(8,128)S(1)} collective-permute-done((f32[256,256]{1,0:T(8,128)}, f32[256,256]{1,0:T(8,128)S(1)}, u32[]{:S(2)}, u32[]{:S(2)}) %collective-permute-start.1) | collective-permute-done | bytes 262176 | tf_op jit(solution)/shard_map/ppermute | solution.py:460
  173.1 0.0 collective-permute-done.6.refs_8_
  173.1 0.7 copy-done.9
  173.8 0.4 copy-done.5
  174.1 7.7 %shard_map.59 = (f32[256,2048]{1,0:T(8,128)}, f32[256,2048]{1,0:T(8,128)}, f32[8,2048]{1,0:T(8,128)}) custom-call(f32[256,256]{1,0:T(8,128)} %slice.12.refs_0_, f32[256,256]{1,0:T(8,128)} %get-tuple-element.28.refs_1_, f32[256,256]{1,0:T(8,128)} %invert.1.refs_2_.refs_0_, f32[256,256]{1,0:T(8,128)} %copy-done.9, f32[256,256]{1,0:T(8,128)} %copy-done.8, ...), custom_call_target="tpu_custom_call" | custom-call | tf_op jit(solution)/shard_map/pallas_call | solution.py:342
  181.8 0.2 collective-permute-start.8
  182.0 1.8 collective-permute-start.7
  183.8 5.2 %shard_map.60 = (f32[256,2048]{1,0:T(8,128)}, f32[8,2048]{1,0:T(8,128)}) custom-call(f32[256,256]{1,0:T(8,128)} %invert.1.refs_2_.refs_0_, f32[256,2048]{1,0:T(8,128)} %refs_2_.1, f32[256,2048]{1,0:T(8,128)} %get-tuple-element.31.refs_2_.refs_4_, f32[8,2048]{1,0:T(8,128)} %get-tuple-element.32.refs_3_), custom_call_target="tpu_custom_call" | custom-call | tf_op jit(solution)/shard_map/pallas_call | solution.py:342
  189.0 37.1 %collective-permute-done.8.refs_4_ = f32[256,2048]{1,0:T(8,128)S(1)} collective-permute-done((f32[256,2048]{1,0:T(8,128)}, f32[256,2048]{1,0:T(8,128)S(1)}, u32[]{:S(2)}, u32[]{:S(2)}) %collective-permute-start.8) | collective-permute-done | bytes 2097184 | tf_op jit(solution)/shard_map/ppermute | solution.py:463
  226.1 0.8 collective-permute-done.7.refs_3_
  226.9 0.5 copy-done.1
  227.4 8.0 %shard_map.61 = (f32[256,2048]{1,0:T(8,128)}, f32[256,1024]{1,0:T(8,128)}, f32[256,1024]{1,0:T(8,128)}, f32[8,2048]{1,0:T(8,128)}) custom-call(f32[256,256]{1,0:T(8,128)} %slice.12.refs_0_, f32[256,256]{1,0:T(8,128)} %get-tuple-element.28.refs_1_, f32[256,256]{1,0:T(8,128)} %invert.1.refs_2_.refs_0_, f32[256,2048]{1,0:T(8,128)} %collective-permute-done.7.refs_3_, ...), custom_call_target="tpu_custom_call" | custom-call | tf_op jit(solution)/shard_map/pallas_call | solution.py:342
  235.5 0.1 collective-permute-start.9
  235.6 2.1 collective-permute-start.10
  237.7 19.7 %collective-permute-done.9.refs_3_ = f32[256,1024]{1,0:T(8,128)S(1)} collective-permute-done((f32[256,1024]{1,0:T(8,128)}, f32[256,1024]{1,0:T(8,128)S(1)}, u32[]{:S(2)}, u32[]{:S(2)}) %collective-permute-start.9) | collective-permute-done | bytes 1048608 | tf_op jit(solution)/shard_map/ppermute | solution.py:463
  257.3 0.1 collective-permute-done.10.refs_5_
  257.4 1.1 copy-done.7
  258.5 3.5 %collective-permute-start.11 = (f32[256,1024]{1,0:T(8,128)}, f32[256,1024]{1,0:T(8,128)S(1)}, u32[]{:S(2)}, u32[]{:S(2)}) collective-permute-start(f32[256,1024]{1,0:T(8,128)} %get-tuple-element.43.refs_2_.refs_8_), channel_id=1, source_target_pairs={{0,1},{1,2},{2,3},{3,4},{4,5},{5,6},{6,7},{7,8},{8,9},{9,10},{10,1... | collective-permute-start | bytes 3145736 | tf_op jit(solution)/shard_map/ppermute | solution.py:460
  262.0 3.7 %collective-permute-start.12 = (f32[256,1024]{1,0:T(8,128)}, f32[256,1024]{1,0:T(8,128)S(1)}, u32[]{:S(2)}, u32[]{:S(2)}) collective-permute-start(f32[256,1024]{1,0:T(8,128)} %get-tuple-element.44.refs_4_.refs_10_), channel_id=1, source_target_pairs={{1,0},{2,1},{3,2},{4,3},{5,4},{6,5},{7,6},{8,7},{9,8},{10,9},{11,1... | collective-permute-start | bytes 3145736 | tf_op jit(solution)/shard_map/ppermute | solution.py:463
  265.7 5.6 %shard_map.62 = (f32[256,2048]{1,0:T(8,128)}, f32[8,2048]{1,0:T(8,128)}) custom-call(f32[256,256]{1,0:T(8,128)} %slice.12.refs_0_, f32[256,256]{1,0:T(8,128)} %get-tuple-element.28.refs_1_, f32[256,1024]{1,0:T(8,128)} %get-tuple-element.43.refs_2_.refs_8_, f32[256,1024]{1,0:T(8,128)} %copy-done.6, f32[256,1024]{1,0:T(8,128)} %get-tuple-element.44.refs_4_.refs_10_, ...), custom_call_target="tpu_custom_call" | custom-call | tf_op jit(solution)/shard_map/pallas_call | solution.py:342
  271.3 3.7 %collective-permute-start.13 = (f32[8,2048]{1,0:T(8,128)}, f32[8,2048]{1,0:T(8,128)S(1)}, u32[]{:S(2)}, u32[]{:S(2)}) collective-permute-start(f32[8,2048]{1,0:T(8,128)} %get-tuple-element.45), channel_id=1, source_target_pairs={{0,64},{1,65},{2,66},{3,67},{4,68},{5,69},{6,70},{7,71},{8,72},{9,... | collective-permute-start | bytes 196616 | tf_op jit(solution)/shard_map/ppermute | solution.py:448
  275.0 2.5 collective-permute-done.13
  277.5 0.9 add.25
  278.3 6.3 %collective-permute-start.14 = (f32[8,2048]{1,0:T(8,128)S(1)}, f32[8,2048]{1,0:T(8,128)S(1)}, u32[]{:S(2)}, u32[]{:S(2)}) collective-permute-start(f32[8,2048]{1,0:T(8,128)S(1)} %add.25), channel_id=1, source_target_pairs={{0,32},{1,33},{2,34},{3,35},{4,36},{5,37},{6,38},{7,39},{8,40},{9,... | collective-permute-start | bytes 196616 | tf_op jit(solution)/shard_map/ppermute | solution.py:448
  284.6 2.6 collective-permute-done.14
  287.2 0.1 collective-permute-start.15
  287.3 5.8 %collective-permute-done.15 = f32[8,2048]{1,0:T(8,128)S(1)} collective-permute-done((f32[8,2048]{1,0:T(8,128)S(1)}, f32[8,2048]{1,0:T(8,128)S(1)}, u32[]{:S(2)}, u32[]{:S(2)}) %collective-permute-start.15) | collective-permute-done | bytes 65568 | tf_op jit(solution)/shard_map/ppermute | solution.py:448
  293.1 0.1 collective-permute-start.16
  293.2 4.3 %collective-permute-done.16 = f32[8,2048]{1,0:T(8,128)S(1)} collective-permute-done((f32[8,2048]{1,0:T(8,128)S(1)}, f32[8,2048]{1,0:T(8,128)S(1)}, u32[]{:S(2)}, u32[]{:S(2)}) %collective-permute-start.16) | collective-permute-done | bytes 65568 | tf_op jit(solution)/shard_map/ppermute | solution.py:448
  297.5 0.1 collective-permute-start.17
  297.5 1.2 collective-permute-done.17
  298.8 0.1 collective-permute-start.18
  298.9 5.8 %collective-permute-done.18 = f32[8,2048]{1,0:T(8,128)S(1)} collective-permute-done((f32[8,2048]{1,0:T(8,128)S(1)}, f32[8,2048]{1,0:T(8,128)S(1)}, u32[]{:S(2)}, u32[]{:S(2)}) %collective-permute-start.18) | collective-permute-done | bytes 65568 | tf_op jit(solution)/shard_map/ppermute | solution.py:448
  304.7 0.1 collective-permute-start.19
  304.8 4.3 %collective-permute-done.19 = f32[8,2048]{1,0:T(8,128)S(1)} collective-permute-done((f32[8,2048]{1,0:T(8,128)S(1)}, f32[8,2048]{1,0:T(8,128)S(1)}, u32[]{:S(2)}, u32[]{:S(2)}) %collective-permute-start.19) | collective-permute-done | bytes 65568 | tf_op jit(solution)/shard_map/ppermute | solution.py:448
  309.0 0.6 add.31.refs_12_
  309.6 0.0 collective-permute-done.11.refs_9_
  309.6 0.0 collective-permute-done.12.refs_11_
  309.7 1.0 copy-done.3
  310.6 0.3 copy-done.4
  311.0 9.3 %shard_map.63 = (f32[256,2048]{1,0:T(8,128)}, f32[256,2048]{1,0:T(8,128)}) custom-call(f32[256,256]{1,0:T(8,128)} %slice.12.refs_0_, f32[256,256]{1,0:T(8,128)} %get-tuple-element.28.refs_1_, f32[256,2048]{1,0:T(8,128)} %refs_2_.1, f32[256,2048]{1,0:T(8,128)} %get-tuple-element.33.refs_3_, f32[256,2048]{1,0:T(8,128)} %get-tuple-element.31.refs_2_.refs_4_, ...), custom_call_target="tpu_custom_call" | custom-call | tf_op jit(solution)/shard_map/pallas_call | solution.py:342
  (19 shorter events, 0.1 us)
Async XLA Ops:
  55.7 5.9 %copy-start = (f32[256,2048]{1,0:T(8,128)S(1)}, f32[256,2048]{1,0:T(8,128)}, u32[]{:S(2)}) copy-start(f32[256,2048]{1,0:T(8,128)} %refs_2_.1) | copy-start | bytes 6291460
  55.7 46.2 %all-to-all-start = ((f32[128,40,128]{2,1,0:T(8,128)}), f32[128,40,128]{2,1,0:T(8,128)}, u32[]{:S(2)}, u32[]{:S(2)}) async-start(f32[128,40,128]{2,1,0:T(8,128)} %bitcast.8), calls=%async_computation | async-start | bytes 5242880 | tf_op jit(solution)/shard_map/all_to_all | solution.py:473
  62.6 99.0 %collective-permute-start.4 = (f32[128,2048]{1,0:T(8,128)}, f32[128,2048]{1,0:T(8,128)}, u32[]{:S(2)}, u32[]{:S(2)}) collective-permute-start(f32[128,2048]{1,0:T(8,128)} %slice.10), channel_id=1, source_target_pairs={{1,0},{2,1},{3,2},{4,3},{5,4},{6,5},{7,6},{8,7},{9,8},{10,9},{11,1... | collective-permute-start | bytes 3145736 | tf_op jit(solution)/shard_map/ppermute | solution.py:463
  69.5 93.8 %collective-permute-start.3 = (f32[128,2048]{1,0:T(8,128)}, f32[128,2048]{1,0:T(8,128)}, u32[]{:S(2)}, u32[]{:S(2)}) collective-permute-start(f32[128,2048]{1,0:T(8,128)} %slice.10), channel_id=1, source_target_pairs={{0,1},{1,2},{2,3},{3,4},{4,5},{5,6},{6,7},{7,8},{8,9},{9,10},{10,1... | collective-permute-start | bytes 3145736 | tf_op jit(solution)/shard_map/ppermute | solution.py:460
  69.6 103.4 %collective-permute-start.6 = (f32[128,2048]{1,0:T(8,128)S(1)}, f32[128,2048]{1,0:T(8,128)S(1)}, u32[]{:S(2)}, u32[]{:S(2)}) collective-permute-start(f32[128,2048]{1,0:T(8,128)S(1)} %slice.11), channel_id=1, source_target_pairs={{1,0},{2,1},{3,2},{4,3},{5,4},{6,5},{7,6},{8,7},{9,8},{10,9},{11,1... | collective-permute-start | bytes 3145736 | tf_op jit(solution)/shard_map/ppermute | solution.py:463
  76.9 96.2 %collective-permute-start.5 = (f32[128,2048]{1,0:T(8,128)S(1)}, f32[128,2048]{1,0:T(8,128)}, u32[]{:S(2)}, u32[]{:S(2)}) collective-permute-start(f32[128,2048]{1,0:T(8,128)S(1)} %slice.11), channel_id=1, source_target_pairs={{0,1},{1,2},{2,3},{3,4},{4,5},{5,6},{6,7},{7,8},{8,9},{9,10},{10,1... | collective-permute-start | bytes 3145736 | tf_op jit(solution)/shard_map/ppermute | solution.py:460
  111.6 32.9 %collective-permute-start = (f32[256,512]{1,0:T(8,128)}, f32[256,512]{1,0:T(8,128)S(1)}, u32[]{:S(2)}, u32[]{:S(2)}) collective-permute-start(f32[256,512]{1,0:T(8,128)} %get-tuple-element.27), channel_id=1, source_target_pairs={{0,1},{1,2},{2,3},{3,4},{4,5},{5,6},{6,7},{7,8},{8,9},{9,10},{10,1... | collective-permute-start | bytes 1572872 | tf_op jit(solution)/shard_map/ppermute | solution.py:460
  144.5 0.8 copy-start.2
  152.9 13.0 %collective-permute-start.2 = (f32[256,256]{1,0:T(8,128)}, f32[256,256]{1,0:T(8,128)S(1)}, u32[]{:S(2)}, u32[]{:S(2)}) collective-permute-start(f32[256,256]{1,0:T(8,128)} %invert.1.refs_2_.refs_0_), channel_id=1, source_target_pairs={{1,0},{2,1},{3,2},{4,3},{5,4},{6,5},{7,6},{8,7},{9,8},{10,9},{11,1... | collective-permute-start | bytes 786440 | tf_op jit(solution)/shard_map/ppermute | solution.py:463
  161.6 11.4 %collective-permute-start.1 = (f32[256,256]{1,0:T(8,128)}, f32[256,256]{1,0:T(8,128)S(1)}, u32[]{:S(2)}, u32[]{:S(2)}) collective-permute-start(f32[256,256]{1,0:T(8,128)} %invert.1.refs_2_.refs_0_), channel_id=1, source_target_pairs={{0,1},{1,2},{2,3},{3,4},{4,5},{5,6},{6,7},{7,8},{8,9},{9,10},{10,1... | collective-permute-start | bytes 786440 | tf_op jit(solution)/shard_map/ppermute | solution.py:460
  165.9 7.2 %copy-start.8 = (f32[256,256]{1,0:T(8,128)}, f32[256,256]{1,0:T(8,128)S(1)}, u32[]{:S(2)}) copy-start(f32[256,256]{1,0:T(8,128)S(1)} %collective-permute-done.2.refs_4_) | copy-start | bytes 786436
  173.0 0.7 copy-start.9
  173.1 1.1 copy-start.5
  181.8 44.3 %collective-permute-start.8 = (f32[256,2048]{1,0:T(8,128)}, f32[256,2048]{1,0:T(8,128)S(1)}, u32[]{:S(2)}, u32[]{:S(2)}) collective-permute-start(f32[256,2048]{1,0:T(8,128)} %get-tuple-element.34.refs_5_), channel_id=1, source_target_pairs={{1,0},{2,1},{3,2},{4,3},{5,4},{6,5},{7,6},{8,7},{9,8},{10,9},{11,1... | collective-permute-start | bytes 6291464 | tf_op jit(solution)/shard_map/ppermute | solution.py:463
  182.0 45.0 %collective-permute-start.7 = (f32[256,2048]{1,0:T(8,128)}, f32[256,2048]{1,0:T(8,128)}, u32[]{:S(2)}, u32[]{:S(2)}) collective-permute-start(f32[256,2048]{1,0:T(8,128)} %get-tuple-element.34.refs_5_), channel_id=1, source_target_pairs={{0,1},{1,2},{2,3},{3,4},{4,5},{5,6},{6,7},{7,8},{8,9},{9,10},{10,1... | collective-permute-start | bytes 6291464 | tf_op jit(solution)/shard_map/ppermute | solution.py:460
  226.1 1.3 copy-start.1
  235.5 21.9 %collective-permute-start.9 = (f32[256,1024]{1,0:T(8,128)}, f32[256,1024]{1,0:T(8,128)S(1)}, u32[]{:S(2)}, u32[]{:S(2)}) collective-permute-start(f32[256,1024]{1,0:T(8,128)} %get-tuple-element.43.refs_2_.refs_8_), channel_id=1, source_target_pairs={{1,0},{2,1},{3,2},{4,3},{5,4},{6,5},{7,6},{8,7},{9,8},{10,9},{11,1... | collective-permute-start | bytes 3145736 | tf_op jit(solution)/shard_map/ppermute | solution.py:463
  235.6 21.9 %collective-permute-start.10 = (f32[256,1024]{1,0:T(8,128)}, f32[256,1024]{1,0:T(8,128)S(1)}, u32[]{:S(2)}, u32[]{:S(2)}) collective-permute-start(f32[256,1024]{1,0:T(8,128)} %get-tuple-element.44.refs_4_.refs_10_), channel_id=1, source_target_pairs={{0,1},{1,2},{2,3},{3,4},{4,5},{5,6},{6,7},{7,8},{8,9},{9,10},{10,1... | collective-permute-start | bytes 3145736 | tf_op jit(solution)/shard_map/ppermute | solution.py:460
  257.3 8.3 %copy-start.6 = (f32[256,1024]{1,0:T(8,128)}, f32[256,1024]{1,0:T(8,128)S(1)}, u32[]{:S(2)}) copy-start(f32[256,1024]{1,0:T(8,128)S(1)} %collective-permute-done.9.refs_3_) | copy-start | bytes 3145732
  257.4 1.1 copy-start.7
  258.5 51.1 %collective-permute-start.11 = (f32[256,1024]{1,0:T(8,128)}, f32[256,1024]{1,0:T(8,128)S(1)}, u32[]{:S(2)}, u32[]{:S(2)}) collective-permute-start(f32[256,1024]{1,0:T(8,128)} %get-tuple-element.43.refs_2_.refs_8_), channel_id=1, source_target_pairs={{0,1},{1,2},{2,3},{3,4},{4,5},{5,6},{6,7},{7,8},{8,9},{9,10},{10,1... | collective-permute-start | bytes 3145736 | tf_op jit(solution)/shard_map/ppermute | solution.py:460
  262.0 47.6 %collective-permute-start.12 = (f32[256,1024]{1,0:T(8,128)}, f32[256,1024]{1,0:T(8,128)S(1)}, u32[]{:S(2)}, u32[]{:S(2)}) collective-permute-start(f32[256,1024]{1,0:T(8,128)} %get-tuple-element.44.refs_4_.refs_10_), channel_id=1, source_target_pairs={{1,0},{2,1},{3,2},{4,3},{5,4},{6,5},{7,6},{8,7},{9,8},{10,9},{11,1... | collective-permute-start | bytes 3145736 | tf_op jit(solution)/shard_map/ppermute | solution.py:463
  271.3 6.2 %collective-permute-start.13 = (f32[8,2048]{1,0:T(8,128)}, f32[8,2048]{1,0:T(8,128)S(1)}, u32[]{:S(2)}, u32[]{:S(2)}) collective-permute-start(f32[8,2048]{1,0:T(8,128)} %get-tuple-element.45), channel_id=1, source_target_pairs={{0,64},{1,65},{2,66},{3,67},{4,68},{5,69},{6,70},{7,71},{8,72},{9,... | collective-permute-start | bytes 196616 | tf_op jit(solution)/shard_map/ppermute | solution.py:448
  278.3 8.9 %collective-permute-start.14 = (f32[8,2048]{1,0:T(8,128)S(1)}, f32[8,2048]{1,0:T(8,128)S(1)}, u32[]{:S(2)}, u32[]{:S(2)}) collective-permute-start(f32[8,2048]{1,0:T(8,128)S(1)} %add.25), channel_id=1, source_target_pairs={{0,32},{1,33},{2,34},{3,35},{4,36},{5,37},{6,38},{7,39},{8,40},{9,... | collective-permute-start | bytes 196616 | tf_op jit(solution)/shard_map/ppermute | solution.py:448
  287.2 5.8 %collective-permute-start.15 = (f32[8,2048]{1,0:T(8,128)S(1)}, f32[8,2048]{1,0:T(8,128)S(1)}, u32[]{:S(2)}, u32[]{:S(2)}) collective-permute-start(f32[8,2048]{1,0:T(8,128)S(1)} %add.26), channel_id=1, source_target_pairs={{0,8},{1,9},{2,10},{3,11},{4,12},{5,13},{6,14},{7,15},{8,0},{9,1},... | collective-permute-start | bytes 196616 | tf_op jit(solution)/shard_map/ppermute | solution.py:448
  293.1 4.3 %collective-permute-start.16 = (f32[8,2048]{1,0:T(8,128)S(1)}, f32[8,2048]{1,0:T(8,128)S(1)}, u32[]{:S(2)}, u32[]{:S(2)}) collective-permute-start(f32[8,2048]{1,0:T(8,128)S(1)} %add.27), channel_id=1, source_target_pairs={{0,4},{1,5},{2,6},{3,7},{4,0},{5,1},{6,2},{7,3},{8,12},{9,13},{10,... | collective-permute-start | bytes 196616 | tf_op jit(solution)/shard_map/ppermute | solution.py:448
  297.5 1.3 collective-permute-start.17
  298.8 5.8 %collective-permute-start.18 = (f32[8,2048]{1,0:T(8,128)S(1)}, f32[8,2048]{1,0:T(8,128)S(1)}, u32[]{:S(2)}, u32[]{:S(2)}) collective-permute-start(f32[8,2048]{1,0:T(8,128)S(1)} %add.29), channel_id=1, source_target_pairs={{0,2},{1,3},{2,0},{3,1},{4,6},{5,7},{6,4},{7,5},{8,10},{9,11},{10,... | collective-permute-start | bytes 196616 | tf_op jit(solution)/shard_map/ppermute | solution.py:448
  304.7 4.3 %collective-permute-start.19 = (f32[8,2048]{1,0:T(8,128)S(1)}, f32[8,2048]{1,0:T(8,128)S(1)}, u32[]{:S(2)}, u32[]{:S(2)}) collective-permute-start(f32[8,2048]{1,0:T(8,128)S(1)} %add.30), channel_id=1, source_target_pairs={{0,1},{1,0},{2,3},{3,2},{4,5},{5,4},{6,7},{7,6},{8,9},{9,8},{10,11... | collective-permute-start | bytes 196616 | tf_op jit(solution)/shard_map/ppermute | solution.py:448
  309.6 1.0 copy-start.3
  309.6 1.3 copy-start.4

commit v4 on v3

--- a/solution.py
+++ b/solution.py
@@ -20,7 +20,7 @@
     return high, low
 
 
-def pack_kernel(owner_ref, ids_ref, x_ref, out0_ref, out1_ref, tail_ref):
+def pack_kernel(owner_ref, ids_ref, blocks_ref, out0_ref, out1_ref, tail_ref, x_ref, sem):
     subs = x_ref.shape[0]
     devs = out0_ref.shape[0] // ROWS
     sub = lax.broadcasted_iota(jnp.int32, (devs, subs), 0)
@@ -39,12 +39,28 @@
     pick = jnp.concatenate([pick, pick], axis=1)
     lane = lax.broadcasted_iota(jnp.int32, (subs, 128), 1)
 
-    def flat(start):
+    part = 12 * NB
+    upper = HALF * NB
+    copies = []
+    for q in range(8):
+        begin = (3 - q // 2) * part + (q % 2) * upper
+        there = pl.ds(begin, part)
+        copies.append(pltpu.make_async_copy(blocks_ref.at[:, there], x_ref.at[:, there], sem.at[q]))
+        copies[-1].start()
+    waited = [0]
+
+    def arrive(i):
+        needed = 2 * (4 - i // 12)
+        while waited[0] < needed:
+            copies[waited[0]].wait()
+            waited[0] += 1
+
+    def flat(start, need):
         tile, off = divmod(start, 128)
         if off == 0:
             return x_ref[:, tile * 128 : tile * 128 + 128]
         one = pltpu.roll(x_ref[:, tile * 128 : tile * 128 + 128], 128 - off, 1)
-        if (tile + 1) * 128 >= x_ref.shape[1]:
+        if off + need <= 128:
             return one
         two = pltpu.roll(x_ref[:, tile * 128 + 128 : tile * 128 + 256], 128 - off, 1)
         return jnp.where(lane < 128 - off, one, two)
@@ -52,20 +68,22 @@
     diag = jnp.zeros((subs, 128), jnp.float32)
 
     def wrow(i, diag):
-        top = flat(NB * i)
-        bottom = flat(NB * (i + HALF) + HALF)
+        arrive(i)
+        top = flat(NB * i, NB)
+        bottom = flat(NB * (i + HALF) + HALF, HALF)
         row = jnp.where(lane < i, bottom, jnp.where(lane == i, 0.5 * top, top))
         return row, jnp.where(lane == i, 0.5 * bottom, diag)
 
     for m in range(8):
         row, diag = wrow(ROWS + m, diag)
         tail_ref[m] = row
-    order = [i for i in range(0, ROWS, 2) if i not in (26, 28)] + [26, 28]
+    order = [i for i in range(ROWS - 2, -2, -2) if i not in (26, 28)] + [26, 28]
     kept = {}
-    for i in (26, 27, 28, 29):
-        kept[i], diag = wrow(i, diag)
     for i0 in order:
         tiles = []
+        if i0 == 26:
+            for i in (26, 27, 28, 29):
+                kept[i], diag = wrow(i, diag)
         for i in (i0, i0 + 1):
             if i in kept:
                 row = kept[i]
@@ -95,7 +113,16 @@
     return pl.pallas_call(
         pack_kernel,
         out_shape=(shape, shape),
-        scratch_shapes=[pltpu.VMEM((8, blocks.shape[0], 128), jnp.float32)],
+        in_specs=[
+            pl.BlockSpec(memory_space=pltpu.VMEM),
+            pl.BlockSpec(memory_space=pltpu.VMEM),
+            pl.BlockSpec(memory_space=pl.ANY),
+        ],
+        scratch_shapes=[
+            pltpu.VMEM((8, blocks.shape[0], 128), jnp.float32),
+            pltpu.VMEM(blocks.shape, jnp.float32),
+            pltpu.SemaphoreType.DMA((8,)),
+        ],
         name="pack",
     )(owner_map.reshape(1, -1), ids, blocks)
 
@@ -301,7 +328,7 @@
 
 
 def at_row(k, value):
-    row = lax.broadcasted_iota(jnp.int32, (8, value.shape[1]), 0)
+    row = lax.broadcasted_iota(jnp.int32, (4, value.shape[1]), 0)
     return jnp.where(row == k, value, 0.0)
 
 
@@ -326,7 +353,7 @@
         "whole": (rows, total),
         "left": (rows, total // 2),
         "right": (rows, total // 2),
-        "sums": (8, total),
+        "sums": (4, total),
     }
 
     def spec(kind, height):
@@ -342,7 +369,7 @@
     return pl.pallas_call(
         run,
         grid=(2 * per,),
-        in_specs=[pl.BlockSpec(x.shape, lambda j: (0, 0)) for x in matrices]
+        in_specs=[pl.BlockSpec((rows, rows), lambda j: (0, 0)) for x in matrices]
         + [spec(kind, x.shape[0]) for kind, x in ins],
         out_specs=tuple(spec(kind, shapes[kind][0]) for kind in outs),
         out_shape=tuple(jax.ShapeDtypeStruct(shapes[kind], jnp.float32) for kind in outs),
@@ -382,12 +409,12 @@
     m_ref[...] = m_in[...] + at_row(0, sums_of(v0[...], w)) + at_row(1, sums_of(v1[...], w))
 
 
-def second_kernel(step, per, mats, three, x_low, x_high, w1, m_in, v_ref, left_ref, right_ref, m_ref):
+def second_kernel(step, per, mats, three, x_low, x_high, w1, v_ref, left_ref, right_ref, m_ref):
     keep(step, mats, three)
     v = dot3(three[0], right3(x_low[...])) + dot3(three[1], right3(x_high[...]))
     w = dot3(three[2], right3(v))
     v_ref[...] = v
-    m_ref[...] = m_in[...] + at_row(3, sums_of(v, w1[...])) + at_row(4, sums_of(v, w))
+    m_ref[...] = at_row(0, sums_of(v, w1[...])) + at_row(1, sums_of(v, w))
 
     @pl.when(step < per)
     def _():
@@ -405,7 +432,7 @@
     w = jnp.where(left, w_left[...], w_right[...])
     t = dot3(three[jnp.where(left, 1, 0)], right3(x))
     t_ref[...] = t
-    m_ref[...] = m_in[...] + at_row(5, 2.0 * sums_of(t, w))
+    m_ref[...] = m_in[...] + at_row(2, 2.0 * sums_of(t, w))
 
 
 def safe(num, den):
@@ -431,20 +458,20 @@
 
 
 def finish_kernel(
-    step, per, mats, three, v0, w0, v1, w1, v2, t, w_left, x_low, w_right, x_high, sums, sol, res
+    step, per, mats, three, v0, w0, v1, w1, v2, t, w_left, x_low, w_right, x_high, early, late, sol, res
 ):
     keep(step, mats, three)
     left = step < per
     far = jnp.where(left, x_low[...], x_high[...])
     w2 = jnp.where(left, w_left[...], w_right[...])
     v3 = t[...] + dot3(three[jnp.where(left, 0, 1)], right3(far))
-    x, c = coefficients([sums[k : k + 1, :] for k in range(6)])
+    x, c = coefficients([m[k : k + 1, :] for m in (early, late) for k in range(3)])
     sol[...] = x[0] * w0[...] + x[1] * w1[...] + x[2] * w2
     res[...] = c[0] * v0[...] + c[1] * v1[...] + c[2] * v2[...] + c[3] * v3
 
 
-def butterfly(x, devices, bits):
-    for bit in bits:
+def butterfly(x, devices):
+    for bit in (64, 32, 8, 4, 16, 2, 1):
         x = x + lax.ppermute(x, AXES, [(i, i ^ bit) for i in range(devices)])
     return x
 
@@ -483,13 +510,12 @@
     part = assemble(base, got0, window)
     center, high_band, lower = assemble(base, got1, window, part)
     lower = from_below(lower)
-    low_band = lower[:, :own]
     inv = invert(center, lower)
     inv_low, inv_high = from_below(inv), from_above(inv)
     v0 = right_side
     v1, w1, sums = in_blocks(
         first_kernel,
-        (low_band, high_band, inv, inv_low, inv_high),
+        (lower, high_band, inv, inv_low, inv_high),
         (r_low[0], r_high[0], r_low[1], r_high[1]),
         (),
         (),
@@ -498,14 +524,15 @@
         3,
     )
     w1_low, w1_high = from_below(w1), from_above(w1)
-    w0, sums = in_blocks(start_kernel, (inv,), (v0, v1), (), (), (sums,), ("whole", "sums"), 1)
+    w0, early = in_blocks(start_kernel, (inv,), (v0, v1), (), (), (sums,), ("whole", "sums"), 1)
+    early = butterfly(early, devices)
     v2, w2_0, w2_1, sums = in_blocks(
         second_kernel,
-        (low_band, high_band, inv),
+        (lower, high_band, inv),
         (w1_low, w1_high, w1),
         (),
         (),
-        (sums,),
+        (),
         ("whole", "left", "right", "sums"),
         3,
     )
@@ -514,18 +541,18 @@
     near_0, near_1, later_0, later_1 = lax.optimization_barrier((near_0, near_1, w2_0, w2_1))
     far_0 = from_below(later_0)
     far_1 = from_above(later_1)
-    bands = (low_band, high_band)
-    t, sums = in_blocks(
+    bands = (lower, high_band)
+    t, late = in_blocks(
         side_kernel, bands, (), (w2_0, near_0), (w2_1, near_1), (sums,), ("whole", "sums"), 2
     )
-    sums = butterfly(sums, devices, (64, 32, 8, 4, 16, 2, 1))
+    late = butterfly(late, devices)
     return in_blocks(
         finish_kernel,
         bands,
         (v0, w0, v1, w1, v2, t),
         (w2_0, far_0),
         (w2_1, far_1),
-        (sums,),
+        (early, late),
         ("whole", "whole"),
         2,
     )

time: 322 us -> 323 us (level)
  starting transfers between devices: 50.9 us -> 61.5 us
  waiting for transfers between devices: 126 us -> 119 us
    ppermute x7 -> x14, waiting for transfers between devices: 26.3 us -> 12.4 us  [butterfly(): x = x + lax.ppermute(x, AXES, [(i, i ^ bit) for i in range(devices)])]
    ppermute x7 -> x14, starting transfers between devices: 10.5 us -> 21.4 us  [butterfly(): x = x + lax.ppermute(x, AXES, [(i, i ^ bit) for i in range(devices)])]
    ppermute x6, waiting for transfers between devices: 59.3 us -> 66.2 us  [from_above(): return lax.ppermute(x, AXES, down)]
  transfers between devices with their start and end apart: 21 -> 28, of which waited for: 14 -> 16; matrix products, arithmetic and copies ran while one was open for 2% -> 1% of each run, Pallas kernels for 16% -> 16%
where the time goes in v4:
time: 323 us
  waiting for transfers between devices  119 us (37%)
  Pallas kernels  85.9 us (27%)
  starting transfers between devices  61.5 us (19%)
  blocking collectives  46.3 us (14%)
  local copies, waits for them, and re-layouts  5.79 us (2%)
    ppermute x6, waiting for transfers between devices, from_above(): return lax.ppermute(x, AXES, down)  66.2 us
    all_to_all x1, blocking collectives, exchange(): lax.all_to_all(send.reshape(devices, ROWS, 128), AXES, split_axis=0, conc...  46.3 us
    ppermute x7, waiting for transfers between devices, from_below(): return lax.ppermute(x, AXES, up)  40.9 us
    pallas_call x5, Pallas kernels, in_blocks(): pl.pallas_call(run, grid=(2 * per,), in_specs=[pl.BlockSpec((rows, rows),...  36 us
    pallas_call x2, Pallas kernels, assemble(): pl.pallas_call(lambda *refs: assemble_kernel(last, *refs), out_shape=out,...  34 us
    ppermute x6, starting transfers between devices, from_above(): return lax.ppermute(x, AXES, down)  26.7 us
    ppermute x14, starting transfers between devices, butterfly(): x = x + lax.ppermute(x, AXES, [(i, i ^ bit) for i in range(devices)])  21.4 us
    ppermute x14, waiting for transfers between devices, butterfly(): x = x + lax.ppermute(x, AXES, [(i, i ^ bit) for i in range(devices)])  12.4 us
  transfers between devices with their start and end apart: 28, of which 16 were waited for; matrix products, arithmetic and copies ran while one was open for 1% of the time, Pallas kernels for 16%

profile of v4, /device:TPU:0, one launch (start us, length us, event | category | flops | bytes accessed | tf_op | source)
XLA Modules:
  0.0 322.7 jit_solution(8940403185758851634)
XLA Ops:
  0.6 8.2 %pack.1 = (f32[5120,128]{1,0:T(8,128)}, f32[5120,128]{1,0:T(8,128)}) custom-call(s32[1,128]{1,0:T(1,128)} %bitcast.11, s32[96,128]{1,0:T(8,128)} %bitcast.10, f32[128,9216]{1,0:T(8,128)} %blocks_ref.1), custom_call_target="tpu_custom_call" | custom-call | tf_op jit(solution)/shard_map/pack/pallas_call | solution.py:113
  8.9 46.3 %all_to_all.10 = f32[128,40,128]{2,1,0:T(8,128)} all-to-all(f32[128,40,128]{2,1,0:T(8,128)} %bitcast.9), channel_id=1, replica_groups=mesh['row'=8,'col'=16] {'row','col'}, dimensions={0} | all-to-all | bytes 5242880 | tf_op jit(solution)/shard_map/all_to_all | solution.py:500
  55.2 5.9 %all-to-all-start = ((f32[128,40,128]{2,1,0:T(8,128)}), f32[128,40,128]{2,1,0:T(8,128)}, u32[]{:S(2)}, u32[]{:S(2)}) async-start(f32[128,40,128]{2,1,0:T(8,128)} %bitcast.8), calls=%async_computation | async-start | bytes 5242880 | tf_op jit(solution)/shard_map/all_to_all | solution.py:500
  61.1 1.0 slice.6
  62.1 7.0 %collective-permute-start.4 = (f32[128,2048]{1,0:T(8,128)}, f32[128,2048]{1,0:T(8,128)}, u32[]{:S(2)}, u32[]{:S(2)}) collective-permute-start(f32[128,2048]{1,0:T(8,128)} %slice.6), channel_id=1, source_target_pairs={{1,0},{2,1},{3,2},{4,3},{5,4},{6,5},{7,6},{8,7},{9,8},{10,9},{11,1... | collective-permute-start | bytes 3145736 | tf_op jit(solution)/shard_map/ppermute | solution.py:490
  69.1 0.1 slice.7
  69.2 7.2 %collective-permute-start.6 = (f32[128,2048]{1,0:T(8,128)S(1)}, f32[128,2048]{1,0:T(8,128)S(1)}, u32[]{:S(2)}, u32[]{:S(2)}) collective-permute-start(f32[128,2048]{1,0:T(8,128)S(1)} %slice.7), channel_id=1, source_target_pairs={{1,0},{2,1},{3,2},{4,3},{5,4},{6,5},{7,6},{8,7},{9,8},{10,9},{11,1... | collective-permute-start | bytes 3145736 | tf_op jit(solution)/shard_map/ppermute | solution.py:490
  76.4 0.7 pad_add_fusion.refs_0_
  77.1 24.4 %assemble_first.1.refs_2_ = f32[512,512]{1,0:T(8,128)} custom-call(s32[2]{0:T(128)} %pad_add_fusion.refs_0_, f32[5120,128]{1,0:T(8,128)} %bitcast.7), custom_call_target="tpu_custom_call" | custom-call | tf_op jit(solution)/shard_map/assemble_first/pallas_call | solution.py:267
  101.5 0.0 all-to-all-done
  101.5 9.6 %assemble_last.1 = (f32[256,256]{1,0:T(8,128)}, f32[256,256]{1,0:T(8,128)}, f32[256,512]{1,0:T(8,128)}) custom-call(s32[2]{0:T(128)} %pad_add_fusion.refs_0_, f32[5120,128]{1,0:T(8,128)} %bitcast.4.refs_1_, f32[512,512]{1,0:T(8,128)} %assemble_first.1.refs_2_), custom_call_target="tpu_custom_call" | custom-call | tf_op jit(solution)/shard_map/assemble_last/pallas_call | solution.py:267
  111.2 0.1 collective-permute-start
  111.3 32.7 %collective-permute-done.lower_ref.refs_0_ = f32[256,512]{1,0:T(8,128)S(1)} collective-permute-done((f32[256,512]{1,0:T(8,128)}, f32[256,512]{1,0:T(8,128)S(1)}, u32[]{:S(2)}, u32[]{:S(2)}) %collective-permute-start) | collective-permute-done | bytes 524320 | tf_op jit(solution)/shard_map/ppermute | solution.py:487
  144.0 0.8 copy-done.1
  144.8 7.6 %invert.1.refs_2_.refs_0_ = f32[256,256]{1,0:T(8,128)} custom-call(f32[256,256]{1,0:T(8,128)} %get-tuple-element.29.upper_ref, f32[256,512]{1,0:T(8,128)} %copy-done.1), custom_call_target="tpu_custom_call" | custom-call | tf_op jit(solution)/shard_map/invert/pallas_call | solution.py:304
  152.4 8.7 %collective-permute-start.2 = (f32[256,256]{1,0:T(8,128)}, f32[256,256]{1,0:T(8,128)S(1)}, u32[]{:S(2)}, u32[]{:S(2)}) collective-permute-start(f32[256,256]{1,0:T(8,128)} %invert.1.refs_2_.refs_0_), channel_id=1, source_target_pairs={{1,0},{2,1},{3,2},{4,3},{5,4},{6,5},{7,6},{8,7},{9,8},{10,9},{11,1... | collective-permute-start | bytes 786440 | tf_op jit(solution)/shard_map/ppermute | solution.py:490
  161.1 4.2 %collective-permute-done.2.refs_4_ = f32[256,256]{1,0:T(8,128)S(1)} collective-permute-done((f32[256,256]{1,0:T(8,128)}, f32[256,256]{1,0:T(8,128)S(1)}, u32[]{:S(2)}, u32[]{:S(2)}) %collective-permute-start.2) | collective-permute-done | bytes 262176 | tf_op jit(solution)/shard_map/ppermute | solution.py:490
  165.4 7.2 %collective-permute-done.1.refs_3_ = f32[256,256]{1,0:T(8,128)S(1)} collective-permute-done((f32[256,256]{1,0:T(8,128)}, f32[256,256]{1,0:T(8,128)S(1)}, u32[]{:S(2)}, u32[]{:S(2)}) %collective-permute-start.1) | collective-permute-done | bytes 262176 | tf_op jit(solution)/shard_map/ppermute | solution.py:487
  172.6 0.7 copy-done.9
  173.3 0.4 copy-done.7
  173.6 7.7 %shard_map.59 = (f32[256,2048]{1,0:T(8,128)}, f32[256,2048]{1,0:T(8,128)}, f32[4,2048]{1,0:T(4,128)}) custom-call(f32[256,512]{1,0:T(8,128)} %copy-done.1, f32[256,256]{1,0:T(8,128)} %get-tuple-element.28.refs_1_, f32[256,256]{1,0:T(8,128)} %invert.1.refs_2_.refs_0_, f32[256,256]{1,0:T(8,128)} %copy-done.9, f32[256,256]{1,0:T(8,128)} %copy-done.8, ...), custom_call_target="tpu_custom_call" | custom-call | tf_op jit(solution)/shard_map/pallas_call | solution.py:369
  181.3 0.2 collective-permute-start.8
  181.5 1.8 collective-permute-start.7
  183.3 42.3 %collective-permute-done.8.refs_4_ = f32[256,2048]{1,0:T(8,128)S(1)} collective-permute-done((f32[256,2048]{1,0:T(8,128)}, f32[256,2048]{1,0:T(8,128)S(1)}, u32[]{:S(2)}, u32[]{:S(2)}) %collective-permute-start.8) | collective-permute-done | bytes 2097184 | tf_op jit(solution)/shard_map/ppermute | solution.py:490
  225.6 0.8 collective-permute-done.7.refs_3_
  226.5 0.5 copy-done.2
  226.9 8.0 %shard_map.61 = (f32[256,2048]{1,0:T(8,128)}, f32[256,1024]{1,0:T(8,128)}, f32[256,1024]{1,0:T(8,128)}, f32[4,2048]{1,0:T(4,128)}) custom-call(f32[256,512]{1,0:T(8,128)} %copy-done.1, f32[256,256]{1,0:T(8,128)} %get-tuple-element.28.refs_1_, f32[256,256]{1,0:T(8,128)} %invert.1.refs_2_.refs_0_, f32[256,2048]{1,0:T(8,128)} %collective-permute-done.7.refs_3_, ...), custom_call_target="tpu_custom_call" | custom-call | tf_op jit(solution)/shard_map/pallas_call | solution.py:369
  235.0 2.1 collective-permute-start.10
  237.1 19.7 %collective-permute-done.9.refs_3_ = f32[256,1024]{1,0:T(8,128)S(1)} collective-permute-done((f32[256,1024]{1,0:T(8,128)}, f32[256,1024]{1,0:T(8,128)S(1)}, u32[]{:S(2)}, u32[]{:S(2)}) %collective-permute-start.9) | collective-permute-done | bytes 1048608 | tf_op jit(solution)/shard_map/ppermute | solution.py:490
  256.8 0.1 collective-permute-done.10.refs_5_
  256.9 1.0 copy-done.6
  257.9 3.5 %collective-permute-start.11 = (f32[256,1024]{1,0:T(8,128)}, f32[256,1024]{1,0:T(8,128)S(1)}, u32[]{:S(2)}, u32[]{:S(2)}) collective-permute-start(f32[256,1024]{1,0:T(8,128)} %get-tuple-element.42.refs_2_.refs_8_), channel_id=1, source_target_pairs={{0,1},{1,2},{2,3},{3,4},{4,5},{5,6},{6,7},{7,8},{8,9},{9,10},{10,1... | collective-permute-start | bytes 3145736 | tf_op jit(solution)/shard_map/ppermute | solution.py:487
  261.5 3.6 %collective-permute-start.12 = (f32[256,1024]{1,0:T(8,128)}, f32[256,1024]{1,0:T(8,128)S(1)}, u32[]{:S(2)}, u32[]{:S(2)}) collective-permute-start(f32[256,1024]{1,0:T(8,128)} %get-tuple-element.43.refs_4_.refs_10_), channel_id=1, source_target_pairs={{1,0},{2,1},{3,2},{4,3},{5,4},{6,5},{7,6},{8,7},{9,8},{10,9},{11,1... | collective-permute-start | bytes 3145736 | tf_op jit(solution)/shard_map/ppermute | solution.py:490
  265.1 5.3 %shard_map.60 = (f32[256,2048]{1,0:T(8,128)}, f32[4,2048]{1,0:T(4,128)}) custom-call(f32[256,256]{1,0:T(8,128)} %invert.1.refs_2_.refs_0_, f32[256,2048]{1,0:T(8,128)} %refs_2_.1, f32[256,2048]{1,0:T(8,128)} %get-tuple-element.31.refs_2_.refs_4_, f32[4,2048]{1,0:T(4,128)} %get-tuple-element.32.refs_3_), custom_call_target="tpu_custom_call" | custom-call | tf_op jit(solution)/shard_map/pallas_call | solution.py:369
  270.4 3.9 %collective-permute-start.13 = (f32[4,2048]{1,0:T(4,128)}, f32[4,2048]{1,0:T(4,128)S(1)}, u32[]{:S(2)}, u32[]{:S(2)}) collective-permute-start(f32[4,2048]{1,0:T(4,128)} %get-tuple-element.44), channel_id=1, source_target_pairs={{0,64},{1,65},{2,66},{3,67},{4,68},{5,69},{6,70},{7,71},{8,72},{9,... | collective-permute-start | bytes 98312 | tf_op jit(solution)/shard_map/ppermute | solution.py:475
  274.2 5.6 %shard_map.62 = (f32[256,2048]{1,0:T(8,128)}, f32[4,2048]{1,0:T(4,128)}) custom-call(f32[256,512]{1,0:T(8,128)} %copy-done.1, f32[256,256]{1,0:T(8,128)} %get-tuple-element.28.refs_1_, f32[256,1024]{1,0:T(8,128)} %get-tuple-element.42.refs_2_.refs_8_, f32[256,1024]{1,0:T(8,128)} %copy-done.5, f32[256,1024]{1,0:T(8,128)} %get-tuple-element.43.refs_4_.refs_10_, ...), custom_call_target="tpu_custom_call" | custom-call | tf_op jit(solution)/shard_map/pallas_call | solution.py:369
  279.8 0.0 collective-permute-start.20
  279.9 2.7 collective-permute-start.14
  282.6 2.9 collective-permute-done.20
  285.5 0.8 add.53
  286.2 0.1 collective-permute-start.21
  286.4 3.1 collective-permute-start.15
  289.4 0.8 collective-permute-done.21
  290.3 1.8 collective-permute-start.22
  292.1 2.6 collective-permute-start.16
  294.7 1.1 collective-permute-done.22
  295.8 2.8 collective-permute-start.23
  298.6 0.1 collective-permute-start.17
  298.7 1.8 collective-permute-done.23
  300.5 0.2 collective-permute-start.24
  300.7 0.1 collective-permute-start.18
  300.8 0.9 collective-permute-done.24
  301.8 2.7 collective-permute-start.25
  304.5 1.9 collective-permute-done.18
  306.4 0.1 collective-permute-start.19
  306.5 0.8 collective-permute-done.25
  307.3 1.3 collective-permute-start.26
  308.6 1.8 collective-permute-done.19
  310.4 0.6 add.52.refs_12_
  311.0 0.3 collective-permute-done.26
  311.3 0.6 add.59.refs_13_
  311.9 1.0 copy-done.3
  312.9 0.3 copy-done.4
  313.2 9.4 %shard_map.63 = (f32[256,2048]{1,0:T(8,128)}, f32[256,2048]{1,0:T(8,128)}) custom-call(f32[256,512]{1,0:T(8,128)} %copy-done.1, f32[256,256]{1,0:T(8,128)} %get-tuple-element.28.refs_1_, f32[256,2048]{1,0:T(8,128)} %refs_2_.1, f32[256,2048]{1,0:T(8,128)} %get-tuple-element.33.refs_3_, f32[256,2048]{1,0:T(8,128)} %get-tuple-element.31.refs_2_.refs_4_, ...), custom_call_target="tpu_custom_call" | custom-call | tf_op jit(solution)/shard_map/pallas_call | solution.py:369
  (41 shorter events, 0.2 us)
Async XLA Ops:
  55.2 5.9 %copy-start = (f32[256,2048]{1,0:T(8,128)S(1)}, f32[256,2048]{1,0:T(8,128)}, u32[]{:S(2)}) copy-start(f32[256,2048]{1,0:T(8,128)} %refs_2_.1) | copy-start | bytes 6291460
  55.2 46.3 %all-to-all-start = ((f32[128,40,128]{2,1,0:T(8,128)}), f32[128,40,128]{2,1,0:T(8,128)}, u32[]{:S(2)}, u32[]{:S(2)}) async-start(f32[128,40,128]{2,1,0:T(8,128)} %bitcast.8), calls=%async_computation | async-start | bytes 5242880 | tf_op jit(solution)/shard_map/all_to_all | solution.py:500
  62.1 99.0 %collective-permute-start.4 = (f32[128,2048]{1,0:T(8,128)}, f32[128,2048]{1,0:T(8,128)}, u32[]{:S(2)}, u32[]{:S(2)}) collective-permute-start(f32[128,2048]{1,0:T(8,128)} %slice.6), channel_id=1, source_target_pairs={{1,0},{2,1},{3,2},{4,3},{5,4},{6,5},{7,6},{8,7},{9,8},{10,9},{11,1... | collective-permute-start | bytes 3145736 | tf_op jit(solution)/shard_map/ppermute | solution.py:490
  69.1 92.1 %collective-permute-start.3 = (f32[128,2048]{1,0:T(8,128)}, f32[128,2048]{1,0:T(8,128)}, u32[]{:S(2)}, u32[]{:S(2)}) collective-permute-start(f32[128,2048]{1,0:T(8,128)} %slice.6), channel_id=1, source_target_pairs={{0,1},{1,2},{2,3},{3,4},{4,5},{5,6},{6,7},{7,8},{8,9},{9,10},{10,1... | collective-permute-start | bytes 3145736 | tf_op jit(solution)/shard_map/ppermute | solution.py:487
  69.2 103.4 %collective-permute-start.6 = (f32[128,2048]{1,0:T(8,128)S(1)}, f32[128,2048]{1,0:T(8,128)S(1)}, u32[]{:S(2)}, u32[]{:S(2)}) collective-permute-start(f32[128,2048]{1,0:T(8,128)S(1)} %slice.7), channel_id=1, source_target_pairs={{1,0},{2,1},{3,2},{4,3},{5,4},{6,5},{7,6},{8,7},{9,8},{10,9},{11,1... | collective-permute-start | bytes 3145736 | tf_op jit(solution)/shard_map/ppermute | solution.py:490
  76.4 96.2 %collective-permute-start.5 = (f32[128,2048]{1,0:T(8,128)S(1)}, f32[128,2048]{1,0:T(8,128)}, u32[]{:S(2)}, u32[]{:S(2)}) collective-permute-start(f32[128,2048]{1,0:T(8,128)S(1)} %slice.7), channel_id=1, source_target_pairs={{0,1},{1,2},{2,3},{3,4},{4,5},{5,6},{6,7},{7,8},{8,9},{9,10},{10,1... | collective-permute-start | bytes 3145736 | tf_op jit(solution)/shard_map/ppermute | solution.py:487
  111.2 32.8 %collective-permute-start = (f32[256,512]{1,0:T(8,128)}, f32[256,512]{1,0:T(8,128)S(1)}, u32[]{:S(2)}, u32[]{:S(2)}) collective-permute-start(f32[256,512]{1,0:T(8,128)} %get-tuple-element.27), channel_id=1, source_target_pairs={{0,1},{1,2},{2,3},{3,4},{4,5},{5,6},{6,7},{7,8},{8,9},{9,10},{10,1... | collective-permute-start | bytes 1572872 | tf_op jit(solution)/shard_map/ppermute | solution.py:487
  144.0 0.8 copy-start.1
  152.4 13.0 %collective-permute-start.2 = (f32[256,256]{1,0:T(8,128)}, f32[256,256]{1,0:T(8,128)S(1)}, u32[]{:S(2)}, u32[]{:S(2)}) collective-permute-start(f32[256,256]{1,0:T(8,128)} %invert.1.refs_2_.refs_0_), channel_id=1, source_target_pairs={{1,0},{2,1},{3,2},{4,3},{5,4},{6,5},{7,6},{8,7},{9,8},{10,9},{11,1... | collective-permute-start | bytes 786440 | tf_op jit(solution)/shard_map/ppermute | solution.py:490
  161.1 11.4 %collective-permute-start.1 = (f32[256,256]{1,0:T(8,128)}, f32[256,256]{1,0:T(8,128)S(1)}, u32[]{:S(2)}, u32[]{:S(2)}) collective-permute-start(f32[256,256]{1,0:T(8,128)} %invert.1.refs_2_.refs_0_), channel_id=1, source_target_pairs={{0,1},{1,2},{2,3},{3,4},{4,5},{5,6},{6,7},{7,8},{8,9},{9,10},{10,1... | collective-permute-start | bytes 786440 | tf_op jit(solution)/shard_map/ppermute | solution.py:487
  165.4 7.2 %copy-start.8 = (f32[256,256]{1,0:T(8,128)}, f32[256,256]{1,0:T(8,128)S(1)}, u32[]{:S(2)}) copy-start(f32[256,256]{1,0:T(8,128)S(1)} %collective-permute-done.2.refs_4_) | copy-start | bytes 786436
  172.6 0.7 copy-start.9
  172.6 1.1 copy-start.7
  181.3 44.3 %collective-permute-start.8 = (f32[256,2048]{1,0:T(8,128)}, f32[256,2048]{1,0:T(8,128)S(1)}, u32[]{:S(2)}, u32[]{:S(2)}) collective-permute-start(f32[256,2048]{1,0:T(8,128)} %get-tuple-element.34.refs_5_), channel_id=1, source_target_pairs={{1,0},{2,1},{3,2},{4,3},{5,4},{6,5},{7,6},{8,7},{9,8},{10,9},{11,1... | collective-permute-start | bytes 6291464 | tf_op jit(solution)/shard_map/ppermute | solution.py:490
  181.5 45.0 %collective-permute-start.7 = (f32[256,2048]{1,0:T(8,128)}, f32[256,2048]{1,0:T(8,128)}, u32[]{:S(2)}, u32[]{:S(2)}) collective-permute-start(f32[256,2048]{1,0:T(8,128)} %get-tuple-element.34.refs_5_), channel_id=1, source_target_pairs={{0,1},{1,2},{2,3},{3,4},{4,5},{5,6},{6,7},{7,8},{8,9},{9,10},{10,1... | collective-permute-start | bytes 6291464 | tf_op jit(solution)/shard_map/ppermute | solution.py:487
  225.6 1.3 copy-start.2
  235.0 21.8 %collective-permute-start.9 = (f32[256,1024]{1,0:T(8,128)}, f32[256,1024]{1,0:T(8,128)S(1)}, u32[]{:S(2)}, u32[]{:S(2)}) collective-permute-start(f32[256,1024]{1,0:T(8,128)} %get-tuple-element.42.refs_2_.refs_8_), channel_id=1, source_target_pairs={{1,0},{2,1},{3,2},{4,3},{5,4},{6,5},{7,6},{8,7},{9,8},{10,9},{11,1... | collective-permute-start | bytes 3145736 | tf_op jit(solution)/shard_map/ppermute | solution.py:490
  235.0 21.9 %collective-permute-start.10 = (f32[256,1024]{1,0:T(8,128)}, f32[256,1024]{1,0:T(8,128)S(1)}, u32[]{:S(2)}, u32[]{:S(2)}) collective-permute-start(f32[256,1024]{1,0:T(8,128)} %get-tuple-element.43.refs_4_.refs_10_), channel_id=1, source_target_pairs={{0,1},{1,2},{2,3},{3,4},{4,5},{5,6},{6,7},{7,8},{8,9},{9,10},{10,1... | collective-permute-start | bytes 3145736 | tf_op jit(solution)/shard_map/ppermute | solution.py:487
  256.8 13.6 %copy-start.5 = (f32[256,1024]{1,0:T(8,128)}, f32[256,1024]{1,0:T(8,128)S(1)}, u32[]{:S(2)}) copy-start(f32[256,1024]{1,0:T(8,128)S(1)} %collective-permute-done.9.refs_3_) | copy-start | bytes 3145732
  256.9 1.0 copy-start.6
  257.9 54.0 %collective-permute-start.11 = (f32[256,1024]{1,0:T(8,128)}, f32[256,1024]{1,0:T(8,128)S(1)}, u32[]{:S(2)}, u32[]{:S(2)}) collective-permute-start(f32[256,1024]{1,0:T(8,128)} %get-tuple-element.42.refs_2_.refs_8_), channel_id=1, source_target_pairs={{0,1},{1,2},{2,3},{3,4},{4,5},{5,6},{6,7},{7,8},{8,9},{9,10},{10,1... | collective-permute-start | bytes 3145736 | tf_op jit(solution)/shard_map/ppermute | solution.py:487
  261.5 50.5 %collective-permute-start.12 = (f32[256,1024]{1,0:T(8,128)}, f32[256,1024]{1,0:T(8,128)S(1)}, u32[]{:S(2)}, u32[]{:S(2)}) collective-permute-start(f32[256,1024]{1,0:T(8,128)} %get-tuple-element.43.refs_4_.refs_10_), channel_id=1, source_target_pairs={{1,0},{2,1},{3,2},{4,3},{5,4},{6,5},{7,6},{8,7},{9,8},{10,9},{11,1... | collective-permute-start | bytes 3145736 | tf_op jit(solution)/shard_map/ppermute | solution.py:490
  270.4 9.5 %collective-permute-start.13 = (f32[4,2048]{1,0:T(4,128)}, f32[4,2048]{1,0:T(4,128)S(1)}, u32[]{:S(2)}, u32[]{:S(2)}) collective-permute-start(f32[4,2048]{1,0:T(4,128)} %get-tuple-element.44), channel_id=1, source_target_pairs={{0,64},{1,65},{2,66},{3,67},{4,68},{5,69},{6,70},{7,71},{8,72},{9,... | collective-permute-start | bytes 98312 | tf_op jit(solution)/shard_map/ppermute | solution.py:475
  274.2 5.7 %copy-start.10 = (f32[4,2048]{1,0:T(4,128)S(1)}, f32[4,2048]{1,0:T(4,128)}, u32[]{:S(2)}) copy-start(f32[4,2048]{1,0:T(4,128)} %get-tuple-element.44) | copy-start | bytes 98308
  279.8 5.6 %collective-permute-start.20 = (f32[4,2048]{1,0:T(4,128)}, f32[4,2048]{1,0:T(4,128)S(1)}, u32[]{:S(2)}, u32[]{:S(2)}) collective-permute-start(f32[4,2048]{1,0:T(4,128)} %get-tuple-element.45), channel_id=1, source_target_pairs={{0,64},{1,65},{2,66},{3,67},{4,68},{5,69},{6,70},{7,71},{8,72},{9,... | collective-permute-start | bytes 98312 | tf_op jit(solution)/shard_map/ppermute | solution.py:475
  279.9 6.4 %collective-permute-start.14 = (f32[4,2048]{1,0:T(4,128)S(1)}, f32[4,2048]{1,0:T(4,128)S(1)}, u32[]{:S(2)}, u32[]{:S(2)}) collective-permute-start(f32[4,2048]{1,0:T(4,128)S(1)} %add.46), channel_id=1, source_target_pairs={{0,32},{1,33},{2,34},{3,35},{4,36},{5,37},{6,38},{7,39},{8,40},{9,... | collective-permute-start | bytes 98312 | tf_op jit(solution)/shard_map/ppermute | solution.py:475
  286.2 4.0 %collective-permute-start.21 = (f32[4,2048]{1,0:T(4,128)S(1)}, f32[4,2048]{1,0:T(4,128)S(1)}, u32[]{:S(2)}, u32[]{:S(2)}) collective-permute-start(f32[4,2048]{1,0:T(4,128)S(1)} %add.53), channel_id=1, source_target_pairs={{0,32},{1,33},{2,34},{3,35},{4,36},{5,37},{6,38},{7,39},{8,40},{9,... | collective-permute-start | bytes 98312 | tf_op jit(solution)/shard_map/ppermute | solution.py:475
  286.4 5.7 %collective-permute-start.15 = (f32[4,2048]{1,0:T(4,128)S(1)}, f32[4,2048]{1,0:T(4,128)S(1)}, u32[]{:S(2)}, u32[]{:S(2)}) collective-permute-start(f32[4,2048]{1,0:T(4,128)S(1)} %add.47), channel_id=1, source_target_pairs={{0,8},{1,9},{2,10},{3,11},{4,12},{5,13},{6,14},{7,15},{8,0},{9,1},... | collective-permute-start | bytes 98312 | tf_op jit(solution)/shard_map/ppermute | solution.py:475
  290.3 5.5 %collective-permute-start.22 = (f32[4,2048]{1,0:T(4,128)S(1)}, f32[4,2048]{1,0:T(4,128)S(1)}, u32[]{:S(2)}, u32[]{:S(2)}) collective-permute-start(f32[4,2048]{1,0:T(4,128)S(1)} %add.54), channel_id=1, source_target_pairs={{0,8},{1,9},{2,10},{3,11},{4,12},{5,13},{6,14},{7,15},{8,0},{9,1},... | collective-permute-start | bytes 98312 | tf_op jit(solution)/shard_map/ppermute | solution.py:475
  292.1 6.5 %collective-permute-start.16 = (f32[4,2048]{1,0:T(4,128)S(1)}, f32[4,2048]{1,0:T(4,128)S(1)}, u32[]{:S(2)}, u32[]{:S(2)}) collective-permute-start(f32[4,2048]{1,0:T(4,128)S(1)} %add.48), channel_id=1, source_target_pairs={{0,4},{1,5},{2,6},{3,7},{4,0},{5,1},{6,2},{7,3},{8,12},{9,13},{10,... | collective-permute-start | bytes 98312 | tf_op jit(solution)/shard_map/ppermute | solution.py:475
  295.8 4.7 %collective-permute-start.23 = (f32[4,2048]{1,0:T(4,128)S(1)}, f32[4,2048]{1,0:T(4,128)S(1)}, u32[]{:S(2)}, u32[]{:S(2)}) collective-permute-start(f32[4,2048]{1,0:T(4,128)S(1)} %add.55), channel_id=1, source_target_pairs={{0,4},{1,5},{2,6},{3,7},{4,0},{5,1},{6,2},{7,3},{8,12},{9,13},{10,... | collective-permute-start | bytes 98312 | tf_op jit(solution)/shard_map/ppermute | solution.py:475
  298.6 2.1 collective-permute-start.17
  300.5 1.3 collective-permute-start.24
  300.7 5.6 %collective-permute-start.18 = (f32[4,2048]{1,0:T(4,128)S(1)}, f32[4,2048]{1,0:T(4,128)S(1)}, u32[]{:S(2)}, u32[]{:S(2)}) collective-permute-start(f32[4,2048]{1,0:T(4,128)S(1)} %add.50), channel_id=1, source_target_pairs={{0,2},{1,3},{2,0},{3,1},{4,6},{5,7},{6,4},{7,5},{8,10},{9,11},{10,... | collective-permute-start | bytes 98312 | tf_op jit(solution)/shard_map/ppermute | solution.py:475
  301.8 5.5 %collective-permute-start.25 = (f32[4,2048]{1,0:T(4,128)S(1)}, f32[4,2048]{1,0:T(4,128)S(1)}, u32[]{:S(2)}, u32[]{:S(2)}) collective-permute-start(f32[4,2048]{1,0:T(4,128)S(1)} %add.57), channel_id=1, source_target_pairs={{0,2},{1,3},{2,0},{3,1},{4,6},{5,7},{6,4},{7,5},{8,10},{9,11},{10,... | collective-permute-start | bytes 98312 | tf_op jit(solution)/shard_map/ppermute | solution.py:475
  306.4 4.0 %collective-permute-start.19 = (f32[4,2048]{1,0:T(4,128)S(1)}, f32[4,2048]{1,0:T(4,128)S(1)}, u32[]{:S(2)}, u32[]{:S(2)}) collective-permute-start(f32[4,2048]{1,0:T(4,128)S(1)} %add.51), channel_id=1, source_target_pairs={{0,1},{1,0},{2,3},{3,2},{4,5},{5,4},{6,7},{7,6},{8,9},{9,8},{10,11... | collective-permute-start | bytes 98312 | tf_op jit(solution)/shard_map/ppermute | solution.py:475
  307.3 4.0 %collective-permute-start.26 = (f32[4,2048]{1,0:T(4,128)S(1)}, f32[4,2048]{1,0:T(4,128)S(1)}, u32[]{:S(2)}, u32[]{:S(2)}) collective-permute-start(f32[4,2048]{1,0:T(4,128)S(1)} %add.58), channel_id=1, source_target_pairs={{0,1},{1,0},{2,3},{3,2},{4,5},{5,4},{6,7},{7,6},{8,9},{9,8},{10,11... | collective-permute-start | bytes 98312 | tf_op jit(solution)/shard_map/ppermute | solution.py:475
  311.9 1.0 copy-start.3
  311.9 1.3 copy-start.4

commit v5 on v4

--- a/solution.py
+++ b/solution.py
@@ -328,7 +328,7 @@
 
 
 def at_row(k, value):
-    row = lax.broadcasted_iota(jnp.int32, (4, value.shape[1]), 0)
+    row = lax.broadcasted_iota(jnp.int32, (8, value.shape[1]), 0)
     return jnp.where(row == k, value, 0.0)
 
 
@@ -353,7 +353,7 @@
         "whole": (rows, total),
         "left": (rows, total // 2),
         "right": (rows, total // 2),
-        "sums": (4, total),
+        "sums": (8, total),
     }
 
     def spec(kind, height):
@@ -409,12 +409,14 @@
     m_ref[...] = m_in[...] + at_row(0, sums_of(v0[...], w)) + at_row(1, sums_of(v1[...], w))
 
 
-def second_kernel(step, per, mats, three, x_low, x_high, w1, v_ref, left_ref, right_ref, m_ref):
+def second_kernel(
+    step, per, mats, three, x_low, x_high, w1, m_in, v_ref, left_ref, right_ref, m_ref
+):
     keep(step, mats, three)
     v = dot3(three[0], right3(x_low[...])) + dot3(three[1], right3(x_high[...]))
     w = dot3(three[2], right3(v))
     v_ref[...] = v
-    m_ref[...] = at_row(0, sums_of(v, w1[...])) + at_row(1, sums_of(v, w))
+    m_ref[...] = m_in[...] + at_row(3, sums_of(v, w1[...])) + at_row(4, sums_of(v, w))
 
     @pl.when(step < per)
     def _():
@@ -432,7 +434,7 @@
     w = jnp.where(left, w_left[...], w_right[...])
     t = dot3(three[jnp.where(left, 1, 0)], right3(x))
     t_ref[...] = t
-    m_ref[...] = m_in[...] + at_row(2, 2.0 * sums_of(t, w))
+    m_ref[...] = m_in[...] + at_row(5, 2.0 * sums_of(t, w))
 
 
 def safe(num, den):
@@ -458,20 +460,20 @@
 
 
 def finish_kernel(
-    step, per, mats, three, v0, w0, v1, w1, v2, t, w_left, x_low, w_right, x_high, early, late, sol, res
+    step, per, mats, three, v0, w0, v1, w1, v2, t, w_left, x_low, w_right, x_high, sums, sol, res
 ):
     keep(step, mats, three)
     left = step < per
     far = jnp.where(left, x_low[...], x_high[...])
     w2 = jnp.where(left, w_left[...], w_right[...])
     v3 = t[...] + dot3(three[jnp.where(left, 0, 1)], right3(far))
-    x, c = coefficients([m[k : k + 1, :] for m in (early, late) for k in range(3)])
+    x, c = coefficients([sums[k : k + 1, :] for k in range(6)])
     sol[...] = x[0] * w0[...] + x[1] * w1[...] + x[2] * w2
     res[...] = c[0] * v0[...] + c[1] * v1[...] + c[2] * v2[...] + c[3] * v3
 
 
 def butterfly(x, devices):
-    for bit in (64, 32, 8, 4, 16, 2, 1):
+    for bit in (16, 64, 32, 8, 4, 2, 1):
         x = x + lax.ppermute(x, AXES, [(i, i ^ bit) for i in range(devices)])
     return x
 
@@ -524,35 +526,33 @@
         3,
     )
     w1_low, w1_high = from_below(w1), from_above(w1)
-    w0, early = in_blocks(start_kernel, (inv,), (v0, v1), (), (), (sums,), ("whole", "sums"), 1)
-    early = butterfly(early, devices)
+    w0, sums = in_blocks(start_kernel, (inv,), (v0, v1), (), (), (sums,), ("whole", "sums"), 1)
     v2, w2_0, w2_1, sums = in_blocks(
         second_kernel,
         (lower, high_band, inv),
         (w1_low, w1_high, w1),
         (),
         (),
-        (),
+        (sums,),
         ("whole", "left", "right", "sums"),
         3,
     )
     near_0 = from_above(w2_0)
     near_1 = from_below(w2_1)
-    near_0, near_1, later_0, later_1 = lax.optimization_barrier((near_0, near_1, w2_0, w2_1))
-    far_0 = from_below(later_0)
-    far_1 = from_above(later_1)
+    far_0 = from_below(w2_0)
+    far_1 = from_above(w2_1)
     bands = (lower, high_band)
-    t, late = in_blocks(
+    t, sums = in_blocks(
         side_kernel, bands, (), (w2_0, near_0), (w2_1, near_1), (sums,), ("whole", "sums"), 2
     )
-    late = butterfly(late, devices)
+    sums = butterfly(sums, devices)
     return in_blocks(
         finish_kernel,
         bands,
         (v0, w0, v1, w1, v2, t),
         (w2_0, far_0),
         (w2_1, far_1),
-        (early, late),
+        (sums,),
         ("whole", "whole"),
         2,
     )

time: 323 us -> 328 us (1.015)
  waiting for transfers between devices: 119 us -> 124 us
    ppermute x14 -> x7, waiting for transfers between devices: 12.4 us -> 28.8 us  [butterfly(): x = x + lax.ppermute(x, AXES, [(i, i ^ bit) for i in range(devices)])]
    ppermute x6, waiting for transfers between devices: 66.2 us -> 53.9 us  [from_above(): return lax.ppermute(x, AXES, down)]
    ppermute x14 -> x7, starting transfers between devices: 21.4 us -> 22.5 us  [butterfly(): x = x + lax.ppermute(x, AXES, [(i, i ^ bit) for i in range(devices)])]
  transfers between devices with their start and end apart: 28 -> 21, of which waited for: 16 -> 14; matrix products, arithmetic and copies ran while one was open for 1% -> 1% of each run, Pallas kernels for 16% -> 16%
where the time goes in v5:
time: 328 us; the launch traced here: 327 us
  waiting for transfers between devices  124 us (38%)
  Pallas kernels  85.7 us (26%)
  starting transfers between devices  62.8 us (19%)
  blocking collectives  46.3 us (14%)
  local copies, waits for them, and re-layouts  5.66 us (2%)
    ppermute x6, waiting for transfers between devices, from_above(): return lax.ppermute(x, AXES, down)  53.9 us
    all_to_all x1, blocking collectives, exchange(): lax.all_to_all(send.reshape(devices, ROWS, 128), AXES, split_axis=0, conc...  46.3 us
    ppermute x7, waiting for transfers between devices, from_below(): return lax.ppermute(x, AXES, up)  41 us
    pallas_call x5, Pallas kernels, in_blocks(): pl.pallas_call(run, grid=(2 * per,), in_specs=[pl.BlockSpec((rows, rows),...  35.8 us
    pallas_call x2, Pallas kernels, assemble(): pl.pallas_call(lambda *refs: assemble_kernel(last, *refs), out_shape=out,...  34 us
    ppermute x7, waiting for transfers between devices, butterfly(): x = x + lax.ppermute(x, AXES, [(i, i ^ bit) for i in range(devices)])  28.8 us
    ppermute x6, starting transfers between devices, from_above(): return lax.ppermute(x, AXES, down)  28.4 us
    ppermute x7, starting transfers between devices, butterfly(): x = x + lax.ppermute(x, AXES, [(i, i ^ bit) for i in range(devices)])  22.5 us
  transfers between devices with their start and end apart: 21, of which 14 were waited for; matrix products, arithmetic and copies ran while one was open for 1% of the time, Pallas kernels for 16%

profile of v5, /device:TPU:0, one launch (start us, length us, event | category | flops | bytes accessed | tf_op | source)
XLA Modules:
  0.0 327.2 jit_solution(16624959428066611824)
XLA Ops:
  0.6 8.2 %pack.1 = (f32[5120,128]{1,0:T(8,128)}, f32[5120,128]{1,0:T(8,128)}) custom-call(s32[1,128]{1,0:T(1,128)} %bitcast.11, s32[96,128]{1,0:T(8,128)} %bitcast.10, f32[128,9216]{1,0:T(8,128)} %blocks_ref.1), custom_call_target="tpu_custom_call" | custom-call | tf_op jit(solution)/shard_map/pack/pallas_call | solution.py:113
  8.9 46.3 %all_to_all.10 = f32[128,40,128]{2,1,0:T(8,128)} all-to-all(f32[128,40,128]{2,1,0:T(8,128)} %bitcast.9), channel_id=1, replica_groups=mesh['row'=8,'col'=16] {'row','col'}, dimensions={0} | all-to-all | bytes 5242880 | tf_op jit(solution)/shard_map/all_to_all | solution.py:502
  55.2 5.9 %all-to-all-start = ((f32[128,40,128]{2,1,0:T(8,128)}), f32[128,40,128]{2,1,0:T(8,128)}, u32[]{:S(2)}, u32[]{:S(2)}) async-start(f32[128,40,128]{2,1,0:T(8,128)} %bitcast.8), calls=%async_computation | async-start | bytes 5242880 | tf_op jit(solution)/shard_map/all_to_all | solution.py:502
  61.1 1.0 slice.6
  62.1 7.0 %collective-permute-start.4 = (f32[128,2048]{1,0:T(8,128)}, f32[128,2048]{1,0:T(8,128)}, u32[]{:S(2)}, u32[]{:S(2)}) collective-permute-start(f32[128,2048]{1,0:T(8,128)} %slice.6), channel_id=1, source_target_pairs={{1,0},{2,1},{3,2},{4,3},{5,4},{6,5},{7,6},{8,7},{9,8},{10,9},{11,1... | collective-permute-start | bytes 3145736 | tf_op jit(solution)/shard_map/ppermute | solution.py:492
  69.1 0.0 collective-permute-start.3
  69.1 0.1 slice.7
  69.2 7.2 %collective-permute-start.6 = (f32[128,2048]{1,0:T(8,128)S(1)}, f32[128,2048]{1,0:T(8,128)S(1)}, u32[]{:S(2)}, u32[]{:S(2)}) collective-permute-start(f32[128,2048]{1,0:T(8,128)S(1)} %slice.7), channel_id=1, source_target_pairs={{1,0},{2,1},{3,2},{4,3},{5,4},{6,5},{7,6},{8,7},{9,8},{10,9},{11,1... | collective-permute-start | bytes 3145736 | tf_op jit(solution)/shard_map/ppermute | solution.py:492
  76.4 0.0 collective-permute-start.5
  76.4 0.6 pad_add_fusion.refs_0_
  77.0 24.4 %assemble_first.1.refs_2_ = f32[512,512]{1,0:T(8,128)} custom-call(s32[2]{0:T(128)} %pad_add_fusion.refs_0_, f32[5120,128]{1,0:T(8,128)} %bitcast.7), custom_call_target="tpu_custom_call" | custom-call | tf_op jit(solution)/shard_map/assemble_first/pallas_call | solution.py:267
  101.4 0.0 all-to-all-done
  101.4 9.6 %assemble_last.1 = (f32[256,256]{1,0:T(8,128)}, f32[256,256]{1,0:T(8,128)}, f32[256,512]{1,0:T(8,128)}) custom-call(s32[2]{0:T(128)} %pad_add_fusion.refs_0_, f32[5120,128]{1,0:T(8,128)} %bitcast.4.refs_1_, f32[512,512]{1,0:T(8,128)} %assemble_first.1.refs_2_), custom_call_target="tpu_custom_call" | custom-call | tf_op jit(solution)/shard_map/assemble_last/pallas_call | solution.py:267
  111.0 0.1 collective-permute-start
  111.1 32.9 %collective-permute-done.lower_ref.refs_0_ = f32[256,512]{1,0:T(8,128)S(1)} collective-permute-done((f32[256,512]{1,0:T(8,128)}, f32[256,512]{1,0:T(8,128)S(1)}, u32[]{:S(2)}, u32[]{:S(2)}) %collective-permute-start) | collective-permute-done | bytes 524320 | tf_op jit(solution)/shard_map/ppermute | solution.py:489
  144.0 0.8 copy-done.1
  144.8 7.6 %invert.1.refs_2_.refs_0_ = f32[256,256]{1,0:T(8,128)} custom-call(f32[256,256]{1,0:T(8,128)} %get-tuple-element.25.upper_ref, f32[256,512]{1,0:T(8,128)} %copy-done.1), custom_call_target="tpu_custom_call" | custom-call | tf_op jit(solution)/shard_map/invert/pallas_call | solution.py:304
  152.5 8.7 %collective-permute-start.2 = (f32[256,256]{1,0:T(8,128)}, f32[256,256]{1,0:T(8,128)S(1)}, u32[]{:S(2)}, u32[]{:S(2)}) collective-permute-start(f32[256,256]{1,0:T(8,128)} %invert.1.refs_2_.refs_0_), channel_id=1, source_target_pairs={{1,0},{2,1},{3,2},{4,3},{5,4},{6,5},{7,6},{8,7},{9,8},{10,9},{11,1... | collective-permute-start | bytes 786440 | tf_op jit(solution)/shard_map/ppermute | solution.py:492
  161.2 0.0 collective-permute-done.4.refs_6_
  161.2 0.0 collective-permute-start.1
  161.2 0.0 collective-permute-done.3.refs_5_
  161.2 4.2 %collective-permute-done.2.refs_4_ = f32[256,256]{1,0:T(8,128)S(1)} collective-permute-done((f32[256,256]{1,0:T(8,128)}, f32[256,256]{1,0:T(8,128)S(1)}, u32[]{:S(2)}, u32[]{:S(2)}) %collective-permute-start.2) | collective-permute-done | bytes 262176 | tf_op jit(solution)/shard_map/ppermute | solution.py:492
  165.4 7.2 %collective-permute-done.1.refs_3_ = f32[256,256]{1,0:T(8,128)S(1)} collective-permute-done((f32[256,256]{1,0:T(8,128)}, f32[256,256]{1,0:T(8,128)S(1)}, u32[]{:S(2)}, u32[]{:S(2)}) %collective-permute-start.1) | collective-permute-done | bytes 262176 | tf_op jit(solution)/shard_map/ppermute | solution.py:489
  172.6 0.0 collective-permute-done.6.refs_8_
  172.6 0.0 collective-permute-done.5.refs_7_
  172.6 0.7 copy-done.8
  173.3 0.4 copy-done.6
  173.7 7.7 %shard_map.59 = (f32[256,2048]{1,0:T(8,128)}, f32[256,2048]{1,0:T(8,128)}, f32[8,2048]{1,0:T(8,128)}) custom-call(f32[256,512]{1,0:T(8,128)} %copy-done.1, f32[256,256]{1,0:T(8,128)} %get-tuple-element.24.refs_1_, f32[256,256]{1,0:T(8,128)} %invert.1.refs_2_.refs_0_, f32[256,256]{1,0:T(8,128)} %copy-done.8, f32[256,256]{1,0:T(8,128)} %copy-done.7, ...), custom_call_target="tpu_custom_call" | custom-call | tf_op jit(solution)/shard_map/pallas_call | solution.py:369
  181.3 0.2 collective-permute-start.8
  181.5 1.8 collective-permute-start.7
  183.4 5.2 %shard_map.60 = (f32[256,2048]{1,0:T(8,128)}, f32[8,2048]{1,0:T(8,128)}) custom-call(f32[256,256]{1,0:T(8,128)} %invert.1.refs_2_.refs_0_, f32[256,2048]{1,0:T(8,128)} %refs_2_.1, f32[256,2048]{1,0:T(8,128)} %get-tuple-element.27.refs_2_.refs_4_, f32[8,2048]{1,0:T(8,128)} %get-tuple-element.28.refs_3_), custom_call_target="tpu_custom_call" | custom-call | tf_op jit(solution)/shard_map/pallas_call | solution.py:369
  188.5 37.1 %collective-permute-done.8.refs_4_ = f32[256,2048]{1,0:T(8,128)S(1)} collective-permute-done((f32[256,2048]{1,0:T(8,128)}, f32[256,2048]{1,0:T(8,128)S(1)}, u32[]{:S(2)}, u32[]{:S(2)}) %collective-permute-start.8) | collective-permute-done | bytes 2097184 | tf_op jit(solution)/shard_map/ppermute | solution.py:492
  225.7 0.8 collective-permute-done.7.refs_3_
  226.5 0.5 copy-done.2
  227.0 8.0 %shard_map.61 = (f32[256,2048]{1,0:T(8,128)}, f32[256,1024]{1,0:T(8,128)}, f32[256,1024]{1,0:T(8,128)}, f32[8,2048]{1,0:T(8,128)}) custom-call(f32[256,512]{1,0:T(8,128)} %copy-done.1, f32[256,256]{1,0:T(8,128)} %get-tuple-element.24.refs_1_, f32[256,256]{1,0:T(8,128)} %invert.1.refs_2_.refs_0_, f32[256,2048]{1,0:T(8,128)} %collective-permute-done.7.refs_3_, ...), custom_call_target="tpu_custom_call" | custom-call | tf_op jit(solution)/shard_map/pallas_call | solution.py:369
  235.0 0.1 collective-permute-start.9
  235.1 2.1 collective-permute-start.10
  237.2 1.9 collective-permute-start.11
  239.1 5.2 %collective-permute-start.12 = (f32[256,1024]{1,0:T(8,128)}, f32[256,1024]{1,0:T(8,128)S(1)}, u32[]{:S(2)}, u32[]{:S(2)}) collective-permute-start(f32[256,1024]{1,0:T(8,128)} %get-tuple-element.34.refs_4_.refs_10_), channel_id=1, source_target_pairs={{1,0},{2,1},{3,2},{4,3},{5,4},{6,5},{7,6},{8,7},{9,8},{10,9},{11,1... | collective-permute-start | bytes 3145736 | tf_op jit(solution)/shard_map/ppermute | solution.py:492
  244.4 12.5 %collective-permute-done.9.refs_3_ = f32[256,1024]{1,0:T(8,128)S(1)} collective-permute-done((f32[256,1024]{1,0:T(8,128)}, f32[256,1024]{1,0:T(8,128)S(1)}, u32[]{:S(2)}, u32[]{:S(2)}) %collective-permute-start.9) | collective-permute-done | bytes 1048608 | tf_op jit(solution)/shard_map/ppermute | solution.py:492
  256.9 0.1 collective-permute-done.10.refs_5_
  257.0 0.9 copy-done.5
  257.9 5.6 %shard_map.62 = (f32[256,2048]{1,0:T(8,128)}, f32[8,2048]{1,0:T(8,128)}) custom-call(f32[256,512]{1,0:T(8,128)} %copy-done.1, f32[256,256]{1,0:T(8,128)} %get-tuple-element.24.refs_1_, f32[256,1024]{1,0:T(8,128)} %get-tuple-element.33.refs_2_.refs_8_, f32[256,1024]{1,0:T(8,128)} %copy-done.5, f32[256,1024]{1,0:T(8,128)} %get-tuple-element.34.refs_4_.refs_10_, ...), custom_call_target="tpu_custom_call" | custom-call | tf_op jit(solution)/shard_map/pallas_call | solution.py:369
  263.4 19.6 %collective-permute-start.13 = (f32[8,2048]{1,0:T(8,128)}, f32[8,2048]{1,0:T(8,128)S(1)}, u32[]{:S(2)}, u32[]{:S(2)}) collective-permute-start(f32[8,2048]{1,0:T(8,128)} %get-tuple-element.37), channel_id=1, source_target_pairs={{0,16},{1,17},{2,18},{3,19},{4,20},{5,21},{6,22},{7,23},{8,24},{9,... | collective-permute-start | bytes 196616 | tf_op jit(solution)/shard_map/ppermute | solution.py:477
  283.0 1.1 collective-permute-done.13
  284.2 0.9 add.25
  285.0 2.5 collective-permute-start.14
  287.5 3.4 %collective-permute-done.14 = f32[8,2048]{1,0:T(8,128)S(1)} collective-permute-done((f32[8,2048]{1,0:T(8,128)S(1)}, f32[8,2048]{1,0:T(8,128)S(1)}, u32[]{:S(2)}, u32[]{:S(2)}) %collective-permute-start.14) | collective-permute-done | bytes 65568 | tf_op jit(solution)/shard_map/ppermute | solution.py:477
  290.9 0.1 collective-permute-start.15
  291.0 4.3 %collective-permute-done.15 = f32[8,2048]{1,0:T(8,128)S(1)} collective-permute-done((f32[8,2048]{1,0:T(8,128)S(1)}, f32[8,2048]{1,0:T(8,128)S(1)}, u32[]{:S(2)}, u32[]{:S(2)}) %collective-permute-start.15) | collective-permute-done | bytes 65568 | tf_op jit(solution)/shard_map/ppermute | solution.py:477
  295.3 0.1 collective-permute-start.16
  295.4 5.8 %collective-permute-done.16 = f32[8,2048]{1,0:T(8,128)S(1)} collective-permute-done((f32[8,2048]{1,0:T(8,128)S(1)}, f32[8,2048]{1,0:T(8,128)S(1)}, u32[]{:S(2)}, u32[]{:S(2)}) %collective-permute-start.16) | collective-permute-done | bytes 65568 | tf_op jit(solution)/shard_map/ppermute | solution.py:477
  301.2 0.1 collective-permute-start.17
  301.3 4.3 %collective-permute-done.17 = f32[8,2048]{1,0:T(8,128)S(1)} collective-permute-done((f32[8,2048]{1,0:T(8,128)S(1)}, f32[8,2048]{1,0:T(8,128)S(1)}, u32[]{:S(2)}, u32[]{:S(2)}) %collective-permute-start.17) | collective-permute-done | bytes 65568 | tf_op jit(solution)/shard_map/ppermute | solution.py:477
  305.5 0.1 collective-permute-start.18
  305.6 5.8 %collective-permute-done.18 = f32[8,2048]{1,0:T(8,128)S(1)} collective-permute-done((f32[8,2048]{1,0:T(8,128)S(1)}, f32[8,2048]{1,0:T(8,128)S(1)}, u32[]{:S(2)}, u32[]{:S(2)}) %collective-permute-start.18) | collective-permute-done | bytes 65568 | tf_op jit(solution)/shard_map/ppermute | solution.py:477
  311.4 0.1 collective-permute-start.19
  311.5 4.3 %collective-permute-done.19 = f32[8,2048]{1,0:T(8,128)S(1)} collective-permute-done((f32[8,2048]{1,0:T(8,128)S(1)}, f32[8,2048]{1,0:T(8,128)S(1)}, u32[]{:S(2)}, u32[]{:S(2)}) %collective-permute-start.19) | collective-permute-done | bytes 65568 | tf_op jit(solution)/shard_map/ppermute | solution.py:477
  315.7 0.6 add.31.refs_12_
  316.4 0.0 collective-permute-done.11.refs_9_
  316.4 0.0 collective-permute-done.12.refs_11_
  316.4 1.0 copy-done.3
  317.4 0.3 copy-done.4
  317.7 9.3 %shard_map.63 = (f32[256,2048]{1,0:T(8,128)}, f32[256,2048]{1,0:T(8,128)}) custom-call(f32[256,512]{1,0:T(8,128)} %copy-done.1, f32[256,256]{1,0:T(8,128)} %get-tuple-element.24.refs_1_, f32[256,2048]{1,0:T(8,128)} %refs_2_.1, f32[256,2048]{1,0:T(8,128)} %get-tuple-element.29.refs_3_, f32[256,2048]{1,0:T(8,128)} %get-tuple-element.27.refs_2_.refs_4_, ...), custom_call_target="tpu_custom_call" | custom-call | tf_op jit(solution)/shard_map/pallas_call | solution.py:369
  (16 shorter events, 0.1 us)
Async XLA Ops:
  55.2 5.9 %copy-start = (f32[256,2048]{1,0:T(8,128)S(1)}, f32[256,2048]{1,0:T(8,128)}, u32[]{:S(2)}) copy-start(f32[256,2048]{1,0:T(8,128)} %refs_2_.1) | copy-start | bytes 6291460
  55.2 46.2 %all-to-all-start = ((f32[128,40,128]{2,1,0:T(8,128)}), f32[128,40,128]{2,1,0:T(8,128)}, u32[]{:S(2)}, u32[]{:S(2)}) async-start(f32[128,40,128]{2,1,0:T(8,128)} %bitcast.8), calls=%async_computation | async-start | bytes 5242880 | tf_op jit(solution)/shard_map/all_to_all | solution.py:502
  62.1 99.0 %collective-permute-start.4 = (f32[128,2048]{1,0:T(8,128)}, f32[128,2048]{1,0:T(8,128)}, u32[]{:S(2)}, u32[]{:S(2)}) collective-permute-start(f32[128,2048]{1,0:T(8,128)} %slice.6), channel_id=1, source_target_pairs={{1,0},{2,1},{3,2},{4,3},{5,4},{6,5},{7,6},{8,7},{9,8},{10,9},{11,1... | collective-permute-start | bytes 3145736 | tf_op jit(solution)/shard_map/ppermute | solution.py:492
  69.1 92.1 %collective-permute-start.3 = (f32[128,2048]{1,0:T(8,128)}, f32[128,2048]{1,0:T(8,128)}, u32[]{:S(2)}, u32[]{:S(2)}) collective-permute-start(f32[128,2048]{1,0:T(8,128)} %slice.6), channel_id=1, source_target_pairs={{0,1},{1,2},{2,3},{3,4},{4,5},{5,6},{6,7},{7,8},{8,9},{9,10},{10,1... | collective-permute-start | bytes 3145736 | tf_op jit(solution)/shard_map/ppermute | solution.py:489
  69.2 103.4 %collective-permute-start.6 = (f32[128,2048]{1,0:T(8,128)S(1)}, f32[128,2048]{1,0:T(8,128)S(1)}, u32[]{:S(2)}, u32[]{:S(2)}) collective-permute-start(f32[128,2048]{1,0:T(8,128)S(1)} %slice.7), channel_id=1, source_target_pairs={{1,0},{2,1},{3,2},{4,3},{5,4},{6,5},{7,6},{8,7},{9,8},{10,9},{11,1... | collective-permute-start | bytes 3145736 | tf_op jit(solution)/shard_map/ppermute | solution.py:492
  76.4 96.2 %collective-permute-start.5 = (f32[128,2048]{1,0:T(8,128)S(1)}, f32[128,2048]{1,0:T(8,128)}, u32[]{:S(2)}, u32[]{:S(2)}) collective-permute-start(f32[128,2048]{1,0:T(8,128)S(1)} %slice.7), channel_id=1, source_target_pairs={{0,1},{1,2},{2,3},{3,4},{4,5},{5,6},{6,7},{7,8},{8,9},{9,10},{10,1... | collective-permute-start | bytes 3145736 | tf_op jit(solution)/shard_map/ppermute | solution.py:489
  111.0 33.0 %collective-permute-start = (f32[256,512]{1,0:T(8,128)}, f32[256,512]{1,0:T(8,128)S(1)}, u32[]{:S(2)}, u32[]{:S(2)}) collective-permute-start(f32[256,512]{1,0:T(8,128)} %get-tuple-element.23), channel_id=1, source_target_pairs={{0,1},{1,2},{2,3},{3,4},{4,5},{5,6},{6,7},{7,8},{8,9},{9,10},{10,1... | collective-permute-start | bytes 1572872 | tf_op jit(solution)/shard_map/ppermute | solution.py:489
  144.0 0.8 copy-start.1
  152.5 13.0 %collective-permute-start.2 = (f32[256,256]{1,0:T(8,128)}, f32[256,256]{1,0:T(8,128)S(1)}, u32[]{:S(2)}, u32[]{:S(2)}) collective-permute-start(f32[256,256]{1,0:T(8,128)} %invert.1.refs_2_.refs_0_), channel_id=1, source_target_pairs={{1,0},{2,1},{3,2},{4,3},{5,4},{6,5},{7,6},{8,7},{9,8},{10,9},{11,1... | collective-permute-start | bytes 786440 | tf_op jit(solution)/shard_map/ppermute | solution.py:492
  161.2 11.4 %collective-permute-start.1 = (f32[256,256]{1,0:T(8,128)}, f32[256,256]{1,0:T(8,128)S(1)}, u32[]{:S(2)}, u32[]{:S(2)}) collective-permute-start(f32[256,256]{1,0:T(8,128)} %invert.1.refs_2_.refs_0_), channel_id=1, source_target_pairs={{0,1},{1,2},{2,3},{3,4},{4,5},{5,6},{6,7},{7,8},{8,9},{9,10},{10,1... | collective-permute-start | bytes 786440 | tf_op jit(solution)/shard_map/ppermute | solution.py:489
  165.4 7.2 %copy-start.7 = (f32[256,256]{1,0:T(8,128)}, f32[256,256]{1,0:T(8,128)S(1)}, u32[]{:S(2)}) copy-start(f32[256,256]{1,0:T(8,128)S(1)} %collective-permute-done.2.refs_4_) | copy-start | bytes 786436
  172.6 0.7 copy-start.8
  172.6 1.1 copy-start.6
  181.3 44.3 %collective-permute-start.8 = (f32[256,2048]{1,0:T(8,128)}, f32[256,2048]{1,0:T(8,128)S(1)}, u32[]{:S(2)}, u32[]{:S(2)}) collective-permute-start(f32[256,2048]{1,0:T(8,128)} %get-tuple-element.30.refs_5_), channel_id=1, source_target_pairs={{1,0},{2,1},{3,2},{4,3},{5,4},{6,5},{7,6},{8,7},{9,8},{10,9},{11,1... | collective-permute-start | bytes 6291464 | tf_op jit(solution)/shard_map/ppermute | solution.py:492
  181.5 45.0 %collective-permute-start.7 = (f32[256,2048]{1,0:T(8,128)}, f32[256,2048]{1,0:T(8,128)}, u32[]{:S(2)}, u32[]{:S(2)}) collective-permute-start(f32[256,2048]{1,0:T(8,128)} %get-tuple-element.30.refs_5_), channel_id=1, source_target_pairs={{0,1},{1,2},{2,3},{3,4},{4,5},{5,6},{6,7},{7,8},{8,9},{9,10},{10,1... | collective-permute-start | bytes 6291464 | tf_op jit(solution)/shard_map/ppermute | solution.py:489
  225.7 1.3 copy-start.2
  235.0 21.9 %collective-permute-start.9 = (f32[256,1024]{1,0:T(8,128)}, f32[256,1024]{1,0:T(8,128)S(1)}, u32[]{:S(2)}, u32[]{:S(2)}) collective-permute-start(f32[256,1024]{1,0:T(8,128)} %get-tuple-element.33.refs_2_.refs_8_), channel_id=1, source_target_pairs={{1,0},{2,1},{3,2},{4,3},{5,4},{6,5},{7,6},{8,7},{9,8},{10,9},{11,1... | collective-permute-start | bytes 3145736 | tf_op jit(solution)/shard_map/ppermute | solution.py:492
  235.1 21.9 %collective-permute-start.10 = (f32[256,1024]{1,0:T(8,128)}, f32[256,1024]{1,0:T(8,128)}, u32[]{:S(2)}, u32[]{:S(2)}) collective-permute-start(f32[256,1024]{1,0:T(8,128)} %get-tuple-element.34.refs_4_.refs_10_), channel_id=1, source_target_pairs={{0,1},{1,2},{2,3},{3,4},{4,5},{5,6},{6,7},{7,8},{8,9},{9,10},{10,1... | collective-permute-start | bytes 3145736 | tf_op jit(solution)/shard_map/ppermute | solution.py:489
  237.2 79.2 %collective-permute-start.11 = (f32[256,1024]{1,0:T(8,128)}, f32[256,1024]{1,0:T(8,128)S(1)}, u32[]{:S(2)}, u32[]{:S(2)}) collective-permute-start(f32[256,1024]{1,0:T(8,128)} %get-tuple-element.33.refs_2_.refs_8_), channel_id=1, source_target_pairs={{0,1},{1,2},{2,3},{3,4},{4,5},{5,6},{6,7},{7,8},{8,9},{9,10},{10,1... | collective-permute-start | bytes 3145736 | tf_op jit(solution)/shard_map/ppermute | solution.py:489
  239.1 77.2 %collective-permute-start.12 = (f32[256,1024]{1,0:T(8,128)}, f32[256,1024]{1,0:T(8,128)S(1)}, u32[]{:S(2)}, u32[]{:S(2)}) collective-permute-start(f32[256,1024]{1,0:T(8,128)} %get-tuple-element.34.refs_4_.refs_10_), channel_id=1, source_target_pairs={{1,0},{2,1},{3,2},{4,3},{5,4},{6,5},{7,6},{8,7},{9,8},{10,9},{11,1... | collective-permute-start | bytes 3145736 | tf_op jit(solution)/shard_map/ppermute | solution.py:492
  256.9 1.0 copy-start.5
  263.4 20.7 %collective-permute-start.13 = (f32[8,2048]{1,0:T(8,128)}, f32[8,2048]{1,0:T(8,128)S(1)}, u32[]{:S(2)}, u32[]{:S(2)}) collective-permute-start(f32[8,2048]{1,0:T(8,128)} %get-tuple-element.37), channel_id=1, source_target_pairs={{0,16},{1,17},{2,18},{3,19},{4,20},{5,21},{6,22},{7,23},{8,24},{9,... | collective-permute-start | bytes 196616 | tf_op jit(solution)/shard_map/ppermute | solution.py:477
  285.0 5.9 %collective-permute-start.14 = (f32[8,2048]{1,0:T(8,128)S(1)}, f32[8,2048]{1,0:T(8,128)S(1)}, u32[]{:S(2)}, u32[]{:S(2)}) collective-permute-start(f32[8,2048]{1,0:T(8,128)S(1)} %add.25), channel_id=1, source_target_pairs={{0,64},{1,65},{2,66},{3,67},{4,68},{5,69},{6,70},{7,71},{8,72},{9,... | collective-permute-start | bytes 196616 | tf_op jit(solution)/shard_map/ppermute | solution.py:477
  290.9 4.3 %collective-permute-start.15 = (f32[8,2048]{1,0:T(8,128)S(1)}, f32[8,2048]{1,0:T(8,128)S(1)}, u32[]{:S(2)}, u32[]{:S(2)}) collective-permute-start(f32[8,2048]{1,0:T(8,128)S(1)} %add.26), channel_id=1, source_target_pairs={{0,32},{1,33},{2,34},{3,35},{4,36},{5,37},{6,38},{7,39},{8,40},{9,... | collective-permute-start | bytes 196616 | tf_op jit(solution)/shard_map/ppermute | solution.py:477
  295.3 5.8 %collective-permute-start.16 = (f32[8,2048]{1,0:T(8,128)S(1)}, f32[8,2048]{1,0:T(8,128)S(1)}, u32[]{:S(2)}, u32[]{:S(2)}) collective-permute-start(f32[8,2048]{1,0:T(8,128)S(1)} %add.27), channel_id=1, source_target_pairs={{0,8},{1,9},{2,10},{3,11},{4,12},{5,13},{6,14},{7,15},{8,0},{9,1},... | collective-permute-start | bytes 196616 | tf_op jit(solution)/shard_map/ppermute | solution.py:477
  301.2 4.3 %collective-permute-start.17 = (f32[8,2048]{1,0:T(8,128)S(1)}, f32[8,2048]{1,0:T(8,128)S(1)}, u32[]{:S(2)}, u32[]{:S(2)}) collective-permute-start(f32[8,2048]{1,0:T(8,128)S(1)} %add.28), channel_id=1, source_target_pairs={{0,4},{1,5},{2,6},{3,7},{4,0},{5,1},{6,2},{7,3},{8,12},{9,13},{10,... | collective-permute-start | bytes 196616 | tf_op jit(solution)/shard_map/ppermute | solution.py:477
  305.5 5.8 %collective-permute-start.18 = (f32[8,2048]{1,0:T(8,128)S(1)}, f32[8,2048]{1,0:T(8,128)S(1)}, u32[]{:S(2)}, u32[]{:S(2)}) collective-permute-start(f32[8,2048]{1,0:T(8,128)S(1)} %add.29), channel_id=1, source_target_pairs={{0,2},{1,3},{2,0},{3,1},{4,6},{5,7},{6,4},{7,5},{8,10},{9,11},{10,... | collective-permute-start | bytes 196616 | tf_op jit(solution)/shard_map/ppermute | solution.py:477
  311.4 4.3 %collective-permute-start.19 = (f32[8,2048]{1,0:T(8,128)S(1)}, f32[8,2048]{1,0:T(8,128)S(1)}, u32[]{:S(2)}, u32[]{:S(2)}) collective-permute-start(f32[8,2048]{1,0:T(8,128)S(1)} %add.30), channel_id=1, source_target_pairs={{0,1},{1,0},{2,3},{3,2},{4,5},{5,4},{6,7},{7,6},{8,9},{9,8},{10,11... | collective-permute-start | bytes 196616 | tf_op jit(solution)/shard_map/ppermute | solution.py:477
  316.4 1.0 copy-start.3
  316.4 1.3 copy-start.4

commit v6 on v5

--- a/solution.py
+++ b/solution.py
@@ -12,6 +12,10 @@
 ROWS = 40
 GROUP = 4
 HI = lax.Precision.HIGHEST
+
+
+def vmem(mib):
+    return pltpu.CompilerParams(vmem_limit_bytes=mib * 1024 * 1024)
 
 
 def split2(x):
@@ -123,6 +127,7 @@
             pltpu.VMEM(blocks.shape, jnp.float32),
             pltpu.SemaphoreType.DMA((8,)),
         ],
+        compiler_params=vmem(24),
         name="pack",
     )(owner_map.reshape(1, -1), ids, blocks)
 
@@ -270,6 +275,7 @@
         in_specs=[pl.BlockSpec(memory_space=pltpu.SMEM)]
         + [pl.BlockSpec(memory_space=pltpu.VMEM)] * (2 if last else 1),
         scratch_shapes=scratch,
+        compiler_params=vmem(20),
         name="assemble_last" if last else "assemble_first",
     )(*((base, got, prev) if last else (base, got)))
 
@@ -305,6 +311,7 @@
         inverse_kernel,
         out_shape=jax.ShapeDtypeStruct(upper.shape, jnp.float32),
         scratch_shapes=[pltpu.VMEM(upper.shape, jnp.float32)],
+        compiler_params=vmem(8),
         name="invert",
     )(upper, lower)
 
@@ -374,6 +381,7 @@
         out_specs=tuple(spec(kind, shapes[kind][0]) for kind in outs),
         out_shape=tuple(jax.ShapeDtypeStruct(shapes[kind], jnp.float32) for kind in outs),
         scratch_shapes=[pltpu.VMEM((kept, rows, 3 * rows), jnp.bfloat16)],
+        compiler_params=vmem(24),
     )(*matrices, *(x for _, x in ins))
 
 

time: 328 us -> 308 us (0.939)
  Pallas kernels: 85.7 us -> 61.8 us
    pallas_call x5, Pallas kernels: 35.8 us -> 20.9 us  [in_blocks(): pl.pallas_call(run, grid=(2 * per,), in_specs=[pl.BlockSpec((rows, rows),...]
    pallas_call x1, Pallas kernels: 8.23 us -> 4.38 us  [pack(): pl.pallas_call(pack_kernel, out_shape=(shape, shape), in_specs=[pl.BlockS...]
  transfers between devices with their start and end apart: 21 -> 21, of which waited for: 14 -> 13; matrix products, arithmetic and copies ran while one was open for 1% -> 1% of each run, Pallas kernels for 16% -> 13%
where the time goes in v6:
time: 308 us; the launch traced here: 307 us
  waiting for transfers between devices  127 us (41%)
  starting transfers between devices  63.5 us (21%)
  Pallas kernels  61.8 us (20%)
  blocking collectives  46.1 us (15%)
  local copies, waits for them, and re-layouts  7.61 us (2%)
    ppermute x6, waiting for transfers between devices, from_above(): return lax.ppermute(x, AXES, down)  56.1 us
    all_to_all x1, blocking collectives, exchange(): lax.all_to_all(send.reshape(devices, ROWS, 128), AXES, split_axis=0, conc...  46.1 us
    ppermute x7, waiting for transfers between devices, from_below(): return lax.ppermute(x, AXES, up)  41.6 us
    pallas_call x2, Pallas kernels, assemble(): pl.pallas_call(lambda *refs: assemble_kernel(last, *refs), out_shape=out,...  30.8 us
    ppermute x7, waiting for transfers between devices, butterfly(): x = x + lax.ppermute(x, AXES, [(i, i ^ bit) for i in range(devices)])  29.5 us
    ppermute x6, starting transfers between devices, from_above(): return lax.ppermute(x, AXES, down)  28.9 us
    ppermute x7, starting transfers between devices, butterfly(): x = x + lax.ppermute(x, AXES, [(i, i ^ bit) for i in range(devices)])  22.4 us
    pallas_call x5, Pallas kernels, in_blocks(): pl.pallas_call(run, grid=(2 * per,), in_specs=[pl.BlockSpec((rows, rows),...  20.9 us
  transfers between devices with their start and end apart: 21, of which 13 were waited for; matrix products, arithmetic and copies ran while one was open for 1% of the time, Pallas kernels for 13%

profile of v6, /device:TPU:0, one launch (start us, length us, event | category | flops | bytes accessed | tf_op | source)
XLA Modules:
  0.0 307.3 jit_solution(5461097797203617100)
XLA Ops:
  0.6 0.0 copy-start.2
  0.6 2.3 copy-done.2
  3.0 0.0 copy-start.4
  3.0 0.8 copy-done.4
  3.8 0.7 copy-done.5
  4.4 4.4 %pack.1 = (f32[5120,128]{1,0:T(8,128)S(1)}, f32[5120,128]{1,0:T(8,128)S(1)}) custom-call(s32[1,128]{1,0:T(1,128)S(1)} %bitcast.11, s32[96,128]{1,0:T(8,128)S(1)} %bitcast.10, f32[128,9216]{1,0:T(8,128)S(1)} %copy-done.2), custom_call_target="tpu_custom_call" | custom-call | tf_op jit(solution)/shard_map/pack/pallas_call | solution.py:117
  8.8 0.0 copy-start.3
  8.8 46.1 %all_to_all.10 = f32[128,40,128]{2,1,0:T(8,128)} all-to-all(f32[128,40,128]{2,1,0:T(8,128)S(1)} %bitcast.9), channel_id=1, replica_groups=mesh['row'=8,'col'=16] {'row','col'}, dimensions={0} | all-to-all | bytes 5242880 | tf_op jit(solution)/shard_map/all_to_all | solution.py:510
  54.9 0.0 copy-done.3
  55.0 5.9 %all-to-all-start = ((f32[128,40,128]{2,1,0:T(8,128)}), f32[128,40,128]{2,1,0:T(8,128)}, u32[]{:S(2)}, u32[]{:S(2)}) async-start(f32[128,40,128]{2,1,0:T(8,128)} %bitcast.8), calls=%async_computation | async-start | bytes 5242880 | tf_op jit(solution)/shard_map/all_to_all | solution.py:510
  60.8 0.0 copy-done
  60.8 1.0 slice.6
  61.9 7.0 %collective-permute-start.4 = (f32[128,2048]{1,0:T(8,128)}, f32[128,2048]{1,0:T(8,128)}, u32[]{:S(2)}, u32[]{:S(2)}) collective-permute-start(f32[128,2048]{1,0:T(8,128)} %slice.6), channel_id=1, source_target_pairs={{1,0},{2,1},{3,2},{4,3},{5,4},{6,5},{7,6},{8,7},{9,8},{10,9},{11,1... | collective-permute-start | bytes 3145736 | tf_op jit(solution)/shard_map/ppermute | solution.py:500
  68.8 0.0 collective-permute-start.3
  68.8 1.0 slice.7
  69.9 7.2 %collective-permute-start.6 = (f32[128,2048]{1,0:T(8,128)}, f32[128,2048]{1,0:T(8,128)}, u32[]{:S(2)}, u32[]{:S(2)}) collective-permute-start(f32[128,2048]{1,0:T(8,128)} %slice.7), channel_id=1, source_target_pairs={{1,0},{2,1},{3,2},{4,3},{5,4},{6,5},{7,6},{8,7},{9,8},{10,9},{11,1... | collective-permute-start | bytes 3145736 | tf_op jit(solution)/shard_map/ppermute | solution.py:500
  77.1 0.0 collective-permute-start.5
  77.1 0.1 pad_add_fusion.refs_0_
  77.1 1.7 copy-done.1
  78.9 22.3 %assemble_first.1.refs_2_ = f32[512,512]{1,0:T(8,128)S(1)} custom-call(s32[2]{0:T(128)S(1)} %pad_add_fusion.refs_0_, f32[5120,128]{1,0:T(8,128)S(1)} %bitcast.7), custom_call_target="tpu_custom_call" | custom-call | tf_op jit(solution)/shard_map/assemble_first/pallas_call | solution.py:272
  101.1 0.0 all-to-all-done
  101.1 8.5 %assemble_last.1 = (f32[256,256]{1,0:T(8,128)S(1)}, f32[256,256]{1,0:T(8,128)S(1)}, f32[256,512]{1,0:T(8,128)S(1)}) custom-call(s32[2]{0:T(128)S(1)} %pad_add_fusion.refs_0_, f32[5120,128]{1,0:T(8,128)} %bitcast.4.refs_1_, f32[512,512]{1,0:T(8,128)S(1)} %assemble_first.1.refs_2_), custom_call_target="tpu_custom_call" | custom-call | tf_op jit(solution)/shard_map/assemble_last/pallas_call | solution.py:272
  109.7 0.3 collective-permute-start
  110.0 33.7 %collective-permute-done.lower_ref.refs_0_ = f32[256,512]{1,0:T(8,128)S(1)} collective-permute-done((f32[256,512]{1,0:T(8,128)S(1)}, f32[256,512]{1,0:T(8,128)S(1)}, u32[]{:S(2)}, u32[]{:S(2)}) %collective-permute-start) | collective-permute-done | bytes 524320 | tf_op jit(solution)/shard_map/ppermute | solution.py:497
  143.7 5.8 %invert.1.refs_2_.refs_0_ = f32[256,256]{1,0:T(8,128)S(1)} custom-call(f32[256,256]{1,0:T(8,128)S(1)} %get-tuple-element.25.upper_ref, f32[256,512]{1,0:T(8,128)S(1)} %collective-permute-done.lower_ref.refs_0_), custom_call_target="tpu_custom_call" | custom-call | tf_op jit(solution)/shard_map/invert/pallas_call | solution.py:310
  149.5 8.9 %collective-permute-start.2 = (f32[256,256]{1,0:T(8,128)S(1)}, f32[256,256]{1,0:T(8,128)S(1)}, u32[]{:S(2)}, u32[]{:S(2)}) collective-permute-start(f32[256,256]{1,0:T(8,128)S(1)} %invert.1.refs_2_.refs_0_), channel_id=1, source_target_pairs={{1,0},{2,1},{3,2},{4,3},{5,4},{6,5},{7,6},{8,7},{9,8},{10,9},{11,1... | collective-permute-start | bytes 786440 | tf_op jit(solution)/shard_map/ppermute | solution.py:500
  158.3 0.0 collective-permute-done.4.refs_6_
  158.3 0.0 collective-permute-start.1
  158.3 0.0 collective-permute-done.3.refs_5_
  158.3 3.9 %collective-permute-done.2.refs_4_ = f32[256,256]{1,0:T(8,128)S(1)} collective-permute-done((f32[256,256]{1,0:T(8,128)S(1)}, f32[256,256]{1,0:T(8,128)S(1)}, u32[]{:S(2)}, u32[]{:S(2)}) %collective-permute-start.2) | collective-permute-done | bytes 262176 | tf_op jit(solution)/shard_map/ppermute | solution.py:500
  162.3 7.3 %collective-permute-done.1.refs_3_ = f32[256,256]{1,0:T(8,128)S(1)} collective-permute-done((f32[256,256]{1,0:T(8,128)S(1)}, f32[256,256]{1,0:T(8,128)S(1)}, u32[]{:S(2)}, u32[]{:S(2)}) %collective-permute-start.1) | collective-permute-done | bytes 262176 | tf_op jit(solution)/shard_map/ppermute | solution.py:497
  169.6 0.0 collective-permute-done.6.refs_8_
  169.6 0.0 collective-permute-done.5.refs_7_
  169.6 6.3 %shard_map.59 = (f32[256,2048]{1,0:T(8,128)S(1)}, f32[256,2048]{1,0:T(8,128)S(1)}, f32[8,2048]{1,0:T(8,128)S(1)}) custom-call(f32[256,512]{1,0:T(8,128)S(1)} %collective-permute-done.lower_ref.refs_0_, f32[256,256]{1,0:T(8,128)S(1)} %get-tuple-element.24.refs_1_, f32[256,256]{1,0:T(8,128)S(1)} %invert.1.refs_2_.refs_0_, ...), custom_call_target="tpu_custom_call" | custom-call | tf_op jit(solution)/shard_map/pallas_call | solution.py:376
  175.9 0.2 collective-permute-start.8
  176.1 1.9 collective-permute-start.7
  178.0 2.1 shard_map.60
  180.1 39.9 %collective-permute-done.8.refs_4_ = f32[256,2048]{1,0:T(8,128)S(1)} collective-permute-done((f32[256,2048]{1,0:T(8,128)S(1)}, f32[256,2048]{1,0:T(8,128)S(1)}, u32[]{:S(2)}, u32[]{:S(2)}) %collective-permute-start.8) | collective-permute-done | bytes 2097184 | tf_op jit(solution)/shard_map/ppermute | solution.py:500
  220.0 0.6 collective-permute-done.7.refs_3_
  220.7 5.0 %shard_map.61 = (f32[256,2048]{1,0:T(8,128)S(1)}, f32[256,1024]{1,0:T(8,128)S(1)}, f32[256,1024]{1,0:T(8,128)S(1)}, f32[8,2048]{1,0:T(8,128)S(1)}) custom-call(f32[256,512]{1,0:T(8,128)S(1)} %collective-permute-done.lower_ref.refs_0_, f32[256,256]{1,0:T(8,128)S(1)} %get-tuple-element.24.refs_1_, f32[256,256]{1,0:T(8,128)S(1)} %invert.1.refs_2_.refs_0_, ...), custom_call_target="tpu_custom_call" | custom-call | tf_op jit(solution)/shard_map/pallas_call | solution.py:376
  225.6 0.4 collective-permute-start.9
  226.1 2.2 collective-permute-start.10
  228.3 1.9 collective-permute-start.11
  230.2 5.2 %collective-permute-start.12 = (f32[256,1024]{1,0:T(8,128)S(1)}, f32[256,1024]{1,0:T(8,128)S(1)}, u32[]{:S(2)}, u32[]{:S(2)}) collective-permute-start(f32[256,1024]{1,0:T(8,128)S(1)} %get-tuple-element.34.refs_4_.refs_10_), channel_id=1, source_target_pairs={{1,0},{2,1},{3,2},{4,3},{5,4},{6,5},{7,6},{8,7},{9,8},{10,9},{11,1... | collective-permute-start | bytes 3145736 | tf_op jit(solution)/shard_map/ppermute | solution.py:500
  235.5 12.3 %collective-permute-done.9.refs_3_ = f32[256,1024]{1,0:T(8,128)S(1)} collective-permute-done((f32[256,1024]{1,0:T(8,128)S(1)}, f32[256,1024]{1,0:T(8,128)S(1)}, u32[]{:S(2)}, u32[]{:S(2)}) %collective-permute-start.9) | collective-permute-done | bytes 1048608 | tf_op jit(solution)/shard_map/ppermute | solution.py:500
  247.7 0.0 collective-permute-done.10.refs_5_
  247.7 2.4 shard_map.62
  250.1 20.4 %collective-permute-start.13 = (f32[8,2048]{1,0:T(8,128)S(1)}, f32[8,2048]{1,0:T(8,128)S(1)}, u32[]{:S(2)}, u32[]{:S(2)}) collective-permute-start(f32[8,2048]{1,0:T(8,128)S(1)} %get-tuple-element.37), channel_id=1, source_target_pairs={{0,16},{1,17},{2,18},{3,19},{4,20},{5,21},{6,22},{7,23},{8,24},{9,... | collective-permute-start | bytes 196616 | tf_op jit(solution)/shard_map/ppermute | solution.py:485
  270.5 0.9 collective-permute-done.13
  271.4 1.6 collective-permute-start.14
  273.0 4.3 %collective-permute-done.14 = f32[8,2048]{1,0:T(8,128)S(1)} collective-permute-done((f32[8,2048]{1,0:T(8,128)S(1)}, f32[8,2048]{1,0:T(8,128)S(1)}, u32[]{:S(2)}, u32[]{:S(2)}) %collective-permute-start.14) | collective-permute-done | bytes 65568 | tf_op jit(solution)/shard_map/ppermute | solution.py:485
  277.3 0.1 collective-permute-start.15
  277.4 4.3 %collective-permute-done.15 = f32[8,2048]{1,0:T(8,128)S(1)} collective-permute-done((f32[8,2048]{1,0:T(8,128)S(1)}, f32[8,2048]{1,0:T(8,128)S(1)}, u32[]{:S(2)}, u32[]{:S(2)}) %collective-permute-start.15) | collective-permute-done | bytes 65568 | tf_op jit(solution)/shard_map/ppermute | solution.py:485
  281.7 0.1 collective-permute-start.16
  281.8 5.8 %collective-permute-done.16 = f32[8,2048]{1,0:T(8,128)S(1)} collective-permute-done((f32[8,2048]{1,0:T(8,128)S(1)}, f32[8,2048]{1,0:T(8,128)S(1)}, u32[]{:S(2)}, u32[]{:S(2)}) %collective-permute-start.16) | collective-permute-done | bytes 65568 | tf_op jit(solution)/shard_map/ppermute | solution.py:485
  287.6 0.1 collective-permute-start.17
  287.7 4.3 %collective-permute-done.17 = f32[8,2048]{1,0:T(8,128)S(1)} collective-permute-done((f32[8,2048]{1,0:T(8,128)S(1)}, f32[8,2048]{1,0:T(8,128)S(1)}, u32[]{:S(2)}, u32[]{:S(2)}) %collective-permute-start.17) | collective-permute-done | bytes 65568 | tf_op jit(solution)/shard_map/ppermute | solution.py:485
  291.9 0.1 collective-permute-start.18
  292.0 5.8 %collective-permute-done.18 = f32[8,2048]{1,0:T(8,128)S(1)} collective-permute-done((f32[8,2048]{1,0:T(8,128)S(1)}, f32[8,2048]{1,0:T(8,128)S(1)}, u32[]{:S(2)}, u32[]{:S(2)}) %collective-permute-start.18) | collective-permute-done | bytes 65568 | tf_op jit(solution)/shard_map/ppermute | solution.py:485
  297.8 0.1 collective-permute-start.19
  297.9 4.3 %collective-permute-done.19 = f32[8,2048]{1,0:T(8,128)S(1)} collective-permute-done((f32[8,2048]{1,0:T(8,128)S(1)}, f32[8,2048]{1,0:T(8,128)S(1)}, u32[]{:S(2)}, u32[]{:S(2)}) %collective-permute-start.19) | collective-permute-done | bytes 65568 | tf_op jit(solution)/shard_map/ppermute | solution.py:485
  302.1 0.0 collective-permute-done.11.refs_9_
  302.1 0.0 collective-permute-done.12.refs_11_
  302.2 5.1 %shard_map.63 = (f32[256,2048]{1,0:T(8,128)}, f32[256,2048]{1,0:T(8,128)}) custom-call(f32[256,512]{1,0:T(8,128)S(1)} %collective-permute-done.lower_ref.refs_0_, f32[256,256]{1,0:T(8,128)S(1)} %get-tuple-element.24.refs_1_, f32[256,2048]{1,0:T(8,128)S(1)} %copy-done, f32[256,2048]{1,0:T(8,128)S(1)} %get-tuple-element.29.refs_3_, ...), custom_call_target="tpu_custom_call" | custom-call | tf_op jit(solution)/shard_map/pallas_call | solution.py:376
  (10 shorter events, 0.1 us)
Async XLA Ops:
  0.6 2.3 copy-start.2
  3.0 0.8 copy-start.4
  3.8 0.7 copy-start.5
  8.8 46.1 %copy-start.3 = (f32[5120,128]{1,0:T(8,128)}, f32[5120,128]{1,0:T(8,128)S(1)}, u32[]{:S(2)}) copy-start(f32[5120,128]{1,0:T(8,128)S(1)} %get-tuple-element.20) | copy-start | bytes 7864324
  54.9 5.9 %copy-start = (f32[256,2048]{1,0:T(8,128)S(1)}, f32[256,2048]{1,0:T(8,128)}, u32[]{:S(2)}) copy-start(f32[256,2048]{1,0:T(8,128)} %refs_2_.1) | copy-start | bytes 6291460
  55.0 46.2 %all-to-all-start = ((f32[128,40,128]{2,1,0:T(8,128)}), f32[128,40,128]{2,1,0:T(8,128)}, u32[]{:S(2)}, u32[]{:S(2)}) async-start(f32[128,40,128]{2,1,0:T(8,128)} %bitcast.8), calls=%async_computation | async-start | bytes 5242880 | tf_op jit(solution)/shard_map/all_to_all | solution.py:510
  61.9 96.5 %collective-permute-start.4 = (f32[128,2048]{1,0:T(8,128)}, f32[128,2048]{1,0:T(8,128)}, u32[]{:S(2)}, u32[]{:S(2)}) collective-permute-start(f32[128,2048]{1,0:T(8,128)} %slice.6), channel_id=1, source_target_pairs={{1,0},{2,1},{3,2},{4,3},{5,4},{6,5},{7,6},{8,7},{9,8},{10,9},{11,1... | collective-permute-start | bytes 3145736 | tf_op jit(solution)/shard_map/ppermute | solution.py:500
  68.8 89.5 %collective-permute-start.3 = (f32[128,2048]{1,0:T(8,128)}, f32[128,2048]{1,0:T(8,128)}, u32[]{:S(2)}, u32[]{:S(2)}) collective-permute-start(f32[128,2048]{1,0:T(8,128)} %slice.6), channel_id=1, source_target_pairs={{0,1},{1,2},{2,3},{3,4},{4,5},{5,6},{6,7},{7,8},{8,9},{9,10},{10,1... | collective-permute-start | bytes 3145736 | tf_op jit(solution)/shard_map/ppermute | solution.py:497
  69.9 99.7 %collective-permute-start.6 = (f32[128,2048]{1,0:T(8,128)}, f32[128,2048]{1,0:T(8,128)}, u32[]{:S(2)}, u32[]{:S(2)}) collective-permute-start(f32[128,2048]{1,0:T(8,128)} %slice.7), channel_id=1, source_target_pairs={{1,0},{2,1},{3,2},{4,3},{5,4},{6,5},{7,6},{8,7},{9,8},{10,9},{11,1... | collective-permute-start | bytes 3145736 | tf_op jit(solution)/shard_map/ppermute | solution.py:500
  77.1 92.5 %collective-permute-start.5 = (f32[128,2048]{1,0:T(8,128)}, f32[128,2048]{1,0:T(8,128)}, u32[]{:S(2)}, u32[]{:S(2)}) collective-permute-start(f32[128,2048]{1,0:T(8,128)} %slice.7), channel_id=1, source_target_pairs={{0,1},{1,2},{2,3},{3,4},{4,5},{5,6},{6,7},{7,8},{8,9},{9,10},{10,1... | collective-permute-start | bytes 3145736 | tf_op jit(solution)/shard_map/ppermute | solution.py:497
  77.1 1.7 copy-start.1
  109.7 34.0 %collective-permute-start = (f32[256,512]{1,0:T(8,128)S(1)}, f32[256,512]{1,0:T(8,128)S(1)}, u32[]{:S(2)}, u32[]{:S(2)}) collective-permute-start(f32[256,512]{1,0:T(8,128)S(1)} %get-tuple-element.23), channel_id=1, source_target_pairs={{0,1},{1,2},{2,3},{3,4},{4,5},{5,6},{6,7},{7,8},{8,9},{9,10},{10,1... | collective-permute-start | bytes 1572872 | tf_op jit(solution)/shard_map/ppermute | solution.py:497
  149.5 12.8 %collective-permute-start.2 = (f32[256,256]{1,0:T(8,128)S(1)}, f32[256,256]{1,0:T(8,128)S(1)}, u32[]{:S(2)}, u32[]{:S(2)}) collective-permute-start(f32[256,256]{1,0:T(8,128)S(1)} %invert.1.refs_2_.refs_0_), channel_id=1, source_target_pairs={{1,0},{2,1},{3,2},{4,3},{5,4},{6,5},{7,6},{8,7},{9,8},{10,9},{11,1... | collective-permute-start | bytes 786440 | tf_op jit(solution)/shard_map/ppermute | solution.py:500
  158.3 11.2 %collective-permute-start.1 = (f32[256,256]{1,0:T(8,128)S(1)}, f32[256,256]{1,0:T(8,128)S(1)}, u32[]{:S(2)}, u32[]{:S(2)}) collective-permute-start(f32[256,256]{1,0:T(8,128)S(1)} %invert.1.refs_2_.refs_0_), channel_id=1, source_target_pairs={{0,1},{1,2},{2,3},{3,4},{4,5},{5,6},{6,7},{7,8},{8,9},{9,10},{10,1... | collective-permute-start | bytes 786440 | tf_op jit(solution)/shard_map/ppermute | solution.py:497
  175.9 44.2 %collective-permute-start.8 = (f32[256,2048]{1,0:T(8,128)S(1)}, f32[256,2048]{1,0:T(8,128)S(1)}, u32[]{:S(2)}, u32[]{:S(2)}) collective-permute-start(f32[256,2048]{1,0:T(8,128)S(1)} %get-tuple-element.30.refs_5_), channel_id=1, source_target_pairs={{1,0},{2,1},{3,2},{4,3},{5,4},{6,5},{7,6},{8,7},{9,8},{10,9},{11,1... | collective-permute-start | bytes 6291464 | tf_op jit(solution)/shard_map/ppermute | solution.py:500
  176.1 44.6 %collective-permute-start.7 = (f32[256,2048]{1,0:T(8,128)S(1)}, f32[256,2048]{1,0:T(8,128)S(1)}, u32[]{:S(2)}, u32[]{:S(2)}) collective-permute-start(f32[256,2048]{1,0:T(8,128)S(1)} %get-tuple-element.30.refs_5_), channel_id=1, source_target_pairs={{0,1},{1,2},{2,3},{3,4},{4,5},{5,6},{6,7},{7,8},{8,9},{9,10},{10,1... | collective-permute-start | bytes 6291464 | tf_op jit(solution)/shard_map/ppermute | solution.py:497
  225.6 22.1 %collective-permute-start.9 = (f32[256,1024]{1,0:T(8,128)S(1)}, f32[256,1024]{1,0:T(8,128)S(1)}, u32[]{:S(2)}, u32[]{:S(2)}) collective-permute-start(f32[256,1024]{1,0:T(8,128)S(1)} %get-tuple-element.33.refs_2_.refs_8_), channel_id=1, source_target_pairs={{1,0},{2,1},{3,2},{4,3},{5,4},{6,5},{7,6},{8,7},{9,8},{10,9},{11,1... | collective-permute-start | bytes 3145736 | tf_op jit(solution)/shard_map/ppermute | solution.py:500
  226.1 21.7 %collective-permute-start.10 = (f32[256,1024]{1,0:T(8,128)S(1)}, f32[256,1024]{1,0:T(8,128)S(1)}, u32[]{:S(2)}, u32[]{:S(2)}) collective-permute-start(f32[256,1024]{1,0:T(8,128)S(1)} %get-tuple-element.34.refs_4_.refs_10_), channel_id=1, source_target_pairs={{0,1},{1,2},{2,3},{3,4},{4,5},{5,6},{6,7},{7,8},{8,9},{9,10},{10,1... | collective-permute-start | bytes 3145736 | tf_op jit(solution)/shard_map/ppermute | solution.py:497
  228.3 73.9 %collective-permute-start.11 = (f32[256,1024]{1,0:T(8,128)S(1)}, f32[256,1024]{1,0:T(8,128)S(1)}, u32[]{:S(2)}, u32[]{:S(2)}) collective-permute-start(f32[256,1024]{1,0:T(8,128)S(1)} %get-tuple-element.33.refs_2_.refs_8_), channel_id=1, source_target_pairs={{0,1},{1,2},{2,3},{3,4},{4,5},{5,6},{6,7},{7,8},{8,9},{9,10},{10,1... | collective-permute-start | bytes 3145736 | tf_op jit(solution)/shard_map/ppermute | solution.py:497
  230.2 71.9 %collective-permute-start.12 = (f32[256,1024]{1,0:T(8,128)S(1)}, f32[256,1024]{1,0:T(8,128)S(1)}, u32[]{:S(2)}, u32[]{:S(2)}) collective-permute-start(f32[256,1024]{1,0:T(8,128)S(1)} %get-tuple-element.34.refs_4_.refs_10_), channel_id=1, source_target_pairs={{1,0},{2,1},{3,2},{4,3},{5,4},{6,5},{7,6},{8,7},{9,8},{10,9},{11,1... | collective-permute-start | bytes 3145736 | tf_op jit(solution)/shard_map/ppermute | solution.py:500
  250.1 21.3 %collective-permute-start.13 = (f32[8,2048]{1,0:T(8,128)S(1)}, f32[8,2048]{1,0:T(8,128)S(1)}, u32[]{:S(2)}, u32[]{:S(2)}) collective-permute-start(f32[8,2048]{1,0:T(8,128)S(1)} %get-tuple-element.37), channel_id=1, source_target_pairs={{0,16},{1,17},{2,18},{3,19},{4,20},{5,21},{6,22},{7,23},{8,24},{9,... | collective-permute-start | bytes 196616 | tf_op jit(solution)/shard_map/ppermute | solution.py:485
  271.4 5.9 %collective-permute-start.14 = (f32[8,2048]{1,0:T(8,128)S(1)}, f32[8,2048]{1,0:T(8,128)S(1)}, u32[]{:S(2)}, u32[]{:S(2)}) collective-permute-start(f32[8,2048]{1,0:T(8,128)S(1)} %add.25), channel_id=1, source_target_pairs={{0,64},{1,65},{2,66},{3,67},{4,68},{5,69},{6,70},{7,71},{8,72},{9,... | collective-permute-start | bytes 196616 | tf_op jit(solution)/shard_map/ppermute | solution.py:485
  277.3 4.3 %collective-permute-start.15 = (f32[8,2048]{1,0:T(8,128)S(1)}, f32[8,2048]{1,0:T(8,128)S(1)}, u32[]{:S(2)}, u32[]{:S(2)}) collective-permute-start(f32[8,2048]{1,0:T(8,128)S(1)} %add.26), channel_id=1, source_target_pairs={{0,32},{1,33},{2,34},{3,35},{4,36},{5,37},{6,38},{7,39},{8,40},{9,... | collective-permute-start | bytes 196616 | tf_op jit(solution)/shard_map/ppermute | solution.py:485
  281.7 5.8 %collective-permute-start.16 = (f32[8,2048]{1,0:T(8,128)S(1)}, f32[8,2048]{1,0:T(8,128)S(1)}, u32[]{:S(2)}, u32[]{:S(2)}) collective-permute-start(f32[8,2048]{1,0:T(8,128)S(1)} %add.27), channel_id=1, source_target_pairs={{0,8},{1,9},{2,10},{3,11},{4,12},{5,13},{6,14},{7,15},{8,0},{9,1},... | collective-permute-start | bytes 196616 | tf_op jit(solution)/shard_map/ppermute | solution.py:485
  287.6 4.3 %collective-permute-start.17 = (f32[8,2048]{1,0:T(8,128)S(1)}, f32[8,2048]{1,0:T(8,128)S(1)}, u32[]{:S(2)}, u32[]{:S(2)}) collective-permute-start(f32[8,2048]{1,0:T(8,128)S(1)} %add.28), channel_id=1, source_target_pairs={{0,4},{1,5},{2,6},{3,7},{4,0},{5,1},{6,2},{7,3},{8,12},{9,13},{10,... | collective-permute-start | bytes 196616 | tf_op jit(solution)/shard_map/ppermute | solution.py:485
  291.9 5.8 %collective-permute-start.18 = (f32[8,2048]{1,0:T(8,128)S(1)}, f32[8,2048]{1,0:T(8,128)S(1)}, u32[]{:S(2)}, u32[]{:S(2)}) collective-permute-start(f32[8,2048]{1,0:T(8,128)S(1)} %add.29), channel_id=1, source_target_pairs={{0,2},{1,3},{2,0},{3,1},{4,6},{5,7},{6,4},{7,5},{8,10},{9,11},{10,... | collective-permute-start | bytes 196616 | tf_op jit(solution)/shard_map/ppermute | solution.py:485
  297.8 4.3 %collective-permute-start.19 = (f32[8,2048]{1,0:T(8,128)S(1)}, f32[8,2048]{1,0:T(8,128)S(1)}, u32[]{:S(2)}, u32[]{:S(2)}) collective-permute-start(f32[8,2048]{1,0:T(8,128)S(1)} %add.30), channel_id=1, source_target_pairs={{0,1},{1,0},{2,3},{3,2},{4,5},{5,4},{6,7},{7,6},{8,9},{9,8},{10,11... | collective-permute-start | bytes 196616 | tf_op jit(solution)/shard_map/ppermute | solution.py:485

commit v7 on v6

--- a/solution.py
+++ b/solution.py
@@ -120,7 +120,7 @@
         in_specs=[
             pl.BlockSpec(memory_space=pltpu.VMEM),
             pl.BlockSpec(memory_space=pltpu.VMEM),
-            pl.BlockSpec(memory_space=pl.ANY),
+            pl.BlockSpec(memory_space=pltpu.HBM),
         ],
         scratch_shapes=[
             pltpu.VMEM((8, blocks.shape[0], 128), jnp.float32),
@@ -249,8 +249,17 @@
     s11_ref[...] = a11 + a11.T
     s12 = acc_ref[:half, half:] + acc_ref[half:, :half].T
     s12_ref[...] = s12
-    low_ref[:, :half] = s12.T
-    low_ref[:, half:] = a22 + a22.T
+    s22 = a22 + a22.T
+    edge = half // 2
+    row = lax.broadcasted_iota(jnp.int32, (edge, edge), 0)
+    col = lax.broadcasted_iota(jnp.int32, (edge, edge), 1)
+    last_part = s22[edge:, edge:]
+    low_ref[:half, :half] = s12.T
+    low_ref[:edge, half:] = s22[:edge, edge:]
+    low_ref[edge:half, half:] = jnp.where(col >= row, s22[:edge, :edge], last_part)
+    diag = jnp.sum(jnp.where(col == row, last_part, 0.0), axis=0, keepdims=True)
+    low_ref[half:, :half] = jnp.zeros((8, half), jnp.float32)
+    low_ref[half:, half:] = jnp.broadcast_to(diag, (8, edge))
 
 
 def assemble(base, got, window, prev=None):
@@ -268,7 +277,8 @@
     ]
     if last:
         scratch = [pltpu.VMEM((window, window), jnp.float32)] + scratch
-    out = (square, square, jax.ShapeDtypeStruct((half, window), jnp.float32)) if last else whole
+    folded = jax.ShapeDtypeStruct((half + 8, half + half // 2), jnp.float32)
+    out = (square, square, folded) if last else whole
     return pl.pallas_call(
         lambda *refs: assemble_kernel(last, *refs),
         out_shape=out,
@@ -288,7 +298,23 @@
         1.0,
         0.0,
     )
-    mat = upper_ref[...] + lower_ref[:, size:] + eye
+    edge = size // 2
+    row = lax.broadcasted_iota(jnp.int32, (edge, edge), 0)
+    col = lax.broadcasted_iota(jnp.int32, (edge, edge), 1)
+    side = lower_ref[:edge, size:]
+    both = lower_ref[edge:size, size:]
+    above = jnp.where(col > row, both, 0.0)
+    below = jnp.where(col < row, both, 0.0)
+    first = jnp.where(col >= row, both, 0.0) + above.T
+    second = below + below.T + jnp.where(col == row, lower_ref[size : size + 1, size:], 0.0)
+    lower = jnp.concatenate(
+        [
+            jnp.concatenate([first, side], axis=1),
+            jnp.concatenate([side.T, second], axis=1),
+        ],
+        axis=0,
+    )
+    mat = upper_ref[...] + lower + eye
     mat_ref[...] = mat
     norm = jnp.max(jnp.sum(jnp.abs(mat), axis=0, keepdims=True))
     out_ref[...] = eye * (2.0 / (norm + 1.0))
@@ -347,7 +373,7 @@
 
 
 def in_blocks(kernel, matrices, wholes, lefts, rights, sums, outs, kept):
-    rows = matrices[0].shape[0]
+    rows = matrices[-1].shape[0]
     total = wholes[0].shape[1] if wholes else 2 * lefts[0].shape[1]
     per = total // 2 // BLOCK
     maps = {
@@ -481,7 +507,7 @@
 
 
 def butterfly(x, devices):
-    for bit in (16, 64, 32, 8, 4, 2, 1):
+    for bit in (16, 32, 96, 4, 12, 1, 3):
         x = x + lax.ppermute(x, AXES, [(i, i ^ bit) for i in range(devices)])
     return x
 
@@ -547,8 +573,9 @@
     )
     near_0 = from_above(w2_0)
     near_1 = from_below(w2_1)
-    far_0 = from_below(w2_0)
-    far_1 = from_above(w2_1)
+    near_0, near_1, later_0, later_1 = lax.optimization_barrier((near_0, near_1, w2_0, w2_1))
+    far_0 = from_below(later_0)
+    far_1 = from_above(later_1)
     bands = (lower, high_band)
     t, sums = in_blocks(
         side_kernel, bands, (), (w2_0, near_0), (w2_1, near_1), (sums,), ("whole", "sums"), 2

time: 308 us -> 309 us (level)
  waiting for transfers between devices: 127 us -> 133 us
  starting transfers between devices: 63.5 us -> 59.8 us
    ppermute x6, waiting for transfers between devices: 56.1 us -> 63.3 us  [from_above(): return lax.ppermute(x, AXES, down)]
    ppermute x7, starting transfers between devices: 22.4 us -> 18.7 us  [butterfly(): x = x + lax.ppermute(x, AXES, [(i, i ^ bit) for i in range(devices)])]
where the time goes in v7:
time: 309 us
  waiting for transfers between devices  133 us (43%)
  Pallas kernels  61.9 us (20%)
  starting transfers between devices  59.8 us (19%)
  blocking collectives  46.1 us (15%)
  local copies, waits for them, and re-layouts  7.61 us (2%)
    ppermute x6, waiting for transfers between devices, from_above(): return lax.ppermute(x, AXES, down)  63.3 us
    all_to_all x1, blocking collectives, exchange(): lax.all_to_all(send.reshape(devices, ROWS, 128), AXES, split_axis=0, conc...  46.1 us
    ppermute x7, waiting for transfers between devices, from_below(): return lax.ppermute(x, AXES, up)  39.1 us
    pallas_call x2, Pallas kernels, assemble(): pl.pallas_call(lambda *refs: assemble_kernel(last, *refs), out_shape=out,...  30.8 us
    ppermute x7, waiting for transfers between devices, butterfly(): x = x + lax.ppermute(x, AXES, [(i, i ^ bit) for i in range(devices)])  30.1 us
    ppermute x6, starting transfers between devices, from_above(): return lax.ppermute(x, AXES, down)  27.2 us
    pallas_call x5, Pallas kernels, in_blocks(): pl.pallas_call(run, grid=(2 * per,), in_specs=[pl.BlockSpec((rows, rows),...  20.9 us
    ppermute x7, starting transfers between devices, butterfly(): x = x + lax.ppermute(x, AXES, [(i, i ^ bit) for i in range(devices)])  18.7 us
  transfers between devices with their start and end apart: 21, of which 13 were waited for; matrix products, arithmetic and copies ran while one was open for 1% of the time, Pallas kernels for 13%

profile of v7, /device:TPU:0, one launch (start us, length us, event | category | flops | bytes accessed | tf_op | source)
XLA Modules:
  0.0 309.0 jit_solution(18187064790494319708)
XLA Ops:
  0.6 0.0 copy-start.2
  0.6 2.3 copy-done.2
  3.0 0.0 copy-start.4
  3.0 0.8 copy-done.4
  3.8 0.7 copy-done.5
  4.4 4.4 %pack.1 = (f32[5120,128]{1,0:T(8,128)S(1)}, f32[5120,128]{1,0:T(8,128)S(1)}) custom-call(s32[1,128]{1,0:T(1,128)S(1)} %bitcast.11, s32[96,128]{1,0:T(8,128)S(1)} %bitcast.10, f32[128,9216]{1,0:T(8,128)S(1)} %copy-done.2), custom_call_target="tpu_custom_call" | custom-call | tf_op jit(solution)/shard_map/pack/pallas_call | solution.py:117
  8.8 0.0 copy-start.3
  8.8 46.1 %all_to_all.10 = f32[128,40,128]{2,1,0:T(8,128)} all-to-all(f32[128,40,128]{2,1,0:T(8,128)S(1)} %bitcast.9), channel_id=1, replica_groups=mesh['row'=8,'col'=16] {'row','col'}, dimensions={0} | all-to-all | bytes 5242880 | tf_op jit(solution)/shard_map/all_to_all | solution.py:536
  54.9 0.0 copy-done.3
  55.0 5.9 %all-to-all-start = ((f32[128,40,128]{2,1,0:T(8,128)}), f32[128,40,128]{2,1,0:T(8,128)}, u32[]{:S(2)}, u32[]{:S(2)}) async-start(f32[128,40,128]{2,1,0:T(8,128)} %bitcast.8), calls=%async_computation | async-start | bytes 5242880 | tf_op jit(solution)/shard_map/all_to_all | solution.py:536
  60.8 0.0 copy-done
  60.8 1.0 slice.6
  61.9 7.0 %collective-permute-start.4 = (f32[128,2048]{1,0:T(8,128)}, f32[128,2048]{1,0:T(8,128)}, u32[]{:S(2)}, u32[]{:S(2)}) collective-permute-start(f32[128,2048]{1,0:T(8,128)} %slice.6), channel_id=1, source_target_pairs={{1,0},{2,1},{3,2},{4,3},{5,4},{6,5},{7,6},{8,7},{9,8},{10,9},{11,1... | collective-permute-start | bytes 3145736 | tf_op jit(solution)/shard_map/ppermute | solution.py:526
  68.8 0.0 collective-permute-start.3
  68.8 1.0 slice.7
  69.9 7.2 %collective-permute-start.6 = (f32[128,2048]{1,0:T(8,128)}, f32[128,2048]{1,0:T(8,128)}, u32[]{:S(2)}, u32[]{:S(2)}) collective-permute-start(f32[128,2048]{1,0:T(8,128)} %slice.7), channel_id=1, source_target_pairs={{1,0},{2,1},{3,2},{4,3},{5,4},{6,5},{7,6},{8,7},{9,8},{10,9},{11,1... | collective-permute-start | bytes 3145736 | tf_op jit(solution)/shard_map/ppermute | solution.py:526
  77.1 0.0 collective-permute-start.5
  77.1 0.1 pad_add_fusion.refs_0_
  77.1 1.7 copy-done.1
  78.9 22.3 %assemble_first.1.refs_2_ = f32[512,512]{1,0:T(8,128)S(1)} custom-call(s32[2]{0:T(128)S(1)} %pad_add_fusion.refs_0_, f32[5120,128]{1,0:T(8,128)S(1)} %bitcast.7), custom_call_target="tpu_custom_call" | custom-call | tf_op jit(solution)/shard_map/assemble_first/pallas_call | solution.py:282
  101.1 0.0 all-to-all-done
  101.1 8.5 %assemble_last.1 = (f32[256,256]{1,0:T(8,128)S(1)}, f32[256,256]{1,0:T(8,128)S(1)}, f32[264,384]{1,0:T(8,128)S(1)}) custom-call(s32[2]{0:T(128)S(1)} %pad_add_fusion.refs_0_, f32[5120,128]{1,0:T(8,128)} %bitcast.4.refs_1_, f32[512,512]{1,0:T(8,128)S(1)} %assemble_first.1.refs_2_), custom_call_target="tpu_custom_call" | custom-call | tf_op jit(solution)/shard_map/assemble_last/pallas_call | solution.py:282
  109.7 0.3 collective-permute-start
  109.9 31.2 %collective-permute-done.lower_ref.refs_0_ = f32[264,384]{1,0:T(8,128)S(1)} collective-permute-done((f32[264,384]{1,0:T(8,128)S(1)}, f32[264,384]{1,0:T(8,128)S(1)}, u32[]{:S(2)}, u32[]{:S(2)}) %collective-permute-start) | collective-permute-done | bytes 405536 | tf_op jit(solution)/shard_map/ppermute | solution.py:523
  141.1 5.9 %invert.1.refs_2_.refs_0_ = f32[256,256]{1,0:T(8,128)S(1)} custom-call(f32[256,256]{1,0:T(8,128)S(1)} %get-tuple-element.29.upper_ref, f32[264,384]{1,0:T(8,128)S(1)} %collective-permute-done.lower_ref.refs_0_), custom_call_target="tpu_custom_call" | custom-call | tf_op jit(solution)/shard_map/invert/pallas_call | solution.py:336
  147.0 8.9 %collective-permute-start.2 = (f32[256,256]{1,0:T(8,128)S(1)}, f32[256,256]{1,0:T(8,128)S(1)}, u32[]{:S(2)}, u32[]{:S(2)}) collective-permute-start(f32[256,256]{1,0:T(8,128)S(1)} %invert.1.refs_2_.refs_0_), channel_id=1, source_target_pairs={{1,0},{2,1},{3,2},{4,3},{5,4},{6,5},{7,6},{8,7},{9,8},{10,9},{11,1... | collective-permute-start | bytes 786440 | tf_op jit(solution)/shard_map/ppermute | solution.py:526
  155.9 0.0 collective-permute-done.4.refs_6_
  155.9 0.0 collective-permute-start.1
  155.9 0.0 collective-permute-done.3.refs_5_
  155.9 3.9 %collective-permute-done.2.refs_4_ = f32[256,256]{1,0:T(8,128)S(1)} collective-permute-done((f32[256,256]{1,0:T(8,128)S(1)}, f32[256,256]{1,0:T(8,128)S(1)}, u32[]{:S(2)}, u32[]{:S(2)}) %collective-permute-start.2) | collective-permute-done | bytes 262176 | tf_op jit(solution)/shard_map/ppermute | solution.py:526
  159.8 7.3 %collective-permute-done.1.refs_3_ = f32[256,256]{1,0:T(8,128)S(1)} collective-permute-done((f32[256,256]{1,0:T(8,128)S(1)}, f32[256,256]{1,0:T(8,128)S(1)}, u32[]{:S(2)}, u32[]{:S(2)}) %collective-permute-start.1) | collective-permute-done | bytes 262176 | tf_op jit(solution)/shard_map/ppermute | solution.py:523
  167.1 0.0 collective-permute-done.6.refs_8_
  167.1 0.0 collective-permute-done.5.refs_7_
  167.1 6.3 %shard_map.59 = (f32[256,2048]{1,0:T(8,128)S(1)}, f32[256,2048]{1,0:T(8,128)S(1)}, f32[8,2048]{1,0:T(8,128)S(1)}) custom-call(f32[264,384]{1,0:T(8,128)S(1)} %collective-permute-done.lower_ref.refs_0_, f32[256,256]{1,0:T(8,128)S(1)} %get-tuple-element.28.refs_1_, f32[256,256]{1,0:T(8,128)S(1)} %invert.1.refs_2_.refs_0_, ...), custom_call_target="tpu_custom_call" | custom-call | tf_op jit(solution)/shard_map/pallas_call | solution.py:402
  173.4 0.2 collective-permute-start.8
  173.6 1.9 collective-permute-start.7
  175.5 2.1 shard_map.60
  177.6 39.9 %collective-permute-done.8.refs_4_ = f32[256,2048]{1,0:T(8,128)S(1)} collective-permute-done((f32[256,2048]{1,0:T(8,128)S(1)}, f32[256,2048]{1,0:T(8,128)S(1)}, u32[]{:S(2)}, u32[]{:S(2)}) %collective-permute-start.8) | collective-permute-done | bytes 2097184 | tf_op jit(solution)/shard_map/ppermute | solution.py:526
  217.6 0.6 collective-permute-done.7.refs_3_
  218.2 5.0 %shard_map.61 = (f32[256,2048]{1,0:T(8,128)S(1)}, f32[256,1024]{1,0:T(8,128)S(1)}, f32[256,1024]{1,0:T(8,128)S(1)}, f32[8,2048]{1,0:T(8,128)S(1)}) custom-call(f32[264,384]{1,0:T(8,128)S(1)} %collective-permute-done.lower_ref.refs_0_, f32[256,256]{1,0:T(8,128)S(1)} %get-tuple-element.28.refs_1_, f32[256,256]{1,0:T(8,128)S(1)} %invert.1.refs_2_.refs_0_, ...), custom_call_target="tpu_custom_call" | custom-call | tf_op jit(solution)/shard_map/pallas_call | solution.py:402
  223.2 0.4 collective-permute-start.9
  223.6 2.2 collective-permute-start.10
  225.8 19.4 %collective-permute-done.9.refs_3_ = f32[256,1024]{1,0:T(8,128)S(1)} collective-permute-done((f32[256,1024]{1,0:T(8,128)S(1)}, f32[256,1024]{1,0:T(8,128)S(1)}, u32[]{:S(2)}, u32[]{:S(2)}) %collective-permute-start.9) | collective-permute-done | bytes 1048608 | tf_op jit(solution)/shard_map/ppermute | solution.py:526
  245.3 0.0 collective-permute-done.10.refs_5_
  245.3 3.6 %collective-permute-start.11 = (f32[256,1024]{1,0:T(8,128)S(1)}, f32[256,1024]{1,0:T(8,128)S(1)}, u32[]{:S(2)}, u32[]{:S(2)}) collective-permute-start(f32[256,1024]{1,0:T(8,128)S(1)} %get-tuple-element.43.refs_2_.refs_8_), channel_id=1, source_target_pairs={{0,1},{1,2},{2,3},{3,4},{4,5},{5,6},{6,7},{7,8},{8,9},{9,10},{10,1... | collective-permute-start | bytes 3145736 | tf_op jit(solution)/shard_map/ppermute | solution.py:523
  248.8 3.6 %collective-permute-start.12 = (f32[256,1024]{1,0:T(8,128)S(1)}, f32[256,1024]{1,0:T(8,128)S(1)}, u32[]{:S(2)}, u32[]{:S(2)}) collective-permute-start(f32[256,1024]{1,0:T(8,128)S(1)} %get-tuple-element.44.refs_4_.refs_10_), channel_id=1, source_target_pairs={{1,0},{2,1},{3,2},{4,3},{5,4},{6,5},{7,6},{8,7},{9,8},{10,9},{11,1... | collective-permute-start | bytes 3145736 | tf_op jit(solution)/shard_map/ppermute | solution.py:526
  252.4 2.4 shard_map.62
  254.8 18.2 %collective-permute-start.13 = (f32[8,2048]{1,0:T(8,128)S(1)}, f32[8,2048]{1,0:T(8,128)S(1)}, u32[]{:S(2)}, u32[]{:S(2)}) collective-permute-start(f32[8,2048]{1,0:T(8,128)S(1)} %get-tuple-element.45), channel_id=1, source_target_pairs={{0,16},{1,17},{2,18},{3,19},{4,20},{5,21},{6,22},{7,23},{8,24},{9,... | collective-permute-start | bytes 196616 | tf_op jit(solution)/shard_map/ppermute | solution.py:511
  273.1 0.9 collective-permute-done.13
  274.0 0.1 collective-permute-start.14
  274.1 4.3 %collective-permute-done.14 = f32[8,2048]{1,0:T(8,128)S(1)} collective-permute-done((f32[8,2048]{1,0:T(8,128)S(1)}, f32[8,2048]{1,0:T(8,128)S(1)}, u32[]{:S(2)}, u32[]{:S(2)}) %collective-permute-start.14) | collective-permute-done | bytes 65568 | tf_op jit(solution)/shard_map/ppermute | solution.py:511
  278.4 0.1 collective-permute-start.15
  278.5 5.5 %collective-permute-done.15 = f32[8,2048]{1,0:T(8,128)S(1)} collective-permute-done((f32[8,2048]{1,0:T(8,128)S(1)}, f32[8,2048]{1,0:T(8,128)S(1)}, u32[]{:S(2)}, u32[]{:S(2)}) %collective-permute-start.15) | collective-permute-done | bytes 65568 | tf_op jit(solution)/shard_map/ppermute | solution.py:511
  284.0 0.1 collective-permute-start.16
  284.1 4.3 %collective-permute-done.16 = f32[8,2048]{1,0:T(8,128)S(1)} collective-permute-done((f32[8,2048]{1,0:T(8,128)S(1)}, f32[8,2048]{1,0:T(8,128)S(1)}, u32[]{:S(2)}, u32[]{:S(2)}) %collective-permute-start.16) | collective-permute-done | bytes 65568 | tf_op jit(solution)/shard_map/ppermute | solution.py:511
  288.3 0.1 collective-permute-start.17
  288.4 5.5 %collective-permute-done.17 = f32[8,2048]{1,0:T(8,128)S(1)} collective-permute-done((f32[8,2048]{1,0:T(8,128)S(1)}, f32[8,2048]{1,0:T(8,128)S(1)}, u32[]{:S(2)}, u32[]{:S(2)}) %collective-permute-start.17) | collective-permute-done | bytes 65568 | tf_op jit(solution)/shard_map/ppermute | solution.py:511
  293.9 0.1 collective-permute-start.18
  294.0 4.3 %collective-permute-done.18 = f32[8,2048]{1,0:T(8,128)S(1)} collective-permute-done((f32[8,2048]{1,0:T(8,128)S(1)}, f32[8,2048]{1,0:T(8,128)S(1)}, u32[]{:S(2)}, u32[]{:S(2)}) %collective-permute-start.18) | collective-permute-done | bytes 65568 | tf_op jit(solution)/shard_map/ppermute | solution.py:511
  298.3 0.1 collective-permute-start.19
  298.4 5.5 %collective-permute-done.19 = f32[8,2048]{1,0:T(8,128)S(1)} collective-permute-done((f32[8,2048]{1,0:T(8,128)S(1)}, f32[8,2048]{1,0:T(8,128)S(1)}, u32[]{:S(2)}, u32[]{:S(2)}) %collective-permute-start.19) | collective-permute-done | bytes 65568 | tf_op jit(solution)/shard_map/ppermute | solution.py:511
  303.8 0.0 collective-permute-done.11.refs_9_
  303.9 0.0 collective-permute-done.12.refs_11_
  303.9 5.1 %shard_map.63 = (f32[256,2048]{1,0:T(8,128)}, f32[256,2048]{1,0:T(8,128)}) custom-call(f32[264,384]{1,0:T(8,128)S(1)} %collective-permute-done.lower_ref.refs_0_, f32[256,256]{1,0:T(8,128)S(1)} %get-tuple-element.28.refs_1_, f32[256,2048]{1,0:T(8,128)S(1)} %copy-done, f32[256,2048]{1,0:T(8,128)S(1)} %get-tuple-element.33.refs_3_, ...), custom_call_target="tpu_custom_call" | custom-call | tf_op jit(solution)/shard_map/pallas_call | solution.py:402
  (10 shorter events, 0.1 us)
Async XLA Ops:
  0.6 2.3 copy-start.2
  3.0 0.8 copy-start.4
  3.8 0.7 copy-start.5
  8.8 46.1 %copy-start.3 = (f32[5120,128]{1,0:T(8,128)}, f32[5120,128]{1,0:T(8,128)S(1)}, u32[]{:S(2)}) copy-start(f32[5120,128]{1,0:T(8,128)S(1)} %get-tuple-element.24) | copy-start | bytes 7864324
  54.9 5.9 %copy-start = (f32[256,2048]{1,0:T(8,128)S(1)}, f32[256,2048]{1,0:T(8,128)}, u32[]{:S(2)}) copy-start(f32[256,2048]{1,0:T(8,128)} %refs_2_.1) | copy-start | bytes 6291460
  55.0 46.2 %all-to-all-start = ((f32[128,40,128]{2,1,0:T(8,128)}), f32[128,40,128]{2,1,0:T(8,128)}, u32[]{:S(2)}, u32[]{:S(2)}) async-start(f32[128,40,128]{2,1,0:T(8,128)} %bitcast.8), calls=%async_computation | async-start | bytes 5242880 | tf_op jit(solution)/shard_map/all_to_all | solution.py:536
  61.9 94.0 %collective-permute-start.4 = (f32[128,2048]{1,0:T(8,128)}, f32[128,2048]{1,0:T(8,128)}, u32[]{:S(2)}, u32[]{:S(2)}) collective-permute-start(f32[128,2048]{1,0:T(8,128)} %slice.6), channel_id=1, source_target_pairs={{1,0},{2,1},{3,2},{4,3},{5,4},{6,5},{7,6},{8,7},{9,8},{10,9},{11,1... | collective-permute-start | bytes 3145736 | tf_op jit(solution)/shard_map/ppermute | solution.py:526
  68.8 87.0 %collective-permute-start.3 = (f32[128,2048]{1,0:T(8,128)}, f32[128,2048]{1,0:T(8,128)}, u32[]{:S(2)}, u32[]{:S(2)}) collective-permute-start(f32[128,2048]{1,0:T(8,128)} %slice.6), channel_id=1, source_target_pairs={{0,1},{1,2},{2,3},{3,4},{4,5},{5,6},{6,7},{7,8},{8,9},{9,10},{10,1... | collective-permute-start | bytes 3145736 | tf_op jit(solution)/shard_map/ppermute | solution.py:523
  69.9 97.2 %collective-permute-start.6 = (f32[128,2048]{1,0:T(8,128)}, f32[128,2048]{1,0:T(8,128)}, u32[]{:S(2)}, u32[]{:S(2)}) collective-permute-start(f32[128,2048]{1,0:T(8,128)} %slice.7), channel_id=1, source_target_pairs={{1,0},{2,1},{3,2},{4,3},{5,4},{6,5},{7,6},{8,7},{9,8},{10,9},{11,1... | collective-permute-start | bytes 3145736 | tf_op jit(solution)/shard_map/ppermute | solution.py:526
  77.1 90.0 %collective-permute-start.5 = (f32[128,2048]{1,0:T(8,128)}, f32[128,2048]{1,0:T(8,128)}, u32[]{:S(2)}, u32[]{:S(2)}) collective-permute-start(f32[128,2048]{1,0:T(8,128)} %slice.7), channel_id=1, source_target_pairs={{0,1},{1,2},{2,3},{3,4},{4,5},{5,6},{6,7},{7,8},{8,9},{9,10},{10,1... | collective-permute-start | bytes 3145736 | tf_op jit(solution)/shard_map/ppermute | solution.py:523
  77.1 1.7 copy-start.1
  109.7 31.4 %collective-permute-start = (f32[264,384]{1,0:T(8,128)S(1)}, f32[264,384]{1,0:T(8,128)S(1)}, u32[]{:S(2)}, u32[]{:S(2)}) collective-permute-start(f32[264,384]{1,0:T(8,128)S(1)} %get-tuple-element.27), channel_id=1, source_target_pairs={{0,1},{1,2},{2,3},{3,4},{4,5},{5,6},{6,7},{7,8},{8,9},{9,10},{10,1... | collective-permute-start | bytes 1216520 | tf_op jit(solution)/shard_map/ppermute | solution.py:523
  147.0 12.8 %collective-permute-start.2 = (f32[256,256]{1,0:T(8,128)S(1)}, f32[256,256]{1,0:T(8,128)S(1)}, u32[]{:S(2)}, u32[]{:S(2)}) collective-permute-start(f32[256,256]{1,0:T(8,128)S(1)} %invert.1.refs_2_.refs_0_), channel_id=1, source_target_pairs={{1,0},{2,1},{3,2},{4,3},{5,4},{6,5},{7,6},{8,7},{9,8},{10,9},{11,1... | collective-permute-start | bytes 786440 | tf_op jit(solution)/shard_map/ppermute | solution.py:526
  155.9 11.2 %collective-permute-start.1 = (f32[256,256]{1,0:T(8,128)S(1)}, f32[256,256]{1,0:T(8,128)S(1)}, u32[]{:S(2)}, u32[]{:S(2)}) collective-permute-start(f32[256,256]{1,0:T(8,128)S(1)} %invert.1.refs_2_.refs_0_), channel_id=1, source_target_pairs={{0,1},{1,2},{2,3},{3,4},{4,5},{5,6},{6,7},{7,8},{8,9},{9,10},{10,1... | collective-permute-start | bytes 786440 | tf_op jit(solution)/shard_map/ppermute | solution.py:523
  173.4 44.2 %collective-permute-start.8 = (f32[256,2048]{1,0:T(8,128)S(1)}, f32[256,2048]{1,0:T(8,128)S(1)}, u32[]{:S(2)}, u32[]{:S(2)}) collective-permute-start(f32[256,2048]{1,0:T(8,128)S(1)} %get-tuple-element.34.refs_5_), channel_id=1, source_target_pairs={{1,0},{2,1},{3,2},{4,3},{5,4},{6,5},{7,6},{8,7},{9,8},{10,9},{11,1... | collective-permute-start | bytes 6291464 | tf_op jit(solution)/shard_map/ppermute | solution.py:526
  173.6 44.6 %collective-permute-start.7 = (f32[256,2048]{1,0:T(8,128)S(1)}, f32[256,2048]{1,0:T(8,128)S(1)}, u32[]{:S(2)}, u32[]{:S(2)}) collective-permute-start(f32[256,2048]{1,0:T(8,128)S(1)} %get-tuple-element.34.refs_5_), channel_id=1, source_target_pairs={{0,1},{1,2},{2,3},{3,4},{4,5},{5,6},{6,7},{7,8},{8,9},{9,10},{10,1... | collective-permute-start | bytes 6291464 | tf_op jit(solution)/shard_map/ppermute | solution.py:523
  223.2 22.1 %collective-permute-start.9 = (f32[256,1024]{1,0:T(8,128)S(1)}, f32[256,1024]{1,0:T(8,128)S(1)}, u32[]{:S(2)}, u32[]{:S(2)}) collective-permute-start(f32[256,1024]{1,0:T(8,128)S(1)} %get-tuple-element.43.refs_2_.refs_8_), channel_id=1, source_target_pairs={{1,0},{2,1},{3,2},{4,3},{5,4},{6,5},{7,6},{8,7},{9,8},{10,9},{11,1... | collective-permute-start | bytes 3145736 | tf_op jit(solution)/shard_map/ppermute | solution.py:526
  223.6 21.7 %collective-permute-start.10 = (f32[256,1024]{1,0:T(8,128)S(1)}, f32[256,1024]{1,0:T(8,128)S(1)}, u32[]{:S(2)}, u32[]{:S(2)}) collective-permute-start(f32[256,1024]{1,0:T(8,128)S(1)} %get-tuple-element.44.refs_4_.refs_10_), channel_id=1, source_target_pairs={{0,1},{1,2},{2,3},{3,4},{4,5},{5,6},{6,7},{7,8},{8,9},{9,10},{10,1... | collective-permute-start | bytes 3145736 | tf_op jit(solution)/shard_map/ppermute | solution.py:523
  245.3 58.6 %collective-permute-start.11 = (f32[256,1024]{1,0:T(8,128)S(1)}, f32[256,1024]{1,0:T(8,128)S(1)}, u32[]{:S(2)}, u32[]{:S(2)}) collective-permute-start(f32[256,1024]{1,0:T(8,128)S(1)} %get-tuple-element.43.refs_2_.refs_8_), channel_id=1, source_target_pairs={{0,1},{1,2},{2,3},{3,4},{4,5},{5,6},{6,7},{7,8},{8,9},{9,10},{10,1... | collective-permute-start | bytes 3145736 | tf_op jit(solution)/shard_map/ppermute | solution.py:523
  248.8 55.0 %collective-permute-start.12 = (f32[256,1024]{1,0:T(8,128)S(1)}, f32[256,1024]{1,0:T(8,128)S(1)}, u32[]{:S(2)}, u32[]{:S(2)}) collective-permute-start(f32[256,1024]{1,0:T(8,128)S(1)} %get-tuple-element.44.refs_4_.refs_10_), channel_id=1, source_target_pairs={{1,0},{2,1},{3,2},{4,3},{5,4},{6,5},{7,6},{8,7},{9,8},{10,9},{11,1... | collective-permute-start | bytes 3145736 | tf_op jit(solution)/shard_map/ppermute | solution.py:526
  254.8 19.1 %collective-permute-start.13 = (f32[8,2048]{1,0:T(8,128)S(1)}, f32[8,2048]{1,0:T(8,128)S(1)}, u32[]{:S(2)}, u32[]{:S(2)}) collective-permute-start(f32[8,2048]{1,0:T(8,128)S(1)} %get-tuple-element.45), channel_id=1, source_target_pairs={{0,16},{1,17},{2,18},{3,19},{4,20},{5,21},{6,22},{7,23},{8,24},{9,... | collective-permute-start | bytes 196616 | tf_op jit(solution)/shard_map/ppermute | solution.py:511
  274.0 4.4 %collective-permute-start.14 = (f32[8,2048]{1,0:T(8,128)S(1)}, f32[8,2048]{1,0:T(8,128)S(1)}, u32[]{:S(2)}, u32[]{:S(2)}) collective-permute-start(f32[8,2048]{1,0:T(8,128)S(1)} %add.25), channel_id=1, source_target_pairs={{0,32},{1,33},{2,34},{3,35},{4,36},{5,37},{6,38},{7,39},{8,40},{9,... | collective-permute-start | bytes 196616 | tf_op jit(solution)/shard_map/ppermute | solution.py:511
  278.4 5.6 %collective-permute-start.15 = (f32[8,2048]{1,0:T(8,128)S(1)}, f32[8,2048]{1,0:T(8,128)S(1)}, u32[]{:S(2)}, u32[]{:S(2)}) collective-permute-start(f32[8,2048]{1,0:T(8,128)S(1)} %add.26), channel_id=1, source_target_pairs={{0,96},{1,97},{2,98},{3,99},{4,100},{5,101},{6,102},{7,103},{8,104... | collective-permute-start | bytes 196616 | tf_op jit(solution)/shard_map/ppermute | solution.py:511
  284.0 4.3 %collective-permute-start.16 = (f32[8,2048]{1,0:T(8,128)S(1)}, f32[8,2048]{1,0:T(8,128)S(1)}, u32[]{:S(2)}, u32[]{:S(2)}) collective-permute-start(f32[8,2048]{1,0:T(8,128)S(1)} %add.27), channel_id=1, source_target_pairs={{0,4},{1,5},{2,6},{3,7},{4,0},{5,1},{6,2},{7,3},{8,12},{9,13},{10,... | collective-permute-start | bytes 196616 | tf_op jit(solution)/shard_map/ppermute | solution.py:511
  288.3 5.6 %collective-permute-start.17 = (f32[8,2048]{1,0:T(8,128)S(1)}, f32[8,2048]{1,0:T(8,128)S(1)}, u32[]{:S(2)}, u32[]{:S(2)}) collective-permute-start(f32[8,2048]{1,0:T(8,128)S(1)} %add.28), channel_id=1, source_target_pairs={{0,12},{1,13},{2,14},{3,15},{4,8},{5,9},{6,10},{7,11},{8,4},{9,5},... | collective-permute-start | bytes 196616 | tf_op jit(solution)/shard_map/ppermute | solution.py:511
  293.9 4.3 %collective-permute-start.18 = (f32[8,2048]{1,0:T(8,128)S(1)}, f32[8,2048]{1,0:T(8,128)S(1)}, u32[]{:S(2)}, u32[]{:S(2)}) collective-permute-start(f32[8,2048]{1,0:T(8,128)S(1)} %add.29), channel_id=1, source_target_pairs={{0,1},{1,0},{2,3},{3,2},{4,5},{5,4},{6,7},{7,6},{8,9},{9,8},{10,11... | collective-permute-start | bytes 196616 | tf_op jit(solution)/shard_map/ppermute | solution.py:511
  298.3 5.6 %collective-permute-start.19 = (f32[8,2048]{1,0:T(8,128)S(1)}, f32[8,2048]{1,0:T(8,128)S(1)}, u32[]{:S(2)}, u32[]{:S(2)}) collective-permute-start(f32[8,2048]{1,0:T(8,128)S(1)} %add.30), channel_id=1, source_target_pairs={{0,3},{1,2},{2,1},{3,0},{4,7},{5,6},{6,5},{7,4},{8,11},{9,10},{10,... | collective-permute-start | bytes 196616 | tf_op jit(solution)/shard_map/ppermute | solution.py:511

commit v8 on v7

--- a/solution.py
+++ b/solution.py
@@ -120,7 +120,7 @@
         in_specs=[
             pl.BlockSpec(memory_space=pltpu.VMEM),
             pl.BlockSpec(memory_space=pltpu.VMEM),
-            pl.BlockSpec(memory_space=pltpu.HBM),
+            pl.BlockSpec(memory_space=pl.ANY),
         ],
         scratch_shapes=[
             pltpu.VMEM((8, blocks.shape[0], 128), jnp.float32),
@@ -542,10 +542,12 @@
     got1 = exchange(send1)
     rest, got0 = lax.optimization_barrier((right_side, got0))
     rest = rest[own // 2 :]
-    r_low[1], r_high[1] = from_below(rest), from_above(rest)
+    r_high[1] = from_above(rest)
     part = assemble(base, got0, window)
     center, high_band, lower = assemble(base, got1, window, part)
+    lower, rest = lax.optimization_barrier((lower, rest))
     lower = from_below(lower)
+    r_low[1] = from_below(rest)
     inv = invert(center, lower)
     inv_low, inv_high = from_below(inv), from_above(inv)
     v0 = right_side
@@ -573,9 +575,8 @@
     )
     near_0 = from_above(w2_0)
     near_1 = from_below(w2_1)
-    near_0, near_1, later_0, later_1 = lax.optimization_barrier((near_0, near_1, w2_0, w2_1))
-    far_0 = from_below(later_0)
-    far_1 = from_above(later_1)
+    far_0 = from_below(w2_0)
+    far_1 = from_above(w2_1)
     bands = (lower, high_band)
     t, sums = in_blocks(
         side_kernel, bands, (), (w2_0, near_0), (w2_1, near_1), (sums,), ("whole", "sums"), 2

time: 309 us -> 304 us (0.984)
  waiting for transfers between devices: 133 us -> 123 us
  starting transfers between devices: 59.8 us -> 64.1 us
    ppermute x6, waiting for transfers between devices: 63.3 us -> 56.1 us  [from_above(): return lax.ppermute(x, AXES, down)]
    ppermute x7, waiting for transfers between devices: 39.1 us -> 35.7 us  [from_below(): return lax.ppermute(x, AXES, up)]
  transfers between devices with their start and end apart: 21 -> 21, of which waited for: 13 -> 14; matrix products, arithmetic and copies ran while one was open for 1% -> 1% of each run, Pallas kernels for 13% -> 14%
where the time goes in v8:
time: 304 us
  waiting for transfers between devices  123 us (40%)
  starting transfers between devices  64.1 us (21%)
  Pallas kernels  61.8 us (20%)
  blocking collectives  46.1 us (15%)
  local copies, waits for them, and re-layouts  7.62 us (3%)
    ppermute x6, waiting for transfers between devices, from_above(): return lax.ppermute(x, AXES, down)  56.1 us
    all_to_all x1, blocking collectives, exchange(): lax.all_to_all(send.reshape(devices, ROWS, 128), AXES, split_axis=0, conc...  46.1 us
    ppermute x7, waiting for transfers between devices, from_below(): return lax.ppermute(x, AXES, up)  35.7 us
    pallas_call x2, Pallas kernels, assemble(): pl.pallas_call(lambda *refs: assemble_kernel(last, *refs), out_shape=out,...  30.8 us
    ppermute x7, waiting for transfers between devices, butterfly(): x = x + lax.ppermute(x, AXES, [(i, i ^ bit) for i in range(devices)])  29.7 us
    ppermute x6, starting transfers between devices, from_above(): return lax.ppermute(x, AXES, down)  26.8 us
    ppermute x7, starting transfers between devices, butterfly(): x = x + lax.ppermute(x, AXES, [(i, i ^ bit) for i in range(devices)])  21.3 us
    pallas_call x5, Pallas kernels, in_blocks(): pl.pallas_call(run, grid=(2 * per,), in_specs=[pl.BlockSpec((rows, rows),...  20.7 us
  transfers between devices with their start and end apart: 21, of which 14 were waited for; matrix products, arithmetic and copies ran while one was open for 1% of the time, Pallas kernels for 14%

profile of v8, /device:TPU:0, one launch (start us, length us, event | category | flops | bytes accessed | tf_op | source)
XLA Modules:
  0.0 303.7 jit_solution(15987306657107321866)
XLA Ops:
  0.6 0.0 copy-start.2
  0.6 2.3 copy-done.2
  3.0 0.8 copy-done.4
  3.8 0.7 copy-done.5
  4.4 4.4 %pack.1 = (f32[5120,128]{1,0:T(8,128)S(1)}, f32[5120,128]{1,0:T(8,128)S(1)}) custom-call(s32[1,128]{1,0:T(1,128)S(1)} %bitcast.11, s32[96,128]{1,0:T(8,128)S(1)} %bitcast.10, f32[128,9216]{1,0:T(8,128)S(1)} %copy-done.2), custom_call_target="tpu_custom_call" | custom-call | tf_op jit(solution)/shard_map/pack/pallas_call | solution.py:117
  8.8 0.0 copy-start.3
  8.8 46.1 %all_to_all.10 = f32[128,40,128]{2,1,0:T(8,128)} all-to-all(f32[128,40,128]{2,1,0:T(8,128)S(1)} %bitcast.9), channel_id=1, replica_groups=mesh['row'=8,'col'=16] {'row','col'}, dimensions={0} | all-to-all | bytes 5242880 | tf_op jit(solution)/shard_map/all_to_all | solution.py:536
  54.9 0.0 copy-done.3
  55.0 5.9 %all-to-all-start = ((f32[128,40,128]{2,1,0:T(8,128)}), f32[128,40,128]{2,1,0:T(8,128)}, u32[]{:S(2)}, u32[]{:S(2)}) async-start(f32[128,40,128]{2,1,0:T(8,128)} %bitcast.8), calls=%async_computation | async-start | bytes 5242880 | tf_op jit(solution)/shard_map/all_to_all | solution.py:536
  60.8 0.0 copy-done
  60.8 1.0 slice.7
  61.9 7.0 %collective-permute-start.4 = (f32[128,2048]{1,0:T(8,128)}, f32[128,2048]{1,0:T(8,128)}, u32[]{:S(2)}, u32[]{:S(2)}) collective-permute-start(f32[128,2048]{1,0:T(8,128)} %slice.7), channel_id=1, source_target_pairs={{1,0},{2,1},{3,2},{4,3},{5,4},{6,5},{7,6},{8,7},{9,8},{10,9},{11,1... | collective-permute-start | bytes 3145736 | tf_op jit(solution)/shard_map/ppermute | solution.py:526
  68.8 0.0 collective-permute-start.3
  68.9 0.1 pad_add_fusion.refs_0_
  68.9 1.0 slice.6
  70.0 1.7 copy-done.1
  71.7 22.2 %assemble_first.1.refs_2_ = f32[512,512]{1,0:T(8,128)S(1)} custom-call(s32[2]{0:T(128)S(1)} %pad_add_fusion.refs_0_, f32[5120,128]{1,0:T(8,128)S(1)} %bitcast.7), custom_call_target="tpu_custom_call" | custom-call | tf_op jit(solution)/shard_map/assemble_first/pallas_call | solution.py:282
  94.0 1.7 all-to-all-done
  95.6 8.6 %assemble_last.1 = (f32[256,256]{1,0:T(8,128)S(1)}, f32[256,256]{1,0:T(8,128)S(1)}, f32[264,384]{1,0:T(8,128)S(1)}) custom-call(s32[2]{0:T(128)S(1)} %pad_add_fusion.refs_0_, f32[5120,128]{1,0:T(8,128)} %bitcast.4.refs_1_, f32[512,512]{1,0:T(8,128)S(1)} %assemble_first.1.refs_2_), custom_call_target="tpu_custom_call" | custom-call | tf_op jit(solution)/shard_map/assemble_last/pallas_call | solution.py:282
  104.2 0.0 copy-done.6
  104.2 4.0 %collective-permute-start.5 = (f32[128,2048]{1,0:T(8,128)S(1)}, f32[128,2048]{1,0:T(8,128)S(1)}, u32[]{:S(2)}, u32[]{:S(2)}) collective-permute-start(f32[128,2048]{1,0:T(8,128)S(1)} %copy-done.6), channel_id=1, source_target_pairs={{0,1},{1,2},{2,3},{3,4},{4,5},{5,6},{6,7},{7,8},{8,9},{9,10},{10,1... | collective-permute-start | bytes 3145736 | tf_op jit(solution)/shard_map/ppermute | solution.py:523
  108.2 5.1 %collective-permute-start.6 = (f32[128,2048]{1,0:T(8,128)S(1)}, f32[128,2048]{1,0:T(8,128)S(1)}, u32[]{:S(2)}, u32[]{:S(2)}) collective-permute-start(f32[128,2048]{1,0:T(8,128)S(1)} %copy-done.6), channel_id=1, source_target_pairs={{1,0},{2,1},{3,2},{4,3},{5,4},{6,5},{7,6},{8,7},{9,8},{10,9},{11,1... | collective-permute-start | bytes 3145736 | tf_op jit(solution)/shard_map/ppermute | solution.py:526
  113.3 0.0 collective-permute-start
  113.3 27.8 %collective-permute-done.lower_ref.refs_0_ = f32[264,384]{1,0:T(8,128)S(1)} collective-permute-done((f32[264,384]{1,0:T(8,128)S(1)}, f32[264,384]{1,0:T(8,128)S(1)}, u32[]{:S(2)}, u32[]{:S(2)}) %collective-permute-start) | collective-permute-done | bytes 405536 | tf_op jit(solution)/shard_map/ppermute | solution.py:523
  141.1 5.9 %invert.1.refs_2_.refs_0_ = f32[256,256]{1,0:T(8,128)S(1)} custom-call(f32[256,256]{1,0:T(8,128)S(1)} %get-tuple-element.29.upper_ref, f32[264,384]{1,0:T(8,128)S(1)} %collective-permute-done.lower_ref.refs_0_), custom_call_target="tpu_custom_call" | custom-call | tf_op jit(solution)/shard_map/invert/pallas_call | solution.py:336
  147.0 8.9 %collective-permute-start.2 = (f32[256,256]{1,0:T(8,128)S(1)}, f32[256,256]{1,0:T(8,128)S(1)}, u32[]{:S(2)}, u32[]{:S(2)}) collective-permute-start(f32[256,256]{1,0:T(8,128)S(1)} %invert.1.refs_2_.refs_0_), channel_id=1, source_target_pairs={{1,0},{2,1},{3,2},{4,3},{5,4},{6,5},{7,6},{8,7},{9,8},{10,9},{11,1... | collective-permute-start | bytes 786440 | tf_op jit(solution)/shard_map/ppermute | solution.py:526
  155.9 0.0 collective-permute-done.4.refs_6_
  155.9 0.0 collective-permute-start.1
  155.9 0.0 collective-permute-done.3.refs_5_
  155.9 3.9 %collective-permute-done.2.refs_4_ = f32[256,256]{1,0:T(8,128)S(1)} collective-permute-done((f32[256,256]{1,0:T(8,128)S(1)}, f32[256,256]{1,0:T(8,128)S(1)}, u32[]{:S(2)}, u32[]{:S(2)}) %collective-permute-start.2) | collective-permute-done | bytes 262176 | tf_op jit(solution)/shard_map/ppermute | solution.py:526
  159.8 7.3 %collective-permute-done.1.refs_3_ = f32[256,256]{1,0:T(8,128)S(1)} collective-permute-done((f32[256,256]{1,0:T(8,128)S(1)}, f32[256,256]{1,0:T(8,128)S(1)}, u32[]{:S(2)}, u32[]{:S(2)}) %collective-permute-start.1) | collective-permute-done | bytes 262176 | tf_op jit(solution)/shard_map/ppermute | solution.py:523
  167.1 0.0 collective-permute-done.5.refs_7_
  167.1 0.0 collective-permute-done.6.refs_8_
  167.1 6.0 %shard_map.59 = (f32[256,2048]{1,0:T(8,128)S(1)}, f32[256,2048]{1,0:T(8,128)S(1)}, f32[8,2048]{1,0:T(8,128)S(1)}) custom-call(f32[264,384]{1,0:T(8,128)S(1)} %collective-permute-done.lower_ref.refs_0_, f32[256,256]{1,0:T(8,128)S(1)} %get-tuple-element.28.refs_1_, f32[256,256]{1,0:T(8,128)S(1)} %invert.1.refs_2_.refs_0_, ...), custom_call_target="tpu_custom_call" | custom-call | tf_op jit(solution)/shard_map/pallas_call | solution.py:402
  173.2 0.2 collective-permute-start.8
  173.3 1.9 collective-permute-start.7
  175.3 2.1 shard_map.60
  177.4 39.9 %collective-permute-done.8.refs_4_ = f32[256,2048]{1,0:T(8,128)S(1)} collective-permute-done((f32[256,2048]{1,0:T(8,128)S(1)}, f32[256,2048]{1,0:T(8,128)S(1)}, u32[]{:S(2)}, u32[]{:S(2)}) %collective-permute-start.8) | collective-permute-done | bytes 2097184 | tf_op jit(solution)/shard_map/ppermute | solution.py:526
  217.3 0.6 collective-permute-done.7.refs_3_
  217.9 5.0 %shard_map.61 = (f32[256,2048]{1,0:T(8,128)S(1)}, f32[256,1024]{1,0:T(8,128)S(1)}, f32[256,1024]{1,0:T(8,128)S(1)}, f32[8,2048]{1,0:T(8,128)S(1)}) custom-call(f32[264,384]{1,0:T(8,128)S(1)} %collective-permute-done.lower_ref.refs_0_, f32[256,256]{1,0:T(8,128)S(1)} %get-tuple-element.28.refs_1_, f32[256,256]{1,0:T(8,128)S(1)} %invert.1.refs_2_.refs_0_, ...), custom_call_target="tpu_custom_call" | custom-call | tf_op jit(solution)/shard_map/pallas_call | solution.py:402
  222.9 0.4 collective-permute-start.9
  223.3 2.2 collective-permute-start.10
  225.6 1.9 collective-permute-start.11
  227.5 5.2 %collective-permute-start.12 = (f32[256,1024]{1,0:T(8,128)S(1)}, f32[256,1024]{1,0:T(8,128)S(1)}, u32[]{:S(2)}, u32[]{:S(2)}) collective-permute-start(f32[256,1024]{1,0:T(8,128)S(1)} %get-tuple-element.38.refs_4_.refs_10_), channel_id=1, source_target_pairs={{1,0},{2,1},{3,2},{4,3},{5,4},{6,5},{7,6},{8,7},{9,8},{10,9},{11,1... | collective-permute-start | bytes 3145736 | tf_op jit(solution)/shard_map/ppermute | solution.py:526
  232.8 12.3 %collective-permute-done.9.refs_3_ = f32[256,1024]{1,0:T(8,128)S(1)} collective-permute-done((f32[256,1024]{1,0:T(8,128)S(1)}, f32[256,1024]{1,0:T(8,128)S(1)}, u32[]{:S(2)}, u32[]{:S(2)}) %collective-permute-start.9) | collective-permute-done | bytes 1048608 | tf_op jit(solution)/shard_map/ppermute | solution.py:526
  245.0 0.0 collective-permute-done.10.refs_5_
  245.0 2.4 shard_map.62
  247.4 20.3 %collective-permute-start.13 = (f32[8,2048]{1,0:T(8,128)S(1)}, f32[8,2048]{1,0:T(8,128)S(1)}, u32[]{:S(2)}, u32[]{:S(2)}) collective-permute-start(f32[8,2048]{1,0:T(8,128)S(1)} %get-tuple-element.41), channel_id=1, source_target_pairs={{0,16},{1,17},{2,18},{3,19},{4,20},{5,21},{6,22},{7,23},{8,24},{9,... | collective-permute-start | bytes 196616 | tf_op jit(solution)/shard_map/ppermute | solution.py:511
  267.8 0.9 collective-permute-done.13
  268.7 0.1 collective-permute-start.14
  268.8 4.3 %collective-permute-done.14 = f32[8,2048]{1,0:T(8,128)S(1)} collective-permute-done((f32[8,2048]{1,0:T(8,128)S(1)}, f32[8,2048]{1,0:T(8,128)S(1)}, u32[]{:S(2)}, u32[]{:S(2)}) %collective-permute-start.14) | collective-permute-done | bytes 65568 | tf_op jit(solution)/shard_map/ppermute | solution.py:511
  273.1 0.5 collective-permute-start.15
  273.7 5.0 %collective-permute-done.15 = f32[8,2048]{1,0:T(8,128)S(1)} collective-permute-done((f32[8,2048]{1,0:T(8,128)S(1)}, f32[8,2048]{1,0:T(8,128)S(1)}, u32[]{:S(2)}, u32[]{:S(2)}) %collective-permute-start.15) | collective-permute-done | bytes 65568 | tf_op jit(solution)/shard_map/ppermute | solution.py:511
  278.7 0.1 collective-permute-start.16
  278.8 4.3 %collective-permute-done.16 = f32[8,2048]{1,0:T(8,128)S(1)} collective-permute-done((f32[8,2048]{1,0:T(8,128)S(1)}, f32[8,2048]{1,0:T(8,128)S(1)}, u32[]{:S(2)}, u32[]{:S(2)}) %collective-permute-start.16) | collective-permute-done | bytes 65568 | tf_op jit(solution)/shard_map/ppermute | solution.py:511
  283.1 0.1 collective-permute-start.17
  283.2 5.5 %collective-permute-done.17 = f32[8,2048]{1,0:T(8,128)S(1)} collective-permute-done((f32[8,2048]{1,0:T(8,128)S(1)}, f32[8,2048]{1,0:T(8,128)S(1)}, u32[]{:S(2)}, u32[]{:S(2)}) %collective-permute-start.17) | collective-permute-done | bytes 65568 | tf_op jit(solution)/shard_map/ppermute | solution.py:511
  288.6 0.1 collective-permute-start.18
  288.7 4.3 %collective-permute-done.18 = f32[8,2048]{1,0:T(8,128)S(1)} collective-permute-done((f32[8,2048]{1,0:T(8,128)S(1)}, f32[8,2048]{1,0:T(8,128)S(1)}, u32[]{:S(2)}, u32[]{:S(2)}) %collective-permute-start.18) | collective-permute-done | bytes 65568 | tf_op jit(solution)/shard_map/ppermute | solution.py:511
  293.0 0.1 collective-permute-start.19
  293.1 5.5 %collective-permute-done.19 = f32[8,2048]{1,0:T(8,128)S(1)} collective-permute-done((f32[8,2048]{1,0:T(8,128)S(1)}, f32[8,2048]{1,0:T(8,128)S(1)}, u32[]{:S(2)}, u32[]{:S(2)}) %collective-permute-start.19) | collective-permute-done | bytes 65568 | tf_op jit(solution)/shard_map/ppermute | solution.py:511
  298.6 0.0 collective-permute-done.11.refs_9_
  298.6 0.0 collective-permute-done.12.refs_11_
  298.6 5.1 %shard_map.63 = (f32[256,2048]{1,0:T(8,128)}, f32[256,2048]{1,0:T(8,128)}) custom-call(f32[264,384]{1,0:T(8,128)S(1)} %collective-permute-done.lower_ref.refs_0_, f32[256,256]{1,0:T(8,128)S(1)} %get-tuple-element.28.refs_1_, f32[256,2048]{1,0:T(8,128)S(1)} %copy-done, f32[256,2048]{1,0:T(8,128)S(1)} %get-tuple-element.33.refs_3_, ...), custom_call_target="tpu_custom_call" | custom-call | tf_op jit(solution)/shard_map/pallas_call | solution.py:402
  (12 shorter events, 0.1 us)
Async XLA Ops:
  0.6 2.3 copy-start.2
  3.0 0.8 copy-start.4
  3.8 0.7 copy-start.5
  8.8 46.1 %copy-start.3 = (f32[5120,128]{1,0:T(8,128)}, f32[5120,128]{1,0:T(8,128)S(1)}, u32[]{:S(2)}) copy-start(f32[5120,128]{1,0:T(8,128)S(1)} %get-tuple-element.22) | copy-start | bytes 7864324
  54.9 5.9 %copy-start = (f32[256,2048]{1,0:T(8,128)S(1)}, f32[256,2048]{1,0:T(8,128)}, u32[]{:S(2)}) copy-start(f32[256,2048]{1,0:T(8,128)} %refs_2_.1) | copy-start | bytes 6291460
  55.0 40.7 %all-to-all-start = ((f32[128,40,128]{2,1,0:T(8,128)}), f32[128,40,128]{2,1,0:T(8,128)}, u32[]{:S(2)}, u32[]{:S(2)}) async-start(f32[128,40,128]{2,1,0:T(8,128)} %bitcast.8), calls=%async_computation | async-start | bytes 5242880 | tf_op jit(solution)/shard_map/all_to_all | solution.py:536
  61.9 94.0 %collective-permute-start.4 = (f32[128,2048]{1,0:T(8,128)}, f32[128,2048]{1,0:T(8,128)}, u32[]{:S(2)}, u32[]{:S(2)}) collective-permute-start(f32[128,2048]{1,0:T(8,128)} %slice.7), channel_id=1, source_target_pairs={{1,0},{2,1},{3,2},{4,3},{5,4},{6,5},{7,6},{8,7},{9,8},{10,9},{11,1... | collective-permute-start | bytes 3145736 | tf_op jit(solution)/shard_map/ppermute | solution.py:526
  68.8 87.0 %collective-permute-start.3 = (f32[128,2048]{1,0:T(8,128)}, f32[128,2048]{1,0:T(8,128)}, u32[]{:S(2)}, u32[]{:S(2)}) collective-permute-start(f32[128,2048]{1,0:T(8,128)} %slice.7), channel_id=1, source_target_pairs={{0,1},{1,2},{2,3},{3,4},{4,5},{5,6},{6,7},{7,8},{8,9},{9,10},{10,1... | collective-permute-start | bytes 3145736 | tf_op jit(solution)/shard_map/ppermute | solution.py:523
  70.0 1.7 copy-start.1
  95.6 8.6 %copy-start.6 = (f32[128,2048]{1,0:T(8,128)S(1)}, f32[128,2048]{1,0:T(8,128)}, u32[]{:S(2)}) copy-start(f32[128,2048]{1,0:T(8,128)} %slice.6) | copy-start | bytes 3145732
  104.2 62.9 %collective-permute-start.5 = (f32[128,2048]{1,0:T(8,128)S(1)}, f32[128,2048]{1,0:T(8,128)S(1)}, u32[]{:S(2)}, u32[]{:S(2)}) collective-permute-start(f32[128,2048]{1,0:T(8,128)S(1)} %copy-done.6), channel_id=1, source_target_pairs={{0,1},{1,2},{2,3},{3,4},{4,5},{5,6},{6,7},{7,8},{8,9},{9,10},{10,1... | collective-permute-start | bytes 3145736 | tf_op jit(solution)/shard_map/ppermute | solution.py:523
  108.2 58.9 %collective-permute-start.6 = (f32[128,2048]{1,0:T(8,128)S(1)}, f32[128,2048]{1,0:T(8,128)S(1)}, u32[]{:S(2)}, u32[]{:S(2)}) collective-permute-start(f32[128,2048]{1,0:T(8,128)S(1)} %copy-done.6), channel_id=1, source_target_pairs={{1,0},{2,1},{3,2},{4,3},{5,4},{6,5},{7,6},{8,7},{9,8},{10,9},{11,1... | collective-permute-start | bytes 3145736 | tf_op jit(solution)/shard_map/ppermute | solution.py:526
  113.3 27.8 %collective-permute-start = (f32[264,384]{1,0:T(8,128)S(1)}, f32[264,384]{1,0:T(8,128)S(1)}, u32[]{:S(2)}, u32[]{:S(2)}) collective-permute-start(f32[264,384]{1,0:T(8,128)S(1)} %get-tuple-element.27), channel_id=1, source_target_pairs={{0,1},{1,2},{2,3},{3,4},{4,5},{5,6},{6,7},{7,8},{8,9},{9,10},{10,1... | collective-permute-start | bytes 1216520 | tf_op jit(solution)/shard_map/ppermute | solution.py:523
  147.0 12.8 %collective-permute-start.2 = (f32[256,256]{1,0:T(8,128)S(1)}, f32[256,256]{1,0:T(8,128)S(1)}, u32[]{:S(2)}, u32[]{:S(2)}) collective-permute-start(f32[256,256]{1,0:T(8,128)S(1)} %invert.1.refs_2_.refs_0_), channel_id=1, source_target_pairs={{1,0},{2,1},{3,2},{4,3},{5,4},{6,5},{7,6},{8,7},{9,8},{10,9},{11,1... | collective-permute-start | bytes 786440 | tf_op jit(solution)/shard_map/ppermute | solution.py:526
  155.9 11.2 %collective-permute-start.1 = (f32[256,256]{1,0:T(8,128)S(1)}, f32[256,256]{1,0:T(8,128)S(1)}, u32[]{:S(2)}, u32[]{:S(2)}) collective-permute-start(f32[256,256]{1,0:T(8,128)S(1)} %invert.1.refs_2_.refs_0_), channel_id=1, source_target_pairs={{0,1},{1,2},{2,3},{3,4},{4,5},{5,6},{6,7},{7,8},{8,9},{9,10},{10,1... | collective-permute-start | bytes 786440 | tf_op jit(solution)/shard_map/ppermute | solution.py:523
  173.2 44.2 %collective-permute-start.8 = (f32[256,2048]{1,0:T(8,128)S(1)}, f32[256,2048]{1,0:T(8,128)S(1)}, u32[]{:S(2)}, u32[]{:S(2)}) collective-permute-start(f32[256,2048]{1,0:T(8,128)S(1)} %get-tuple-element.34.refs_5_), channel_id=1, source_target_pairs={{1,0},{2,1},{3,2},{4,3},{5,4},{6,5},{7,6},{8,7},{9,8},{10,9},{11,1... | collective-permute-start | bytes 6291464 | tf_op jit(solution)/shard_map/ppermute | solution.py:526
  173.3 44.6 %collective-permute-start.7 = (f32[256,2048]{1,0:T(8,128)S(1)}, f32[256,2048]{1,0:T(8,128)S(1)}, u32[]{:S(2)}, u32[]{:S(2)}) collective-permute-start(f32[256,2048]{1,0:T(8,128)S(1)} %get-tuple-element.34.refs_5_), channel_id=1, source_target_pairs={{0,1},{1,2},{2,3},{3,4},{4,5},{5,6},{6,7},{7,8},{8,9},{9,10},{10,1... | collective-permute-start | bytes 6291464 | tf_op jit(solution)/shard_map/ppermute | solution.py:523
  222.9 22.1 %collective-permute-start.9 = (f32[256,1024]{1,0:T(8,128)S(1)}, f32[256,1024]{1,0:T(8,128)S(1)}, u32[]{:S(2)}, u32[]{:S(2)}) collective-permute-start(f32[256,1024]{1,0:T(8,128)S(1)} %get-tuple-element.37.refs_2_.refs_8_), channel_id=1, source_target_pairs={{1,0},{2,1},{3,2},{4,3},{5,4},{6,5},{7,6},{8,7},{9,8},{10,9},{11,1... | collective-permute-start | bytes 3145736 | tf_op jit(solution)/shard_map/ppermute | solution.py:526
  223.3 21.7 %collective-permute-start.10 = (f32[256,1024]{1,0:T(8,128)S(1)}, f32[256,1024]{1,0:T(8,128)S(1)}, u32[]{:S(2)}, u32[]{:S(2)}) collective-permute-start(f32[256,1024]{1,0:T(8,128)S(1)} %get-tuple-element.38.refs_4_.refs_10_), channel_id=1, source_target_pairs={{0,1},{1,2},{2,3},{3,4},{4,5},{5,6},{6,7},{7,8},{8,9},{9,10},{10,1... | collective-permute-start | bytes 3145736 | tf_op jit(solution)/shard_map/ppermute | solution.py:523
  225.6 73.0 %collective-permute-start.11 = (f32[256,1024]{1,0:T(8,128)S(1)}, f32[256,1024]{1,0:T(8,128)S(1)}, u32[]{:S(2)}, u32[]{:S(2)}) collective-permute-start(f32[256,1024]{1,0:T(8,128)S(1)} %get-tuple-element.37.refs_2_.refs_8_), channel_id=1, source_target_pairs={{0,1},{1,2},{2,3},{3,4},{4,5},{5,6},{6,7},{7,8},{8,9},{9,10},{10,1... | collective-permute-start | bytes 3145736 | tf_op jit(solution)/shard_map/ppermute | solution.py:523
  227.5 71.1 %collective-permute-start.12 = (f32[256,1024]{1,0:T(8,128)S(1)}, f32[256,1024]{1,0:T(8,128)S(1)}, u32[]{:S(2)}, u32[]{:S(2)}) collective-permute-start(f32[256,1024]{1,0:T(8,128)S(1)} %get-tuple-element.38.refs_4_.refs_10_), channel_id=1, source_target_pairs={{1,0},{2,1},{3,2},{4,3},{5,4},{6,5},{7,6},{8,7},{9,8},{10,9},{11,1... | collective-permute-start | bytes 3145736 | tf_op jit(solution)/shard_map/ppermute | solution.py:526
  247.4 21.2 %collective-permute-start.13 = (f32[8,2048]{1,0:T(8,128)S(1)}, f32[8,2048]{1,0:T(8,128)S(1)}, u32[]{:S(2)}, u32[]{:S(2)}) collective-permute-start(f32[8,2048]{1,0:T(8,128)S(1)} %get-tuple-element.41), channel_id=1, source_target_pairs={{0,16},{1,17},{2,18},{3,19},{4,20},{5,21},{6,22},{7,23},{8,24},{9,... | collective-permute-start | bytes 196616 | tf_op jit(solution)/shard_map/ppermute | solution.py:511
  268.7 4.4 %collective-permute-start.14 = (f32[8,2048]{1,0:T(8,128)S(1)}, f32[8,2048]{1,0:T(8,128)S(1)}, u32[]{:S(2)}, u32[]{:S(2)}) collective-permute-start(f32[8,2048]{1,0:T(8,128)S(1)} %add.25), channel_id=1, source_target_pairs={{0,32},{1,33},{2,34},{3,35},{4,36},{5,37},{6,38},{7,39},{8,40},{9,... | collective-permute-start | bytes 196616 | tf_op jit(solution)/shard_map/ppermute | solution.py:511
  273.1 5.6 %collective-permute-start.15 = (f32[8,2048]{1,0:T(8,128)S(1)}, f32[8,2048]{1,0:T(8,128)S(1)}, u32[]{:S(2)}, u32[]{:S(2)}) collective-permute-start(f32[8,2048]{1,0:T(8,128)S(1)} %add.26), channel_id=1, source_target_pairs={{0,96},{1,97},{2,98},{3,99},{4,100},{5,101},{6,102},{7,103},{8,104... | collective-permute-start | bytes 196616 | tf_op jit(solution)/shard_map/ppermute | solution.py:511
  278.7 4.3 %collective-permute-start.16 = (f32[8,2048]{1,0:T(8,128)S(1)}, f32[8,2048]{1,0:T(8,128)S(1)}, u32[]{:S(2)}, u32[]{:S(2)}) collective-permute-start(f32[8,2048]{1,0:T(8,128)S(1)} %add.27), channel_id=1, source_target_pairs={{0,4},{1,5},{2,6},{3,7},{4,0},{5,1},{6,2},{7,3},{8,12},{9,13},{10,... | collective-permute-start | bytes 196616 | tf_op jit(solution)/shard_map/ppermute | solution.py:511
  283.1 5.6 %collective-permute-start.17 = (f32[8,2048]{1,0:T(8,128)S(1)}, f32[8,2048]{1,0:T(8,128)S(1)}, u32[]{:S(2)}, u32[]{:S(2)}) collective-permute-start(f32[8,2048]{1,0:T(8,128)S(1)} %add.28), channel_id=1, source_target_pairs={{0,12},{1,13},{2,14},{3,15},{4,8},{5,9},{6,10},{7,11},{8,4},{9,5},... | collective-permute-start | bytes 196616 | tf_op jit(solution)/shard_map/ppermute | solution.py:511
  288.6 4.3 %collective-permute-start.18 = (f32[8,2048]{1,0:T(8,128)S(1)}, f32[8,2048]{1,0:T(8,128)S(1)}, u32[]{:S(2)}, u32[]{:S(2)}) collective-permute-start(f32[8,2048]{1,0:T(8,128)S(1)} %add.29), channel_id=1, source_target_pairs={{0,1},{1,0},{2,3},{3,2},{4,5},{5,4},{6,7},{7,6},{8,9},{9,8},{10,11... | collective-permute-start | bytes 196616 | tf_op jit(solution)/shard_map/ppermute | solution.py:511
  293.0 5.6 %collective-permute-start.19 = (f32[8,2048]{1,0:T(8,128)S(1)}, f32[8,2048]{1,0:T(8,128)S(1)}, u32[]{:S(2)}, u32[]{:S(2)}) collective-permute-start(f32[8,2048]{1,0:T(8,128)S(1)} %add.30), channel_id=1, source_target_pairs={{0,3},{1,2},{2,1},{3,0},{4,7},{5,6},{6,5},{7,4},{8,11},{9,10},{10,... | collective-permute-start | bytes 196616 | tf_op jit(solution)/shard_map/ppermute | solution.py:511

commit v9 on v8

--- a/solution.py
+++ b/solution.py
@@ -527,7 +527,7 @@
 
     base = jnp.stack([lax.axis_index(AXES) * own, own * devices]).astype(jnp.int32)
     r_low, r_high = {}, {}
-    start = right_side[: own // 2]
+    start = right_side[: own * 5 // 8]
     r_low[0] = from_below(start)
     r_high[0] = from_above(start)
     send0, send1 = pack(owner_map, connect.T, blocks, devices)
@@ -541,13 +541,11 @@
     got0 = exchange(send0)
     got1 = exchange(send1)
     rest, got0 = lax.optimization_barrier((right_side, got0))
-    rest = rest[own // 2 :]
-    r_high[1] = from_above(rest)
+    rest = rest[own * 5 // 8 :]
+    r_low[1], r_high[1] = from_below(rest), from_above(rest)
     part = assemble(base, got0, window)
     center, high_band, lower = assemble(base, got1, window, part)
-    lower, rest = lax.optimization_barrier((lower, rest))
     lower = from_below(lower)
-    r_low[1] = from_below(rest)
     inv = invert(center, lower)
     inv_low, inv_high = from_below(inv), from_above(inv)
     v0 = right_side

time: 304 us -> 304 us (level)
    ppermute x7, starting transfers between devices: 10.1 us -> 6.36 us  [from_below(): return lax.ppermute(x, AXES, up)]
    ppermute x7, waiting for transfers between devices: 35.7 us -> 39.1 us  [from_below(): return lax.ppermute(x, AXES, up)]
  transfers between devices with their start and end apart: 21 -> 21, of which waited for: 14 -> 13; matrix products, arithmetic and copies ran while one was open for 1% -> 1% of each run, Pallas kernels for 14% -> 14%
where the time goes in v9:
time: 304 us
  waiting for transfers between devices  125 us (41%)
  starting transfers between devices  62.4 us (21%)
  Pallas kernels  61.9 us (20%)
  blocking collectives  46.1 us (15%)
  local copies, waits for them, and re-layouts  7.61 us (3%)
    ppermute x6, waiting for transfers between devices, from_above(): return lax.ppermute(x, AXES, down)  56.1 us
    all_to_all x1, blocking collectives, exchange(): lax.all_to_all(send.reshape(devices, ROWS, 128), AXES, split_axis=0, conc...  46.1 us
    ppermute x7, waiting for transfers between devices, from_below(): return lax.ppermute(x, AXES, up)  39.1 us
    pallas_call x2, Pallas kernels, assemble(): pl.pallas_call(lambda *refs: assemble_kernel(last, *refs), out_shape=out,...  30.8 us
    ppermute x7, waiting for transfers between devices, butterfly(): x = x + lax.ppermute(x, AXES, [(i, i ^ bit) for i in range(devices)])  29.7 us
    ppermute x6, starting transfers between devices, from_above(): return lax.ppermute(x, AXES, down)  28.8 us
    ppermute x7, starting transfers between devices, butterfly(): x = x + lax.ppermute(x, AXES, [(i, i ^ bit) for i in range(devices)])  21.3 us
    pallas_call x5, Pallas kernels, in_blocks(): pl.pallas_call(run, grid=(2 * per,), in_specs=[pl.BlockSpec((rows, rows),...  20.9 us
  transfers between devices with their start and end apart: 21, of which 13 were waited for; matrix products, arithmetic and copies ran while one was open for 1% of the time, Pallas kernels for 14%

profile of v9, /device:TPU:0, one launch (start us, length us, event | category | flops | bytes accessed | tf_op | source)
XLA Modules:
  0.0 303.9 jit_solution(5927364614929590468)
XLA Ops:
  0.6 0.0 copy-start.2
  0.6 2.3 copy-done.2
  3.0 0.0 copy-start.4
  3.0 0.8 copy-done.4
  3.8 0.7 copy-done.5
  4.4 4.4 %pack.1 = (f32[5120,128]{1,0:T(8,128)S(1)}, f32[5120,128]{1,0:T(8,128)S(1)}) custom-call(s32[1,128]{1,0:T(1,128)S(1)} %bitcast.11, s32[96,128]{1,0:T(8,128)S(1)} %bitcast.10, f32[128,9216]{1,0:T(8,128)S(1)} %copy-done.2), custom_call_target="tpu_custom_call" | custom-call | tf_op jit(solution)/shard_map/pack/pallas_call | solution.py:117
  8.8 0.0 copy-start.3
  8.8 46.1 %all_to_all.10 = f32[128,40,128]{2,1,0:T(8,128)} all-to-all(f32[128,40,128]{2,1,0:T(8,128)S(1)} %bitcast.9), channel_id=1, replica_groups=mesh['row'=8,'col'=16] {'row','col'}, dimensions={0} | all-to-all | bytes 5242880 | tf_op jit(solution)/shard_map/all_to_all | solution.py:536
  54.9 0.0 copy-done.3
  55.0 5.9 %all-to-all-start = ((f32[128,40,128]{2,1,0:T(8,128)}), f32[128,40,128]{2,1,0:T(8,128)}, u32[]{:S(2)}, u32[]{:S(2)}) async-start(f32[128,40,128]{2,1,0:T(8,128)} %bitcast.8), calls=%async_computation | async-start | bytes 5242880 | tf_op jit(solution)/shard_map/all_to_all | solution.py:536
  60.8 0.0 copy-done
  60.8 1.1 slice.6
  62.0 7.0 %collective-permute-start.4 = (f32[160,2048]{1,0:T(8,128)}, f32[160,2048]{1,0:T(8,128)}, u32[]{:S(2)}, u32[]{:S(2)}) collective-permute-start(f32[160,2048]{1,0:T(8,128)} %slice.6), channel_id=1, source_target_pairs={{1,0},{2,1},{3,2},{4,3},{5,4},{6,5},{7,6},{8,7},{9,8},{10,9},{11,1... | collective-permute-start | bytes 3932168 | tf_op jit(solution)/shard_map/ppermute | solution.py:526
  68.9 0.0 collective-permute-start.3
  68.9 0.9 slice.7
  69.9 7.2 %collective-permute-start.6 = (f32[96,2048]{1,0:T(8,128)}, f32[96,2048]{1,0:T(8,128)}, u32[]{:S(2)}, u32[]{:S(2)}) collective-permute-start(f32[96,2048]{1,0:T(8,128)} %slice.7), channel_id=1, source_target_pairs={{1,0},{2,1},{3,2},{4,3},{5,4},{6,5},{7,6},{8,7},{9,8},{10,9},{11,1... | collective-permute-start | bytes 2359304 | tf_op jit(solution)/shard_map/ppermute | solution.py:526
  77.1 0.0 collective-permute-start.5
  77.1 0.1 pad_add_fusion.refs_0_
  77.1 1.7 copy-done.1
  78.9 22.2 %assemble_first.1.refs_2_ = f32[512,512]{1,0:T(8,128)S(1)} custom-call(s32[2]{0:T(128)S(1)} %pad_add_fusion.refs_0_, f32[5120,128]{1,0:T(8,128)S(1)} %bitcast.7), custom_call_target="tpu_custom_call" | custom-call | tf_op jit(solution)/shard_map/assemble_first/pallas_call | solution.py:282
  101.1 0.0 all-to-all-done
  101.1 8.5 %assemble_last.1 = (f32[256,256]{1,0:T(8,128)S(1)}, f32[256,256]{1,0:T(8,128)S(1)}, f32[264,384]{1,0:T(8,128)S(1)}) custom-call(s32[2]{0:T(128)S(1)} %pad_add_fusion.refs_0_, f32[5120,128]{1,0:T(8,128)} %bitcast.4.refs_1_, f32[512,512]{1,0:T(8,128)S(1)} %assemble_first.1.refs_2_), custom_call_target="tpu_custom_call" | custom-call | tf_op jit(solution)/shard_map/assemble_last/pallas_call | solution.py:282
  109.7 0.3 collective-permute-start
  109.9 31.2 %collective-permute-done.lower_ref.refs_0_ = f32[264,384]{1,0:T(8,128)S(1)} collective-permute-done((f32[264,384]{1,0:T(8,128)S(1)}, f32[264,384]{1,0:T(8,128)S(1)}, u32[]{:S(2)}, u32[]{:S(2)}) %collective-permute-start) | collective-permute-done | bytes 405536 | tf_op jit(solution)/shard_map/ppermute | solution.py:523
  141.1 5.9 %invert.1.refs_2_.refs_0_ = f32[256,256]{1,0:T(8,128)S(1)} custom-call(f32[256,256]{1,0:T(8,128)S(1)} %get-tuple-element.25.upper_ref, f32[264,384]{1,0:T(8,128)S(1)} %collective-permute-done.lower_ref.refs_0_), custom_call_target="tpu_custom_call" | custom-call | tf_op jit(solution)/shard_map/invert/pallas_call | solution.py:336
  147.0 8.9 %collective-permute-start.2 = (f32[256,256]{1,0:T(8,128)S(1)}, f32[256,256]{1,0:T(8,128)S(1)}, u32[]{:S(2)}, u32[]{:S(2)}) collective-permute-start(f32[256,256]{1,0:T(8,128)S(1)} %invert.1.refs_2_.refs_0_), channel_id=1, source_target_pairs={{1,0},{2,1},{3,2},{4,3},{5,4},{6,5},{7,6},{8,7},{9,8},{10,9},{11,1... | collective-permute-start | bytes 786440 | tf_op jit(solution)/shard_map/ppermute | solution.py:526
  155.9 0.0 collective-permute-done.4.refs_6_
  155.9 0.0 collective-permute-start.1
  155.9 0.0 collective-permute-done.3.refs_5_
  155.9 3.9 %collective-permute-done.2.refs_4_ = f32[256,256]{1,0:T(8,128)S(1)} collective-permute-done((f32[256,256]{1,0:T(8,128)S(1)}, f32[256,256]{1,0:T(8,128)S(1)}, u32[]{:S(2)}, u32[]{:S(2)}) %collective-permute-start.2) | collective-permute-done | bytes 262176 | tf_op jit(solution)/shard_map/ppermute | solution.py:526
  159.8 7.3 %collective-permute-done.1.refs_3_ = f32[256,256]{1,0:T(8,128)S(1)} collective-permute-done((f32[256,256]{1,0:T(8,128)S(1)}, f32[256,256]{1,0:T(8,128)S(1)}, u32[]{:S(2)}, u32[]{:S(2)}) %collective-permute-start.1) | collective-permute-done | bytes 262176 | tf_op jit(solution)/shard_map/ppermute | solution.py:523
  167.1 0.0 collective-permute-done.6.refs_8_
  167.1 0.0 collective-permute-done.5.refs_7_
  167.1 6.3 %shard_map.59 = (f32[256,2048]{1,0:T(8,128)S(1)}, f32[256,2048]{1,0:T(8,128)S(1)}, f32[8,2048]{1,0:T(8,128)S(1)}) custom-call(f32[264,384]{1,0:T(8,128)S(1)} %collective-permute-done.lower_ref.refs_0_, f32[256,256]{1,0:T(8,128)S(1)} %get-tuple-element.24.refs_1_, f32[256,256]{1,0:T(8,128)S(1)} %invert.1.refs_2_.refs_0_, ...), custom_call_target="tpu_custom_call" | custom-call | tf_op jit(solution)/shard_map/pallas_call | solution.py:402
  173.4 0.2 collective-permute-start.8
  173.6 1.9 collective-permute-start.7
  175.5 2.1 shard_map.60
  177.6 40.0 %collective-permute-done.8.refs_4_ = f32[256,2048]{1,0:T(8,128)S(1)} collective-permute-done((f32[256,2048]{1,0:T(8,128)S(1)}, f32[256,2048]{1,0:T(8,128)S(1)}, u32[]{:S(2)}, u32[]{:S(2)}) %collective-permute-start.8) | collective-permute-done | bytes 2097184 | tf_op jit(solution)/shard_map/ppermute | solution.py:526
  217.6 0.6 collective-permute-done.7.refs_3_
  218.2 5.0 %shard_map.61 = (f32[256,2048]{1,0:T(8,128)S(1)}, f32[256,1024]{1,0:T(8,128)S(1)}, f32[256,1024]{1,0:T(8,128)S(1)}, f32[8,2048]{1,0:T(8,128)S(1)}) custom-call(f32[264,384]{1,0:T(8,128)S(1)} %collective-permute-done.lower_ref.refs_0_, f32[256,256]{1,0:T(8,128)S(1)} %get-tuple-element.24.refs_1_, f32[256,256]{1,0:T(8,128)S(1)} %invert.1.refs_2_.refs_0_, ...), custom_call_target="tpu_custom_call" | custom-call | tf_op jit(solution)/shard_map/pallas_call | solution.py:402
  223.2 0.4 collective-permute-start.9
  223.6 2.2 collective-permute-start.10
  225.8 1.9 collective-permute-start.11
  227.7 5.2 %collective-permute-start.12 = (f32[256,1024]{1,0:T(8,128)S(1)}, f32[256,1024]{1,0:T(8,128)S(1)}, u32[]{:S(2)}, u32[]{:S(2)}) collective-permute-start(f32[256,1024]{1,0:T(8,128)S(1)} %get-tuple-element.34.refs_4_.refs_10_), channel_id=1, source_target_pairs={{1,0},{2,1},{3,2},{4,3},{5,4},{6,5},{7,6},{8,7},{9,8},{10,9},{11,1... | collective-permute-start | bytes 3145736 | tf_op jit(solution)/shard_map/ppermute | solution.py:526
  233.0 12.3 %collective-permute-done.9.refs_3_ = f32[256,1024]{1,0:T(8,128)S(1)} collective-permute-done((f32[256,1024]{1,0:T(8,128)S(1)}, f32[256,1024]{1,0:T(8,128)S(1)}, u32[]{:S(2)}, u32[]{:S(2)}) %collective-permute-start.9) | collective-permute-done | bytes 1048608 | tf_op jit(solution)/shard_map/ppermute | solution.py:526
  245.2 0.0 collective-permute-done.10.refs_5_
  245.3 2.4 shard_map.62
  247.7 20.3 %collective-permute-start.13 = (f32[8,2048]{1,0:T(8,128)S(1)}, f32[8,2048]{1,0:T(8,128)S(1)}, u32[]{:S(2)}, u32[]{:S(2)}) collective-permute-start(f32[8,2048]{1,0:T(8,128)S(1)} %get-tuple-element.37), channel_id=1, source_target_pairs={{0,16},{1,17},{2,18},{3,19},{4,20},{5,21},{6,22},{7,23},{8,24},{9,... | collective-permute-start | bytes 196616 | tf_op jit(solution)/shard_map/ppermute | solution.py:511
  268.0 0.9 collective-permute-done.13
  268.9 0.1 collective-permute-start.14
  269.0 4.3 %collective-permute-done.14 = f32[8,2048]{1,0:T(8,128)S(1)} collective-permute-done((f32[8,2048]{1,0:T(8,128)S(1)}, f32[8,2048]{1,0:T(8,128)S(1)}, u32[]{:S(2)}, u32[]{:S(2)}) %collective-permute-start.14) | collective-permute-done | bytes 65568 | tf_op jit(solution)/shard_map/ppermute | solution.py:511
  273.4 0.5 collective-permute-start.15
  273.9 5.0 %collective-permute-done.15 = f32[8,2048]{1,0:T(8,128)S(1)} collective-permute-done((f32[8,2048]{1,0:T(8,128)S(1)}, f32[8,2048]{1,0:T(8,128)S(1)}, u32[]{:S(2)}, u32[]{:S(2)}) %collective-permute-start.15) | collective-permute-done | bytes 65568 | tf_op jit(solution)/shard_map/ppermute | solution.py:511
  278.9 0.1 collective-permute-start.16
  279.0 4.3 %collective-permute-done.16 = f32[8,2048]{1,0:T(8,128)S(1)} collective-permute-done((f32[8,2048]{1,0:T(8,128)S(1)}, f32[8,2048]{1,0:T(8,128)S(1)}, u32[]{:S(2)}, u32[]{:S(2)}) %collective-permute-start.16) | collective-permute-done | bytes 65568 | tf_op jit(solution)/shard_map/ppermute | solution.py:511
  283.3 0.1 collective-permute-start.17
  283.4 5.5 %collective-permute-done.17 = f32[8,2048]{1,0:T(8,128)S(1)} collective-permute-done((f32[8,2048]{1,0:T(8,128)S(1)}, f32[8,2048]{1,0:T(8,128)S(1)}, u32[]{:S(2)}, u32[]{:S(2)}) %collective-permute-start.17) | collective-permute-done | bytes 65568 | tf_op jit(solution)/shard_map/ppermute | solution.py:511
  288.8 0.1 collective-permute-start.18
  288.9 4.3 %collective-permute-done.18 = f32[8,2048]{1,0:T(8,128)S(1)} collective-permute-done((f32[8,2048]{1,0:T(8,128)S(1)}, f32[8,2048]{1,0:T(8,128)S(1)}, u32[]{:S(2)}, u32[]{:S(2)}) %collective-permute-start.18) | collective-permute-done | bytes 65568 | tf_op jit(solution)/shard_map/ppermute | solution.py:511
  293.2 0.1 collective-permute-start.19
  293.3 5.5 %collective-permute-done.19 = f32[8,2048]{1,0:T(8,128)S(1)} collective-permute-done((f32[8,2048]{1,0:T(8,128)S(1)}, f32[8,2048]{1,0:T(8,128)S(1)}, u32[]{:S(2)}, u32[]{:S(2)}) %collective-permute-start.19) | collective-permute-done | bytes 65568 | tf_op jit(solution)/shard_map/ppermute | solution.py:511
  298.8 0.0 collective-permute-done.11.refs_9_
  298.8 0.0 collective-permute-done.12.refs_11_
  298.8 5.1 %shard_map.63 = (f32[256,2048]{1,0:T(8,128)}, f32[256,2048]{1,0:T(8,128)}) custom-call(f32[264,384]{1,0:T(8,128)S(1)} %collective-permute-done.lower_ref.refs_0_, f32[256,256]{1,0:T(8,128)S(1)} %get-tuple-element.24.refs_1_, f32[256,2048]{1,0:T(8,128)S(1)} %copy-done, f32[256,2048]{1,0:T(8,128)S(1)} %get-tuple-element.29.refs_3_, ...), custom_call_target="tpu_custom_call" | custom-call | tf_op jit(solution)/shard_map/pallas_call | solution.py:402
  (10 shorter events, 0.1 us)
Async XLA Ops:
  0.6 2.3 copy-start.2
  3.0 0.8 copy-start.4
  3.8 0.7 copy-start.5
  8.8 46.1 %copy-start.3 = (f32[5120,128]{1,0:T(8,128)}, f32[5120,128]{1,0:T(8,128)S(1)}, u32[]{:S(2)}) copy-start(f32[5120,128]{1,0:T(8,128)S(1)} %get-tuple-element.20) | copy-start | bytes 7864324
  54.9 5.9 %copy-start = (f32[256,2048]{1,0:T(8,128)S(1)}, f32[256,2048]{1,0:T(8,128)}, u32[]{:S(2)}) copy-start(f32[256,2048]{1,0:T(8,128)} %refs_2_.1) | copy-start | bytes 6291460
  55.0 46.2 %all-to-all-start = ((f32[128,40,128]{2,1,0:T(8,128)}), f32[128,40,128]{2,1,0:T(8,128)}, u32[]{:S(2)}, u32[]{:S(2)}) async-start(f32[128,40,128]{2,1,0:T(8,128)} %bitcast.8), calls=%async_computation | async-start | bytes 5242880 | tf_op jit(solution)/shard_map/all_to_all | solution.py:536
  62.0 93.9 %collective-permute-start.4 = (f32[160,2048]{1,0:T(8,128)}, f32[160,2048]{1,0:T(8,128)}, u32[]{:S(2)}, u32[]{:S(2)}) collective-permute-start(f32[160,2048]{1,0:T(8,128)} %slice.6), channel_id=1, source_target_pairs={{1,0},{2,1},{3,2},{4,3},{5,4},{6,5},{7,6},{8,7},{9,8},{10,9},{11,1... | collective-permute-start | bytes 3932168 | tf_op jit(solution)/shard_map/ppermute | solution.py:526
  68.9 86.9 %collective-permute-start.3 = (f32[160,2048]{1,0:T(8,128)}, f32[160,2048]{1,0:T(8,128)}, u32[]{:S(2)}, u32[]{:S(2)}) collective-permute-start(f32[160,2048]{1,0:T(8,128)} %slice.6), channel_id=1, source_target_pairs={{0,1},{1,2},{2,3},{3,4},{4,5},{5,6},{6,7},{7,8},{8,9},{9,10},{10,1... | collective-permute-start | bytes 3932168 | tf_op jit(solution)/shard_map/ppermute | solution.py:523
  69.9 97.2 %collective-permute-start.6 = (f32[96,2048]{1,0:T(8,128)}, f32[96,2048]{1,0:T(8,128)}, u32[]{:S(2)}, u32[]{:S(2)}) collective-permute-start(f32[96,2048]{1,0:T(8,128)} %slice.7), channel_id=1, source_target_pairs={{1,0},{2,1},{3,2},{4,3},{5,4},{6,5},{7,6},{8,7},{9,8},{10,9},{11,1... | collective-permute-start | bytes 2359304 | tf_op jit(solution)/shard_map/ppermute | solution.py:526
  77.1 90.0 %collective-permute-start.5 = (f32[96,2048]{1,0:T(8,128)}, f32[96,2048]{1,0:T(8,128)}, u32[]{:S(2)}, u32[]{:S(2)}) collective-permute-start(f32[96,2048]{1,0:T(8,128)} %slice.7), channel_id=1, source_target_pairs={{0,1},{1,2},{2,3},{3,4},{4,5},{5,6},{6,7},{7,8},{8,9},{9,10},{10,1... | collective-permute-start | bytes 2359304 | tf_op jit(solution)/shard_map/ppermute | solution.py:523
  77.1 1.7 copy-start.1
  109.7 31.5 %collective-permute-start = (f32[264,384]{1,0:T(8,128)S(1)}, f32[264,384]{1,0:T(8,128)S(1)}, u32[]{:S(2)}, u32[]{:S(2)}) collective-permute-start(f32[264,384]{1,0:T(8,128)S(1)} %get-tuple-element.23), channel_id=1, source_target_pairs={{0,1},{1,2},{2,3},{3,4},{4,5},{5,6},{6,7},{7,8},{8,9},{9,10},{10,1... | collective-permute-start | bytes 1216520 | tf_op jit(solution)/shard_map/ppermute | solution.py:523
  147.0 12.8 %collective-permute-start.2 = (f32[256,256]{1,0:T(8,128)S(1)}, f32[256,256]{1,0:T(8,128)S(1)}, u32[]{:S(2)}, u32[]{:S(2)}) collective-permute-start(f32[256,256]{1,0:T(8,128)S(1)} %invert.1.refs_2_.refs_0_), channel_id=1, source_target_pairs={{1,0},{2,1},{3,2},{4,3},{5,4},{6,5},{7,6},{8,7},{9,8},{10,9},{11,1... | collective-permute-start | bytes 786440 | tf_op jit(solution)/shard_map/ppermute | solution.py:526
  155.9 11.2 %collective-permute-start.1 = (f32[256,256]{1,0:T(8,128)S(1)}, f32[256,256]{1,0:T(8,128)S(1)}, u32[]{:S(2)}, u32[]{:S(2)}) collective-permute-start(f32[256,256]{1,0:T(8,128)S(1)} %invert.1.refs_2_.refs_0_), channel_id=1, source_target_pairs={{0,1},{1,2},{2,3},{3,4},{4,5},{5,6},{6,7},{7,8},{8,9},{9,10},{10,1... | collective-permute-start | bytes 786440 | tf_op jit(solution)/shard_map/ppermute | solution.py:523
  173.4 44.2 %collective-permute-start.8 = (f32[256,2048]{1,0:T(8,128)S(1)}, f32[256,2048]{1,0:T(8,128)S(1)}, u32[]{:S(2)}, u32[]{:S(2)}) collective-permute-start(f32[256,2048]{1,0:T(8,128)S(1)} %get-tuple-element.30.refs_5_), channel_id=1, source_target_pairs={{1,0},{2,1},{3,2},{4,3},{5,4},{6,5},{7,6},{8,7},{9,8},{10,9},{11,1... | collective-permute-start | bytes 6291464 | tf_op jit(solution)/shard_map/ppermute | solution.py:526
  173.6 44.6 %collective-permute-start.7 = (f32[256,2048]{1,0:T(8,128)S(1)}, f32[256,2048]{1,0:T(8,128)S(1)}, u32[]{:S(2)}, u32[]{:S(2)}) collective-permute-start(f32[256,2048]{1,0:T(8,128)S(1)} %get-tuple-element.30.refs_5_), channel_id=1, source_target_pairs={{0,1},{1,2},{2,3},{3,4},{4,5},{5,6},{6,7},{7,8},{8,9},{9,10},{10,1... | collective-permute-start | bytes 6291464 | tf_op jit(solution)/shard_map/ppermute | solution.py:523
  223.2 22.1 %collective-permute-start.9 = (f32[256,1024]{1,0:T(8,128)S(1)}, f32[256,1024]{1,0:T(8,128)S(1)}, u32[]{:S(2)}, u32[]{:S(2)}) collective-permute-start(f32[256,1024]{1,0:T(8,128)S(1)} %get-tuple-element.33.refs_2_.refs_8_), channel_id=1, source_target_pairs={{1,0},{2,1},{3,2},{4,3},{5,4},{6,5},{7,6},{8,7},{9,8},{10,9},{11,1... | collective-permute-start | bytes 3145736 | tf_op jit(solution)/shard_map/ppermute | solution.py:526
  223.6 21.7 %collective-permute-start.10 = (f32[256,1024]{1,0:T(8,128)S(1)}, f32[256,1024]{1,0:T(8,128)S(1)}, u32[]{:S(2)}, u32[]{:S(2)}) collective-permute-start(f32[256,1024]{1,0:T(8,128)S(1)} %get-tuple-element.34.refs_4_.refs_10_), channel_id=1, source_target_pairs={{0,1},{1,2},{2,3},{3,4},{4,5},{5,6},{6,7},{7,8},{8,9},{9,10},{10,1... | collective-permute-start | bytes 3145736 | tf_op jit(solution)/shard_map/ppermute | solution.py:523
  225.8 73.0 %collective-permute-start.11 = (f32[256,1024]{1,0:T(8,128)S(1)}, f32[256,1024]{1,0:T(8,128)S(1)}, u32[]{:S(2)}, u32[]{:S(2)}) collective-permute-start(f32[256,1024]{1,0:T(8,128)S(1)} %get-tuple-element.33.refs_2_.refs_8_), channel_id=1, source_target_pairs={{0,1},{1,2},{2,3},{3,4},{4,5},{5,6},{6,7},{7,8},{8,9},{9,10},{10,1... | collective-permute-start | bytes 3145736 | tf_op jit(solution)/shard_map/ppermute | solution.py:523
  227.7 71.0 %collective-permute-start.12 = (f32[256,1024]{1,0:T(8,128)S(1)}, f32[256,1024]{1,0:T(8,128)S(1)}, u32[]{:S(2)}, u32[]{:S(2)}) collective-permute-start(f32[256,1024]{1,0:T(8,128)S(1)} %get-tuple-element.34.refs_4_.refs_10_), channel_id=1, source_target_pairs={{1,0},{2,1},{3,2},{4,3},{5,4},{6,5},{7,6},{8,7},{9,8},{10,9},{11,1... | collective-permute-start | bytes 3145736 | tf_op jit(solution)/shard_map/ppermute | solution.py:526
  247.7 21.2 %collective-permute-start.13 = (f32[8,2048]{1,0:T(8,128)S(1)}, f32[8,2048]{1,0:T(8,128)S(1)}, u32[]{:S(2)}, u32[]{:S(2)}) collective-permute-start(f32[8,2048]{1,0:T(8,128)S(1)} %get-tuple-element.37), channel_id=1, source_target_pairs={{0,16},{1,17},{2,18},{3,19},{4,20},{5,21},{6,22},{7,23},{8,24},{9,... | collective-permute-start | bytes 196616 | tf_op jit(solution)/shard_map/ppermute | solution.py:511
  268.9 4.4 %collective-permute-start.14 = (f32[8,2048]{1,0:T(8,128)S(1)}, f32[8,2048]{1,0:T(8,128)S(1)}, u32[]{:S(2)}, u32[]{:S(2)}) collective-permute-start(f32[8,2048]{1,0:T(8,128)S(1)} %add.25), channel_id=1, source_target_pairs={{0,32},{1,33},{2,34},{3,35},{4,36},{5,37},{6,38},{7,39},{8,40},{9,... | collective-permute-start | bytes 196616 | tf_op jit(solution)/shard_map/ppermute | solution.py:511
  273.4 5.6 %collective-permute-start.15 = (f32[8,2048]{1,0:T(8,128)S(1)}, f32[8,2048]{1,0:T(8,128)S(1)}, u32[]{:S(2)}, u32[]{:S(2)}) collective-permute-start(f32[8,2048]{1,0:T(8,128)S(1)} %add.26), channel_id=1, source_target_pairs={{0,96},{1,97},{2,98},{3,99},{4,100},{5,101},{6,102},{7,103},{8,104... | collective-permute-start | bytes 196616 | tf_op jit(solution)/shard_map/ppermute | solution.py:511
  278.9 4.3 %collective-permute-start.16 = (f32[8,2048]{1,0:T(8,128)S(1)}, f32[8,2048]{1,0:T(8,128)S(1)}, u32[]{:S(2)}, u32[]{:S(2)}) collective-permute-start(f32[8,2048]{1,0:T(8,128)S(1)} %add.27), channel_id=1, source_target_pairs={{0,4},{1,5},{2,6},{3,7},{4,0},{5,1},{6,2},{7,3},{8,12},{9,13},{10,... | collective-permute-start | bytes 196616 | tf_op jit(solution)/shard_map/ppermute | solution.py:511
  283.3 5.6 %collective-permute-start.17 = (f32[8,2048]{1,0:T(8,128)S(1)}, f32[8,2048]{1,0:T(8,128)S(1)}, u32[]{:S(2)}, u32[]{:S(2)}) collective-permute-start(f32[8,2048]{1,0:T(8,128)S(1)} %add.28), channel_id=1, source_target_pairs={{0,12},{1,13},{2,14},{3,15},{4,8},{5,9},{6,10},{7,11},{8,4},{9,5},... | collective-permute-start | bytes 196616 | tf_op jit(solution)/shard_map/ppermute | solution.py:511
  288.8 4.3 %collective-permute-start.18 = (f32[8,2048]{1,0:T(8,128)S(1)}, f32[8,2048]{1,0:T(8,128)S(1)}, u32[]{:S(2)}, u32[]{:S(2)}) collective-permute-start(f32[8,2048]{1,0:T(8,128)S(1)} %add.29), channel_id=1, source_target_pairs={{0,1},{1,0},{2,3},{3,2},{4,5},{5,4},{6,7},{7,6},{8,9},{9,8},{10,11... | collective-permute-start | bytes 196616 | tf_op jit(solution)/shard_map/ppermute | solution.py:511
  293.2 5.6 %collective-permute-start.19 = (f32[8,2048]{1,0:T(8,128)S(1)}, f32[8,2048]{1,0:T(8,128)S(1)}, u32[]{:S(2)}, u32[]{:S(2)}) collective-permute-start(f32[8,2048]{1,0:T(8,128)S(1)} %add.30), channel_id=1, source_target_pairs={{0,3},{1,2},{2,1},{3,0},{4,7},{5,6},{6,5},{7,4},{8,11},{9,10},{10,... | collective-permute-start | bytes 196616 | tf_op jit(solution)/shard_map/ppermute | solution.py:511
